TPU v7x, 128 devices: a whole 4x4x4 slice. The times are simulated.
128 devices in a mesh: slab: 32 (over y, z, core), md: 4 (over x).
Axes of the slice: x: 4, y: 4, z: 4, core: 2. Of those that a mesh axis runs over, the one named last changes fastest.
Arguments:
- populations: float32 [19, 64, 256, 128], P(None, 'slab', 'md'), may hold values from 0.02 to 0.1
- relax: float32 [64, 256, 128], P('slab', 'md'), may hold values from 0.8 to 1.8
- owners: int32 [64, 256, 2], P('slab', 'md'), may hold values from 0 to 127, all different within a row; in each aligned block of 64 rows (0 to 63, 64 to 127, ..., all dimensions but the last counted through in order) at most 2 rows name the same one
- positions: float32 [3, 131072], P(None, ('slab', 'md')), may hold values from 0 to 3
- velocities: float32 [3, 131072], P(None, ('slab', 'md')), may hold values from -5 to 5
- neighbours: int32 [131072, 64], P(('slab', 'md')), may hold values from 0 to 1023
- atom_slots: int32 [131072], P(('slab', 'md')), may hold values from 0 to 511
Outputs:
- populations_out: float32 [19, 64, 256, 128], P(None, 'slab', 'md')
- positions_out: float32 [3, 131072], P(None, ('slab', 'md'))
- velocities_out: float32 [3, 131072], P(None, ('slab', 'md'))
- cell_moments: float32 [4, 64, 256], P(None, 'slab', 'md')
Inputs may be any that keep to these rules, and one draw needn't show every extreme that they name: The 64 entries of one z position on one device name any owner at most 2 times in each column k and across k; the 2 owners of one cell differ. `neighbours`: entries index atoms of the same subdomain's block of 1024 atoms; an atom that lists itself is padding.
All inputs are finite; a program needn't handle non-finite values.
Results may differ from a plain program's by a relative error of at most 0.0003.
Values sent between devices are 32-bit elements; how exact they have to be, the bound alone decides.
No kernel may reach another device: no remote copies, remote signals or barrier semaphores. Data moves between devices by JAX's collectives and lax.ppermute only.
A program may use at most 64 MiB of HBM per device.

v0:
```python
import jax
import jax.numpy as jnp
from jax import lax
from jax.experimental import pallas as pl
from jax.experimental.pallas import tpu as pltpu
from jax.sharding import PartitionSpec as P

LB_STEPS = 4
MD_STEPS = 5
f32 = jnp.float32
i32 = jnp.int32
bf16 = jnp.bfloat16

lattice_dirs = [
    (0, 0, 0),
    (1, 0, 0),
    (-1, 0, 0),
    (0, 1, 0),
    (0, -1, 0),
    (0, 0, 1),
    (0, 0, -1),
    (1, 1, 0),
    (-1, -1, 0),
    (1, -1, 0),
    (-1, 1, 0),
    (1, 0, 1),
    (-1, 0, -1),
    (1, 0, -1),
    (-1, 0, 1),
    (0, 1, 1),
    (0, -1, -1),
    (0, 1, -1),
    (0, -1, 1),
]
lattice_weights = [1.0 / 3.0] + [1.0 / 18.0] * 6 + [1.0 / 36.0] * 12
velocity_scale = 10.0
pair_strength = 0.5
friction = 2.0
time_step = 0.1


def padded_2(cells, sides, width):
    for axis, dim in sides:
        count = lax.axis_size(axis)
        head = lax.slice_in_dim(cells, 0, width, axis=dim)
        tail = lax.slice_in_dim(cells, cells.shape[dim] - width, cells.shape[dim], axis=dim)
        cells = jnp.concatenate(
            [
                lax.ppermute(tail, axis, [(i, (i + 1) % count) for i in range(count)]),
                cells,
                lax.ppermute(head, axis, [((i + 1) % count, i) for i in range(count)]),
            ],
            axis=dim,
        )
    return cells


def shifted(shard, axis, by):
    devices = lax.axis_size(axis)
    return lax.ppermute(shard, axis, [(i, (i + by) % devices) for i in range(devices)])


def velocity(f, density):
    comps = []
    for axis_id in range(3):
        total = jnp.zeros_like(density)
        for index, direction in enumerate(lattice_dirs):
            if direction[axis_id] != 0:
                total = total + direction[axis_id] * f[index]
        comps.append(total / density)
    return comps


def collide(f, relax):
    density = jnp.sum(f, axis=0)
    vel_x, vel_y, vel_z = velocity(f, density)
    usq = vel_x * vel_x + vel_y * vel_y + vel_z * vel_z
    result = []
    for index, direction in enumerate(lattice_dirs):
        along = direction[0] * vel_x + direction[1] * vel_y + direction[2] * vel_z
        equil = (
            lattice_weights[index] * density * (1.0 + 3.0 * along + 4.5 * along * along - 1.5 * usq)
        )
        result.append(f[index] - relax * (f[index] - equil))
    return result


def lanes(table, index):
    return jnp.take_along_axis(table, index, axis=1, mode="promise_in_bounds")


def spread(block, index, rows=8):
    return jnp.broadcast_to(block[index : index + 1, :], (rows, 128))


def pair_sum(coords, nbr_ref):
    tables = [[spread(comp, chunk) for chunk in range(8)] for comp in coords]

    def entry(k, total):
        index = nbr_ref[k]
        low = index & 127
        bits = [(index & mask) != 0 for mask in (128, 256, 512)]
        gaps = []
        for comp in range(3):
            level = [lanes(table, low) for table in tables[comp]]
            for bit in bits:
                level = [
                    jnp.where(bit, level[2 * j + 1], level[2 * j]) for j in range(len(level) // 2)
                ]
            gaps.append(level[0] - coords[comp])
        weight = jnp.exp(-0.5 * (gaps[0] * gaps[0] + gaps[1] * gaps[1] + gaps[2] * gaps[2]))
        return tuple(t + g * weight for t, g in zip(total, gaps))

    zero = jnp.zeros((8, 128), f32)
    return lax.fori_loop(0, nbr_ref.shape[0], entry, (zero, zero, zero), unroll=16)


def prep_kernel(own_ref, slot_ref, pos_ref, vel_ref, nbr_ref,
                inv_ref, rank_ref, hot_ref, icnt_ref, force_ref, p8_ref, v8_ref):
    row_id = lax.broadcasted_iota(i32, (128, 128), 0)
    lane_id = lax.broadcasted_iota(i32, (128, 128), 1)
    own = [spread(own_ref[...], k, 128) for k in range(2)]
    own_t = [o.T for o in own]
    ranks = []
    for k in range(2):
        count = jnp.zeros((128, 128), i32)
        for other in range(2):
            count = count + jnp.where((own_t[other] == own[k]) & (row_id < lane_id), 1, 0)
        ranks.append(jnp.sum(count, axis=0, keepdims=True))
    rank_ref[...] = jnp.concatenate(ranks + [jnp.zeros((6, 128), i32)], axis=0)
    rank_t = [jnp.broadcast_to(r, (128, 128)).T for r in ranks]
    rows = []
    for r in range(4):
        cell = jnp.zeros((128, 128), i32)
        for k in range(2):
            cell = cell + jnp.where((own_t[k] == lane_id) & (rank_t[k] == r), row_id + 1, 0)
        rows.append(jnp.sum(cell, axis=0, keepdims=True) - 1)
    inv_ref[...] = jnp.concatenate(rows + [jnp.zeros((4, 128), i32)], axis=0)
    slots = slot_ref[...]
    count = jnp.zeros((128, 16), f32)
    want = lax.broadcasted_iota(i32, (16, 128), 0) >> 2
    for s in range(8):
        one = spread(slots, s, 128)
        hot = jnp.where((one >> 2) == row_id, 1.0, 0.0).astype(bf16)
        hot_ref[:, s * 128 : (s + 1) * 128] = hot
        match = jnp.where((spread(slots, s, 16) & 3) == want, 1.0, 0.0).astype(bf16)
        count = count + lax.dot_general(
            hot, match, (((1,), (1,)), ((), ())), preferred_element_type=f32
        )
    icnt_ref[...] = 1.0 / jnp.maximum(count, 1.0)
    for c in range(3):
        for s in range(8):
            p8_ref[c, s : s + 1, :] = pos_ref[c : c + 1, s * 128 : (s + 1) * 128]
            v8_ref[c, s : s + 1, :] = vel_ref[c : c + 1, s * 128 : (s + 1) * 128]
    total = pair_sum([p8_ref[0], p8_ref[1], p8_ref[2]], nbr_ref)
    for c in range(3):
        force_ref[c] = total[c]


def pack_kernel(t_ref, inv_ref, out_ref):
    t16 = jnp.concatenate([t_ref[...]] * 4, axis=0)
    inv16 = jnp.concatenate(
        [jnp.broadcast_to(inv_ref[r : r + 1, :], (4, 128)) for r in range(4)], axis=0
    )
    picked = jnp.where(inv16 >= 0, lanes(t16, jnp.maximum(inv16, 0)), 0.0)
    out_ref[...] = jnp.concatenate([picked, jnp.zeros((112, 128), f32)], axis=0).T


def md_kernel(arr_ref, p8_ref, v8_ref, force_ref, nbr_ref, slot_ref, hot_ref, icnt_ref,
              pos_ref, vel_ref, mom_ref):
    table = arr_ref[...].T
    slots = slot_ref[...]
    source = slots >> 2
    which = slots & 3
    target = []
    for c in range(4):
        value = lanes(spread(table, c), source)
        for r in range(1, 4):
            value = jnp.where(which == r, lanes(spread(table, r * 4 + c), source), value)
        target.append(value)
    drag = friction * target[3]
    pos = [p8_ref[c] for c in range(3)]
    vel = [v8_ref[c] for c in range(3)]
    for step in range(MD_STEPS):
        pair = [force_ref[c] for c in range(3)] if step == 0 else pair_sum(pos, nbr_ref)
        for c in range(3):
            force = pair_strength * pair[c] + drag * (target[c] - vel[c])
            vel[c] = vel[c] + time_step * force
            pos[c] = pos[c] + time_step * vel[c]
    speed = vel[0] * vel[0] + vel[1] * vel[1] + vel[2] * vel[2]
    data = vel + [speed]
    row_id = lax.broadcasted_iota(i32, (16, 128), 0)
    comp = row_id & 3
    sums = jnp.zeros((128, 16), f32)
    for s in range(8):
        value = spread(data[0], s, 16)
        for c in range(1, 4):
            value = jnp.where(comp == c, spread(data[c], s, 16), value)
        value = jnp.where((spread(slots, s, 16) & 3) == (row_id >> 2), value, 0.0)
        hot = hot_ref[:, s * 128 : (s + 1) * 128]
        for part in range(3):
            piece = value.astype(bf16)
            value = value - piece.astype(f32)
            sums = sums + lax.dot_general(
                hot, piece, (((1,), (1,)), ((), ())), preferred_element_type=f32
            )
    mom_ref[...] = jnp.zeros((128, 128), f32)
    mom_ref[:, :16] = sums * icnt_ref[...]
    for c in range(3):
        for s in range(8):
            pos_ref[c : c + 1, s * 128 : (s + 1) * 128] = pos[c][s : s + 1, :]
            vel_ref[c : c + 1, s * 128 : (s + 1) * 128] = vel[c][s : s + 1, :]


def cell_kernel(back_ref, own_ref, rank_ref, out_ref):
    table = back_ref[...].T[:16, :]
    which = lax.broadcasted_iota(i32, (16, 128), 0) >> 2
    total = jnp.zeros((16, 128), f32)
    for k in range(2):
        picked = lanes(table, spread(own_ref[...], k, 16))
        total = total + jnp.where(spread(rank_ref[...], k, 16) == which, picked, 0.0)
    cell = total[0:4] + total[4:8] + total[8:12] + total[12:16]
    out_ref[:, 0, :] = cell[:, :64]
    out_ref[:, 1, :] = cell[:, 64:]


def shape(*dims, dtype=f32):
    return jax.ShapeDtypeStruct(dims, dtype)


def exchange(rows):
    return lax.all_to_all(rows, ("slab", "md"), split_axis=0, concat_axis=0, tiled=True)


def on_device(populations, relax, owners, positions, velocities, neighbours, atom_slots):
    own = owners.reshape(128, 2).T
    slots = atom_slots.reshape(8, 128)
    nbr = neighbours.reshape(8, 128, 64).transpose(2, 0, 1)
    inv, rank, hot, icnt, force, p8, v8 = pl.pallas_call(
        prep_kernel,
        out_shape=(
            shape(8, 128, dtype=i32),
            shape(8, 128, dtype=i32),
            shape(128, 1024, dtype=bf16),
            shape(128, 16),
            shape(3, 8, 128),
            shape(3, 8, 128),
            shape(3, 8, 128),
        ),
        name="prep",
    )(own, slots, positions, velocities, nbr)
    f = populations
    cz_len = f.shape[1]
    cx_len = f.shape[2]
    rising = [i for i, c in enumerate(lattice_dirs) if c[2] == 1]
    falling = [i for i, c in enumerate(lattice_dirs) if c[2] == -1]
    for step in range(LB_STEPS):
        post = jnp.stack(collide(f, relax))
        padded = padded_2(post, (("md", 2),), 1)
        moved = jnp.stack(
            [
                jnp.roll(padded[i, :, 1 - c[0] : 1 - c[0] + cx_len, :], c[1], axis=2)
                for i, c in enumerate(lattice_dirs)
            ]
        )
        top_planes = jnp.stack([moved[i, cz_len - 1 :] for i in rising])
        low_planes = jnp.stack([moved[i, :1] for i in falling])
        below = shifted(top_planes, "slab", 1)
        above = shifted(low_planes, "slab", -1)
        pieces = []
        for i, c in enumerate(lattice_dirs):
            if c[2] == 1:
                pieces.append(
                    jnp.concatenate([below[rising.index(i)], moved[i, : cz_len - 1]], axis=0)
                )
            elif c[2] == -1:
                pieces.append(jnp.concatenate([moved[i, 1:], above[falling.index(i)]], axis=0))
            else:
                pieces.append(moved[i])
        f = jnp.stack(pieces)
    density = jnp.sum(f, axis=0)
    vel_x, vel_y, vel_z = velocity(f, density)
    targets = jnp.stack(
        [
            jnp.mean(velocity_scale * vel_x, axis=2),
            jnp.mean(velocity_scale * vel_y, axis=2),
            jnp.mean(velocity_scale * vel_z, axis=2),
            jnp.mean(density, axis=2),
        ]
    )
    outgoing = pl.pallas_call(pack_kernel, out_shape=shape(128, 128), name="pack")(
        targets.reshape(4, 128), inv
    )
    arrived = exchange(outgoing)
    pos_out, vel_out, moms = pl.pallas_call(
        md_kernel, out_shape=(shape(3, 1024), shape(3, 1024), shape(128, 128)), name="md"
    )(arrived, p8, v8, force, nbr, slots, hot, icnt)
    returned = exchange(moms)
    cell = pl.pallas_call(cell_kernel, out_shape=shape(4, 2, 64), name="cells")(
        returned, own, rank
    )
    return (f, pos_out, vel_out, cell)


def solution(mesh):
    return jax.shard_map(
        on_device,
        mesh=mesh,
        in_specs=(
            P(None, "slab", "md", None),
            P("slab", "md", None),
            P("slab", "md", None),
            P(None, ("slab", "md")),
            P(None, ("slab", "md")),
            P(("slab", "md"), None),
            P(("slab", "md")),
        ),
        out_specs=(
            P(None, "slab", "md", None),
            P(None, ("slab", "md")),
            P(None, ("slab", "md")),
            P(None, "slab", "md"),
        ),
        check_vma=False,
    )
```

profile of v0, /device:TPU:1, one launch (start us, length us, event | category | flops | bytes accessed | tf_op | source)
XLA Modules:
  0.0 119.8 jit_solution(1576335561192874991)
XLA Ops:
  0.7 1.5 %reduce_sum.289 = f32[2,64,128]{2,1,0:T(8,128)S(1)} reduce(f32[19,2,64,128]{3,2,1,0:T(8,128)} %param.7, f32[]{:T(128)} %constant.11.clone.1), dimensions={0}, to_apply=%region_0.0 | reduce | flops 294912 | bytes 1310724 | tf_op jit(solution)/shard_map/reduce_sum | solution.py:75
  3.4 2.1 %collective-permute-start = (f32[19,2,1,128]{3,2,1,0:T(1,128)S(1)}, f32[19,2,1,128]{3,2,1,0:T(1,128)S(1)}, u32[]{:S(2)}, u32[]{:S(2)}) collective-permute-start(f32[19,2,1,128]{3,2,1,0:T(1,128)S(1)} %get-tuple-element.201), channel_id=1, source_target_pairs={{0,1},{1,2},{2,3},{3,0},{4,5},{5,6},{6,7},{7,4},{8,9},{9,10},{10,1... | collective-permute-start | bytes 58376 | tf_op jit(solution)/shard_map/ppermute | solution.py:49
  5.5 1.3 %collective-permute-start.1 = (f32[19,2,1,128]{3,2,1,0:T(1,128)S(1)}, f32[19,2,1,128]{3,2,1,0:T(1,128)S(1)}, u32[]{:S(2)}, u32[]{:S(2)}) collective-permute-start(f32[19,2,1,128]{3,2,1,0:T(1,128)S(1)} %get-tuple-element.202), channel_id=1, source_target_pairs={{1,0},{2,1},{3,2},{0,3},{5,4},{6,5},{7,6},{4,7},{9,8},{10,9},{11,1... | collective-permute-start | bytes 58376 | tf_op jit(solution)/shard_map/ppermute | solution.py:51
  7.8 0.8 copy.15
  8.5 0.6 reshape.222
  9.2 4.1 %prep.1 = (s32[8,128]{1,0:T(8,128)}, s32[8,128]{1,0:T(8,128)}, bf16[128,1024]{1,0:T(8,128)(2,1)}, f32[128,16]{1,0:T(8,128)}, f32[3,8,128]{2,1,0:T(8,128)}, /*index=5*/f32[3,8,128]{2,1,0:T(8,128)}, f32[3,8,128]{2,1,0:T(8,128)}) custom-call(s32[2,128]{1,0:T(2,128)} %bitcast.884, s32[8,128]{1,0:T(8,128)} %bitcast.882, f32[3,1024]{1,0:T(4,128)} %pos_ref.1, ...), custom_call_target="tpu_custom_call" | custom-call | tf_op jit(solution)/shard_map/prep/pallas_call | solution.py:239
  13.8 1.3 %collective-permute-start.3 = (f32[5,1,64,128]{3,2,1,0:T(8,128)S(1)}, f32[5,1,64,128]{3,2,1,0:T(8,128)S(1)}, u32[]{:S(2)}, u32[]{:S(2)}) collective-permute-start(f32[5,1,64,128]{3,2,1,0:T(8,128)S(1)} %get-tuple-element.288), channel_id=1, source_target_pairs={{0,124},{4,0},{8,4},{12,8},{16,12},{20,16},{24,20},{28,24},{32,28}... | collective-permute-start | bytes 491528 | tf_op jit(solution)/shard_map/ppermute | solution.py:60
  15.1 1.7 %collective-permute-start.2 = (f32[5,1,64,128]{3,2,1,0:T(8,128)S(1)}, f32[5,1,64,128]{3,2,1,0:T(8,128)S(1)}, u32[]{:S(2)}, u32[]{:S(2)}) collective-permute-start(f32[5,1,64,128]{3,2,1,0:T(8,128)S(1)} %get-tuple-element.290), channel_id=1, source_target_pairs={{0,4},{4,8},{8,12},{12,16},{16,20},{20,24},{24,28},{28,32},{32,36}... | collective-permute-start | bytes 491528 | tf_op jit(solution)/shard_map/ppermute | solution.py:60
  16.8 2.9 %collective-permute-done.3 = f32[5,1,64,128]{3,2,1,0:T(8,128)S(1)} collective-permute-done((f32[5,1,64,128]{3,2,1,0:T(8,128)S(1)}, f32[5,1,64,128]{3,2,1,0:T(8,128)S(1)}, u32[]{:S(2)}, u32[]{:S(2)}) %collective-permute-start.3) | collective-permute-done | bytes 163872 | tf_op jit(solution)/shard_map/ppermute | solution.py:60
  19.7 1.8 %collective-permute-done.2 = f32[5,1,64,128]{3,2,1,0:T(8,128)S(1)} collective-permute-done((f32[5,1,64,128]{3,2,1,0:T(8,128)S(1)}, f32[5,1,64,128]{3,2,1,0:T(8,128)S(1)}, u32[]{:S(2)}, u32[]{:S(2)}) %collective-permute-start.2) | collective-permute-done | bytes 163872 | tf_op jit(solution)/shard_map/ppermute | solution.py:60
  23.0 2.7 %collective-permute-start.5 = (f32[19,2,1,128]{3,2,1,0:T(1,128)S(1)}, f32[19,2,1,128]{3,2,1,0:T(1,128)S(1)}, u32[]{:S(2)}, u32[]{:S(2)}) collective-permute-start(f32[19,2,1,128]{3,2,1,0:T(1,128)S(1)} %get-tuple-element.198), channel_id=1, source_target_pairs={{1,0},{2,1},{3,2},{0,3},{5,4},{6,5},{7,6},{4,7},{9,8},{10,9},{11,1... | collective-permute-start | bytes 58376 | tf_op jit(solution)/shard_map/ppermute | solution.py:51
  27.5 8.1 %collective-permute-start.7 = (f32[5,1,64,128]{3,2,1,0:T(8,128)S(1)}, f32[5,1,64,128]{3,2,1,0:T(8,128)S(1)}, u32[]{:S(2)}, u32[]{:S(2)}) collective-permute-start(f32[5,1,64,128]{3,2,1,0:T(8,128)S(1)} %get-tuple-element.276), channel_id=1, source_target_pairs={{0,124},{4,0},{8,4},{12,8},{16,12},{20,16},{24,20},{28,24},{32,28}... | collective-permute-start | bytes 491528 | tf_op jit(solution)/shard_map/ppermute | solution.py:60
  35.8 0.9 collective-permute-done.7
  36.7 1.3 %collective-permute-done.6 = f32[5,1,64,128]{3,2,1,0:T(8,128)S(1)} collective-permute-done((f32[5,1,64,128]{3,2,1,0:T(8,128)S(1)}, f32[5,1,64,128]{3,2,1,0:T(8,128)S(1)}, u32[]{:S(2)}, u32[]{:S(2)}) %collective-permute-start.6) | collective-permute-done | bytes 163872 | tf_op jit(solution)/shard_map/ppermute | solution.py:60
  39.7 2.8 %collective-permute-start.9 = (f32[19,2,1,128]{3,2,1,0:T(1,128)S(1)}, f32[19,2,1,128]{3,2,1,0:T(1,128)S(1)}, u32[]{:S(2)}, u32[]{:S(2)}) collective-permute-start(f32[19,2,1,128]{3,2,1,0:T(1,128)S(1)} %get-tuple-element.194), channel_id=1, source_target_pairs={{1,0},{2,1},{3,2},{0,3},{5,4},{6,5},{7,6},{4,7},{9,8},{10,9},{11,1... | collective-permute-start | bytes 58376 | tf_op jit(solution)/shard_map/ppermute | solution.py:51
  44.0 6.8 %collective-permute-start.11 = (f32[5,1,64,128]{3,2,1,0:T(8,128)S(1)}, f32[5,1,64,128]{3,2,1,0:T(8,128)S(1)}, u32[]{:S(2)}, u32[]{:S(2)}) collective-permute-start(f32[5,1,64,128]{3,2,1,0:T(8,128)S(1)} %get-tuple-element.264), channel_id=1, source_target_pairs={{0,124},{4,0},{8,4},{12,8},{16,12},{20,16},{24,20},{28,24},{32,28}... | collective-permute-start | bytes 491528 | tf_op jit(solution)/shard_map/ppermute | solution.py:60
  50.9 0.9 collective-permute-done.11
  51.8 1.3 %collective-permute-done.10 = f32[5,1,64,128]{3,2,1,0:T(8,128)S(1)} collective-permute-done((f32[5,1,64,128]{3,2,1,0:T(8,128)S(1)}, f32[5,1,64,128]{3,2,1,0:T(8,128)S(1)}, u32[]{:S(2)}, u32[]{:S(2)}) %collective-permute-start.10) | collective-permute-done | bytes 163872 | tf_op jit(solution)/shard_map/ppermute | solution.py:60
  54.7 1.4 %collective-permute-start.12 = (f32[19,2,1,128]{3,2,1,0:T(1,128)S(1)}, f32[19,2,1,128]{3,2,1,0:T(1,128)S(1)}, u32[]{:S(2)}, u32[]{:S(2)}) collective-permute-start(f32[19,2,1,128]{3,2,1,0:T(1,128)S(1)} %get-tuple-element.190), channel_id=1, source_target_pairs={{0,1},{1,2},{2,3},{3,0},{4,5},{5,6},{6,7},{7,4},{8,9},{9,10},{10,1... | collective-permute-start | bytes 58376 | tf_op jit(solution)/shard_map/ppermute | solution.py:49
  56.1 2.0 %collective-permute-start.13 = (f32[19,2,1,128]{3,2,1,0:T(1,128)S(1)}, f32[19,2,1,128]{3,2,1,0:T(1,128)S(1)}, u32[]{:S(2)}, u32[]{:S(2)}) collective-permute-start(f32[19,2,1,128]{3,2,1,0:T(1,128)S(1)} %get-tuple-element.189), channel_id=1, source_target_pairs={{1,0},{2,1},{3,2},{0,3},{5,4},{6,5},{7,6},{4,7},{9,8},{10,9},{11,1... | collective-permute-start | bytes 58376 | tf_op jit(solution)/shard_map/ppermute | solution.py:51
  59.6 6.9 %collective-permute-start.15 = (f32[5,1,64,128]{3,2,1,0:T(8,128)S(1)}, f32[5,1,64,128]{3,2,1,0:T(8,128)S(1)}, u32[]{:S(2)}, u32[]{:S(2)}) collective-permute-start(f32[5,1,64,128]{3,2,1,0:T(8,128)S(1)} %get-tuple-element.252), channel_id=1, source_target_pairs={{0,124},{4,0},{8,4},{12,8},{16,12},{20,16},{24,20},{28,24},{32,28}... | collective-permute-start | bytes 491528 | tf_op jit(solution)/shard_map/ppermute | solution.py:60
  66.6 0.9 collective-permute-done.15
  67.5 1.3 %collective-permute-done.14 = f32[5,1,64,128]{3,2,1,0:T(8,128)S(1)} collective-permute-done((f32[5,1,64,128]{3,2,1,0:T(8,128)S(1)}, f32[5,1,64,128]{3,2,1,0:T(8,128)S(1)}, u32[]{:S(2)}, u32[]{:S(2)}) %collective-permute-start.14) | collective-permute-done | bytes 163872 | tf_op jit(solution)/shard_map/ppermute | solution.py:60
  70.4 1.5 %pack.1 = f32[128,128]{1,0:T(8,128)} custom-call(f32[4,128]{1,0:T(4,128)} %pad_maximum_fusion.74.t_ref, s32[8,128]{1,0:T(8,128)} %get-tuple-element.14.inv_ref), custom_call_target="tpu_custom_call" | custom-call | tf_op jit(solution)/shard_map/pack/pallas_call | solution.py:291
  71.9 10.0 %all-to-all-start = ((f32[128,1,128]{2,1,0:T(1,128)}), f32[128,1,128]{2,1,0:T(1,128)S(1)}, u32[]{:S(2)}, u32[]{:S(2)}) async-start(f32[128,1,128]{2,1,0:T(1,128)} %bitcast.878), calls=%async_computation | async-start | bytes 131072 | tf_op jit(solution)/shard_map/all_to_all | solution.py:232
  82.3 9.5 %all-to-all-done = f32[128,1,128]{2,1,0:T(1,128)S(1)} async-done(((f32[128,1,128]{2,1,0:T(1,128)}), f32[128,1,128]{2,1,0:T(1,128)S(1)}, u32[]{:S(2)}, u32[]{:S(2)}) %all-to-all-start) | async-done | bytes 65568 | tf_op jit(solution)/shard_map/all_to_all | solution.py:232
  91.8 0.6 copy-done.5
  92.5 11.1 %md.1 = (f32[3,1024]{1,0:T(4,128)}, f32[3,1024]{1,0:T(4,128)}, f32[128,128]{1,0:T(8,128)}) custom-call(f32[128,128]{1,0:T(8,128)} %bitcast.880, f32[3,8,128]{2,1,0:T(8,128)} %get-tuple-element.15.p8_ref, f32[3,8,128]{2,1,0:T(8,128)} %get-tuple-element.16.v8_ref, f32[3,8,128]{2,1,0:T(8,128)} %get-tuple-element.17.force_ref, s32[64,8,128]{2,1,0:T(8,128)} %bitcast.828, ...), custom_call_target="tpu_custom_call" | custom-call | tf_op jit(solution)/shard_map/md/pallas_call | solution.py:295
  103.5 4.1 %all-to-all-start.1 = ((f32[128,1,128]{2,1,0:T(1,128)}), f32[128,1,128]{2,1,0:T(1,128)S(1)}, u32[]{:S(2)}, u32[]{:S(2)}) async-start(f32[128,1,128]{2,1,0:T(1,128)} %bitcast.881), calls=%async_computation.1 | async-start | bytes 131072 | tf_op jit(solution)/shard_map/all_to_all | solution.py:232
  107.6 9.9 %all-to-all-done.1 = f32[128,1,128]{2,1,0:T(1,128)S(1)} async-done(((f32[128,1,128]{2,1,0:T(1,128)}), f32[128,1,128]{2,1,0:T(1,128)S(1)}, u32[]{:S(2)}, u32[]{:S(2)}) %all-to-all-start.1) | async-done | bytes 65568 | tf_op jit(solution)/shard_map/all_to_all | solution.py:232
  117.5 0.6 copy-done.4
  118.1 1.7 %cells.1 = f32[4,2,64]{2,1,0:T(2,128)} custom-call(f32[128,128]{1,0:T(8,128)} %bitcast.879, s32[2,128]{1,0:T(2,128)} %bitcast.885, s32[8,128]{1,0:T(8,128)} %get-tuple-element.23.rank_ref), custom_call_target="tpu_custom_call" | custom-call | tf_op jit(solution)/shard_map/cells/pallas_call | solution.py:299
  (240 shorter events, 13.7 us)
Async XLA Ops:
  0.6 1.7 %copy-start.1 = (f32[19,2,64,128]{3,2,1,0:T(8,128)S(1)}, f32[19,2,64,128]{3,2,1,0:T(8,128)}, u32[]{:S(2)}) copy-start(f32[19,2,64,128]{3,2,1,0:T(8,128)} %param.7) | copy-start | bytes 3735556
  0.6 1.7 %copy-start = (f32[2,64,128]{2,1,0:T(8,128)S(1)}, f32[2,64,128]{2,1,0:T(8,128)}, u32[]{:S(2)}) copy-start(f32[2,64,128]{2,1,0:T(8,128)} %param.8) | copy-start | bytes 196612
  3.3 4.5 %copy-start.3 = (s32[1024,64]{0,1:T(8,128)S(1)}, s32[1024,64]{0,1:T(8,128)}, u32[]{:S(2)}) copy-start(s32[1024,64]{0,1:T(8,128)} %param.12) | copy-start | bytes 786436
  3.4 5.2 %copy-start.6 = (s32[2,64,2]{1,2,0:T(2,128)S(1)}, s32[2,64,2]{1,2,0:T(2,128)}, u32[]{:S(2)}) copy-start(s32[2,64,2]{1,2,0:T(2,128)} %param.9) | copy-start | bytes 3076
  3.4 9.9 %collective-permute-start = (f32[19,2,1,128]{3,2,1,0:T(1,128)S(1)}, f32[19,2,1,128]{3,2,1,0:T(1,128)S(1)}, u32[]{:S(2)}, u32[]{:S(2)}) collective-permute-start(f32[19,2,1,128]{3,2,1,0:T(1,128)S(1)} %get-tuple-element.201), channel_id=1, source_target_pairs={{0,1},{1,2},{2,3},{3,0},{4,5},{5,6},{6,7},{7,4},{8,9},{9,10},{10,1... | collective-permute-start | bytes 58376 | tf_op jit(solution)/shard_map/ppermute | solution.py:49
  5.5 7.8 %collective-permute-start.1 = (f32[19,2,1,128]{3,2,1,0:T(1,128)S(1)}, f32[19,2,1,128]{3,2,1,0:T(1,128)S(1)}, u32[]{:S(2)}, u32[]{:S(2)}) collective-permute-start(f32[19,2,1,128]{3,2,1,0:T(1,128)S(1)} %get-tuple-element.202), channel_id=1, source_target_pairs={{1,0},{2,1},{3,2},{0,3},{5,4},{6,5},{7,6},{4,7},{9,8},{10,9},{11,1... | collective-permute-start | bytes 58376 | tf_op jit(solution)/shard_map/ppermute | solution.py:51
  13.8 5.9 %collective-permute-start.3 = (f32[5,1,64,128]{3,2,1,0:T(8,128)S(1)}, f32[5,1,64,128]{3,2,1,0:T(8,128)S(1)}, u32[]{:S(2)}, u32[]{:S(2)}) collective-permute-start(f32[5,1,64,128]{3,2,1,0:T(8,128)S(1)} %get-tuple-element.288), channel_id=1, source_target_pairs={{0,124},{4,0},{8,4},{12,8},{16,12},{20,16},{24,20},{28,24},{32,28}... | collective-permute-start | bytes 491528 | tf_op jit(solution)/shard_map/ppermute | solution.py:60
  15.1 6.4 %collective-permute-start.2 = (f32[5,1,64,128]{3,2,1,0:T(8,128)S(1)}, f32[5,1,64,128]{3,2,1,0:T(8,128)S(1)}, u32[]{:S(2)}, u32[]{:S(2)}) collective-permute-start(f32[5,1,64,128]{3,2,1,0:T(8,128)S(1)} %get-tuple-element.290), channel_id=1, source_target_pairs={{0,4},{4,8},{8,12},{12,16},{16,20},{20,24},{24,28},{28,32},{32,36}... | collective-permute-start | bytes 491528 | tf_op jit(solution)/shard_map/ppermute | solution.py:60
  22.9 4.2 %collective-permute-start.4 = (f32[19,2,1,128]{3,2,1,0:T(1,128)S(1)}, f32[19,2,1,128]{3,2,1,0:T(1,128)S(1)}, u32[]{:S(2)}, u32[]{:S(2)}) collective-permute-start(f32[19,2,1,128]{3,2,1,0:T(1,128)S(1)} %get-tuple-element.197), channel_id=1, source_target_pairs={{0,1},{1,2},{2,3},{3,0},{4,5},{5,6},{6,7},{7,4},{8,9},{9,10},{10,1... | collective-permute-start | bytes 58376 | tf_op jit(solution)/shard_map/ppermute | solution.py:49
  23.0 4.1 %collective-permute-start.5 = (f32[19,2,1,128]{3,2,1,0:T(1,128)S(1)}, f32[19,2,1,128]{3,2,1,0:T(1,128)S(1)}, u32[]{:S(2)}, u32[]{:S(2)}) collective-permute-start(f32[19,2,1,128]{3,2,1,0:T(1,128)S(1)} %get-tuple-element.198), channel_id=1, source_target_pairs={{1,0},{2,1},{3,2},{0,3},{5,4},{6,5},{7,6},{4,7},{9,8},{10,9},{11,1... | collective-permute-start | bytes 58376 | tf_op jit(solution)/shard_map/ppermute | solution.py:51
  27.5 9.1 %collective-permute-start.7 = (f32[5,1,64,128]{3,2,1,0:T(8,128)S(1)}, f32[5,1,64,128]{3,2,1,0:T(8,128)S(1)}, u32[]{:S(2)}, u32[]{:S(2)}) collective-permute-start(f32[5,1,64,128]{3,2,1,0:T(8,128)S(1)} %get-tuple-element.276), channel_id=1, source_target_pairs={{0,124},{4,0},{8,4},{12,8},{16,12},{20,16},{24,20},{28,24},{32,28}... | collective-permute-start | bytes 491528 | tf_op jit(solution)/shard_map/ppermute | solution.py:60
  35.7 2.3 %collective-permute-start.6 = (f32[5,1,64,128]{3,2,1,0:T(8,128)S(1)}, f32[5,1,64,128]{3,2,1,0:T(8,128)S(1)}, u32[]{:S(2)}, u32[]{:S(2)}) collective-permute-start(f32[5,1,64,128]{3,2,1,0:T(8,128)S(1)} %get-tuple-element.278), channel_id=1, source_target_pairs={{0,4},{4,8},{8,12},{12,16},{16,20},{20,24},{24,28},{28,32},{32,36}... | collective-permute-start | bytes 491528 | tf_op jit(solution)/shard_map/ppermute | solution.py:60
  39.4 4.2 %collective-permute-start.8 = (f32[19,2,1,128]{3,2,1,0:T(1,128)S(1)}, f32[19,2,1,128]{3,2,1,0:T(1,128)S(1)}, u32[]{:S(2)}, u32[]{:S(2)}) collective-permute-start(f32[19,2,1,128]{3,2,1,0:T(1,128)S(1)} %get-tuple-element.193), channel_id=1, source_target_pairs={{0,1},{1,2},{2,3},{3,0},{4,5},{5,6},{6,7},{7,4},{8,9},{9,10},{10,1... | collective-permute-start | bytes 58376 | tf_op jit(solution)/shard_map/ppermute | solution.py:49
  39.7 3.8 %collective-permute-start.9 = (f32[19,2,1,128]{3,2,1,0:T(1,128)S(1)}, f32[19,2,1,128]{3,2,1,0:T(1,128)S(1)}, u32[]{:S(2)}, u32[]{:S(2)}) collective-permute-start(f32[19,2,1,128]{3,2,1,0:T(1,128)S(1)} %get-tuple-element.194), channel_id=1, source_target_pairs={{1,0},{2,1},{3,2},{0,3},{5,4},{6,5},{7,6},{4,7},{9,8},{10,9},{11,1... | collective-permute-start | bytes 58376 | tf_op jit(solution)/shard_map/ppermute | solution.py:51
  44.0 7.8 %collective-permute-start.11 = (f32[5,1,64,128]{3,2,1,0:T(8,128)S(1)}, f32[5,1,64,128]{3,2,1,0:T(8,128)S(1)}, u32[]{:S(2)}, u32[]{:S(2)}) collective-permute-start(f32[5,1,64,128]{3,2,1,0:T(8,128)S(1)} %get-tuple-element.264), channel_id=1, source_target_pairs={{0,124},{4,0},{8,4},{12,8},{16,12},{20,16},{24,20},{28,24},{32,28}... | collective-permute-start | bytes 491528 | tf_op jit(solution)/shard_map/ppermute | solution.py:60
  50.8 2.3 %collective-permute-start.10 = (f32[5,1,64,128]{3,2,1,0:T(8,128)S(1)}, f32[5,1,64,128]{3,2,1,0:T(8,128)S(1)}, u32[]{:S(2)}, u32[]{:S(2)}) collective-permute-start(f32[5,1,64,128]{3,2,1,0:T(8,128)S(1)} %get-tuple-element.266), channel_id=1, source_target_pairs={{0,4},{4,8},{8,12},{12,16},{16,20},{20,24},{24,28},{28,32},{32,36}... | collective-permute-start | bytes 491528 | tf_op jit(solution)/shard_map/ppermute | solution.py:60
  54.7 4.4 %collective-permute-start.12 = (f32[19,2,1,128]{3,2,1,0:T(1,128)S(1)}, f32[19,2,1,128]{3,2,1,0:T(1,128)S(1)}, u32[]{:S(2)}, u32[]{:S(2)}) collective-permute-start(f32[19,2,1,128]{3,2,1,0:T(1,128)S(1)} %get-tuple-element.190), channel_id=1, source_target_pairs={{0,1},{1,2},{2,3},{3,0},{4,5},{5,6},{6,7},{7,4},{8,9},{9,10},{10,1... | collective-permute-start | bytes 58376 | tf_op jit(solution)/shard_map/ppermute | solution.py:49
  56.1 3.1 %collective-permute-start.13 = (f32[19,2,1,128]{3,2,1,0:T(1,128)S(1)}, f32[19,2,1,128]{3,2,1,0:T(1,128)S(1)}, u32[]{:S(2)}, u32[]{:S(2)}) collective-permute-start(f32[19,2,1,128]{3,2,1,0:T(1,128)S(1)} %get-tuple-element.189), channel_id=1, source_target_pairs={{1,0},{2,1},{3,2},{0,3},{5,4},{6,5},{7,6},{4,7},{9,8},{10,9},{11,1... | collective-permute-start | bytes 58376 | tf_op jit(solution)/shard_map/ppermute | solution.py:51
  59.6 7.9 %collective-permute-start.15 = (f32[5,1,64,128]{3,2,1,0:T(8,128)S(1)}, f32[5,1,64,128]{3,2,1,0:T(8,128)S(1)}, u32[]{:S(2)}, u32[]{:S(2)}) collective-permute-start(f32[5,1,64,128]{3,2,1,0:T(8,128)S(1)} %get-tuple-element.252), channel_id=1, source_target_pairs={{0,124},{4,0},{8,4},{12,8},{16,12},{20,16},{24,20},{28,24},{32,28}... | collective-permute-start | bytes 491528 | tf_op jit(solution)/shard_map/ppermute | solution.py:60
  66.5 2.3 %collective-permute-start.14 = (f32[5,1,64,128]{3,2,1,0:T(8,128)S(1)}, f32[5,1,64,128]{3,2,1,0:T(8,128)S(1)}, u32[]{:S(2)}, u32[]{:S(2)}) collective-permute-start(f32[5,1,64,128]{3,2,1,0:T(8,128)S(1)} %get-tuple-element.253), channel_id=1, source_target_pairs={{0,4},{4,8},{8,12},{12,16},{16,20},{20,24},{24,28},{28,32},{32,36}... | collective-permute-start | bytes 491528 | tf_op jit(solution)/shard_map/ppermute | solution.py:60
  71.9 20.0 %all-to-all-start = ((f32[128,1,128]{2,1,0:T(1,128)}), f32[128,1,128]{2,1,0:T(1,128)S(1)}, u32[]{:S(2)}, u32[]{:S(2)}) async-start(f32[128,1,128]{2,1,0:T(1,128)} %bitcast.878), calls=%async_computation | async-start | bytes 131072 | tf_op jit(solution)/shard_map/all_to_all | solution.py:232
  91.8 0.6 copy-start.5
  103.5 14.0 %all-to-all-start.1 = ((f32[128,1,128]{2,1,0:T(1,128)}), f32[128,1,128]{2,1,0:T(1,128)S(1)}, u32[]{:S(2)}, u32[]{:S(2)}) async-start(f32[128,1,128]{2,1,0:T(1,128)} %bitcast.881), calls=%async_computation.1 | async-start | bytes 131072 | tf_op jit(solution)/shard_map/all_to_all | solution.py:232
  107.6 12.2 %copy-start.2 = (f32[19,2,64,128]{3,2,1,0:T(8,128)}, f32[19,2,64,128]{3,2,1,0:T(8,128)S(1)}, u32[]{:S(2)}) copy-start(f32[19,2,64,128]{3,2,1,0:T(8,128)S(1)} %constant_dynamic-update-slice_fusion.116) | copy-start | bytes 3735556
  117.5 0.6 copy-start.4
where the time goes:
time: 120 us
  starting transfers between devices  51.7 us (43%)
  waiting for transfers between devices  31.8 us (26%)
  Pallas kernels  18.3 us (15%)
  other arithmetic  9.22 us (8%)
  local copies, waits for them, and re-layouts  6.97 us (6%)
  between operations  1.76 us (1%)
    ppermute x8, starting transfers between devices, shifted(): lax.ppermute(shard, axis, [(i, (i + by) % devices) for i in range(devices)])  25 us
    all_to_all x2, waiting for transfers between devices, exchange(): lax.all_to_all(rows, ('slab', 'md'), split_axis=0, concat_axis=0, tiled=T...  19.4 us
    all_to_all x2, starting transfers between devices, exchange(): lax.all_to_all(rows, ('slab', 'md'), split_axis=0, concat_axis=0, tiled=T...  14.1 us
    ppermute x8, waiting for transfers between devices, shifted(): lax.ppermute(shard, axis, [(i, (i + by) % devices) for i in range(devices)])  11.4 us
    pallas_call x1, Pallas kernels, on_device(): pl.pallas_call(md_kernel, out_shape=(shape(3, 1024), shape(3, 1024), shap...  11.1 us
    ppermute x4, starting transfers between devices, padded_2(): lax.ppermute(head, axis, [((i + 1) % count, i) for i in range(count)])  8.75 us
    unnamed x86, other arithmetic  4.74 us
    pallas_call x1, Pallas kernels, on_device(): pl.pallas_call(prep_kernel, out_shape=(shape(8, 128, dtype=i32), shape(8,...  4.12 us
  transfers between devices with their start and end apart: 18, of which 13 were waited for; matrix products, arithmetic and copies ran while one was open for 4% of the time, Pallas kernels for 3%

commit v1 on v0

--- a/solution.py
+++ b/solution.py
@@ -5,7 +5,6 @@
 from jax.experimental.pallas import tpu as pltpu
 from jax.sharding import PartitionSpec as P
 
-LB_STEPS = 4
 MD_STEPS = 5
 f32 = jnp.float32
 i32 = jnp.int32
@@ -39,50 +38,308 @@
 time_step = 0.1
 
 
-def padded_2(cells, sides, width):
-    for axis, dim in sides:
-        count = lax.axis_size(axis)
-        head = lax.slice_in_dim(cells, 0, width, axis=dim)
-        tail = lax.slice_in_dim(cells, cells.shape[dim] - width, cells.shape[dim], axis=dim)
-        cells = jnp.concatenate(
-            [
-                lax.ppermute(tail, axis, [(i, (i + 1) % count) for i in range(count)]),
-                cells,
-                lax.ppermute(head, axis, [((i + 1) % count, i) for i in range(count)]),
-            ],
-            axis=dim,
-        )
-    return cells
-
-
-def shifted(shard, axis, by):
-    devices = lax.axis_size(axis)
-    return lax.ppermute(shard, axis, [(i, (i + by) % devices) for i in range(devices)])
-
-
-def velocity(f, density):
-    comps = []
+def mirrored(direction):
+    return lattice_dirs.index((direction[0], direction[1], -direction[2]))
+
+
+flip = [mirrored(c) for c in lattice_dirs]
+rising = [i for i, c in enumerate(lattice_dirs) if c[2] == 1]
+falling = [flip[i] for i in rising]
+level = [i for i, c in enumerate(lattice_dirs) if c[2] == 0]
+pairs = [(1, 2), (3, 4), (5, 6)] + [(i, i + 1) for i in range(7, 19, 2)]
+NEAR = 14
+RELAX = 19
+ROWS = 72
+PAD = 88
+
+
+def parity():
+    return lax.axis_index("slab") & 1
+
+
+def actual(index, odd):
+    return jnp.where(odd == 1, flip[index], index)
+
+
+def moments_of(f):
+    s = {}
+    for plus, minus in pairs:
+        s[plus] = (f[plus] + f[minus], f[plus] - f[minus])
+    density = f[0]
+    for plus, _ in pairs:
+        density = density + s[plus][0]
+    flow = []
     for axis_id in range(3):
-        total = jnp.zeros_like(density)
-        for index, direction in enumerate(lattice_dirs):
-            if direction[axis_id] != 0:
-                total = total + direction[axis_id] * f[index]
-        comps.append(total / density)
-    return comps
-
-
-def collide(f, relax):
-    density = jnp.sum(f, axis=0)
-    vel_x, vel_y, vel_z = velocity(f, density)
-    usq = vel_x * vel_x + vel_y * vel_y + vel_z * vel_z
-    result = []
-    for index, direction in enumerate(lattice_dirs):
-        along = direction[0] * vel_x + direction[1] * vel_y + direction[2] * vel_z
-        equil = (
-            lattice_weights[index] * density * (1.0 + 3.0 * along + 4.5 * along * along - 1.5 * usq)
-        )
-        result.append(f[index] - relax * (f[index] - equil))
-    return result
+        total = None
+        for plus, _ in pairs:
+            sign = lattice_dirs[plus][axis_id]
+            if sign == 0:
+                continue
+            term = s[plus][1]
+            if total is None:
+                total = term
+            else:
+                total = total + term if sign > 0 else total - term
+        flow.append(total)
+    return density, flow
+
+
+def collided(f, relax, wanted):
+    density, flow = moments_of(f)
+    inverse = 1.0 / density
+    vel = [j * inverse for j in flow]
+    usq = vel[0] * vel[0] + vel[1] * vel[1] + vel[2] * vel[2]
+    keep = 1.0 - relax
+    gain = relax * density
+    base = gain - (1.5 * gain) * usq
+    result = {}
+    if 0 in wanted:
+        result[0] = keep * f[0] + lattice_weights[0] * base
+    for plus, minus in pairs:
+        if plus not in wanted and minus not in wanted:
+            continue
+        along = None
+        for axis_id in range(3):
+            sign = lattice_dirs[plus][axis_id]
+            if sign != 0:
+                part = vel[axis_id]
+                if along is None:
+                    along = part
+                else:
+                    along = along + part if sign > 0 else along - part
+        weight = lattice_weights[plus]
+        slope = (3.0 * weight) * (gain * along)
+        even = weight * base + 1.5 * (along * slope)
+        if plus in wanted:
+            result[plus] = keep * f[plus] + (even + slope)
+        if minus in wanted:
+            result[minus] = keep * f[minus] + (even - slope)
+    return {i: rolled(v, lattice_dirs[i][1]) for i, v in result.items()}
+
+
+def rolled(block, by):
+    return block if by == 0 else pltpu.roll(block, by % 128, 1)
+
+
+def put(ref, where, block_id, value):
+    ref[(*where, pl.ds(8 + 8 * block_id, 8), slice(None))] = value
+    if block_id == 0:
+        ref[(*where, pl.ds(8 + ROWS, 1), slice(None))] = value[0:1, :]
+    if block_id == 8:
+        ref[(*where, pl.ds(7, 1), slice(None))] = value[7:8, :]
+
+
+def get(ref, where, block_id, shift):
+    return ref[(*where, pl.ds(8 + 8 * block_id - shift, 8), slice(None))]
+
+
+def rows_of(block_id):
+    return pl.ds(8 * block_id, 8)
+
+
+def send_planes(up_ref, down_ref, plane, block, post, relax):
+    for k in range(5):
+        up_ref[k if plane == 1 else NEAR + k, block, :] = post[rising[k]]
+        down_ref[k if plane == 0 else NEAR + k, block, :] = post[falling[k]]
+    near_ref = up_ref if plane == 1 else down_ref
+    for k, i in enumerate(level):
+        near_ref[5 + k, block, :] = post[i]
+    if relax is not None:
+        near_ref[RELAX, block, :] = relax
+
+
+everything = set(range(19))
+
+
+def first_kernel(f_ref, relax_ref, post_ref, up_ref, down_ref, low_ref, high_ref):
+    odd = parity()
+    for plane in range(2):
+        actual_plane = jnp.where(odd == 1, 1 - plane, plane)
+        for b in range(8):
+            f = {i: f_ref[actual(i, odd), actual_plane, rows_of(b), :] for i in range(19)}
+            relax = relax_ref[actual_plane, rows_of(b), :]
+            if b in (0, 7):
+                edge_ref = low_ref if b == 0 else high_ref
+                for i in range(19):
+                    edge_ref[i, plane] = f[i]
+                edge_ref[RELAX, plane] = relax
+            post = collided(f, relax, everything)
+            for i in range(19):
+                post_ref[i, plane, rows_of(b), :] = post[i]
+            send_planes(up_ref, down_ref, plane, rows_of(b), post, relax)
+
+
+def edge_kernel(low_ref, high_ref, post_ref, up_ref, down_ref, relax_ref):
+    head = lax.broadcasted_iota(i32, (8, 128), 0) < 4
+    for plane in range(2):
+        mixed = [jnp.where(head, high_ref[i, plane], low_ref[i, plane]) for i in range(20)]
+        post = collided(dict(enumerate(mixed[:19])), mixed[RELAX], everything)
+        relax_ref[plane] = mixed[RELAX]
+        for i in range(19):
+            post_ref[i, plane] = post[i]
+        send_planes(up_ref, down_ref, plane, rows_of(0), post, mixed[RELAX])
+
+
+def two_steps(own, below, above, relax, second_ref, from_below_ref, from_above_ref):
+    for b in range(9):
+        for plane in (-1, 0, 1, 2):
+            f = {}
+            for i, c in enumerate(lattice_dirs):
+                source = plane - c[2]
+                if source in (0, 1):
+                    f[i] = own(i, source, b, c[0])
+                else:
+                    side = below if source < 0 else above
+                    if c[2] == 0:
+                        j = 5 + level.index(i)
+                    else:
+                        j = (rising if c[2] == 1 else falling).index(i)
+                        if source in (-2, 3):
+                            j = NEAR + j
+                    f[i] = side(j, b, c[0])
+            wanted = everything
+            if plane == -1:
+                wanted = set(rising)
+            elif plane == 2:
+                wanted = set(falling)
+            post = collided(f, relax(plane, b), wanted)
+            for i, value in post.items():
+                if plane == -1:
+                    put(from_below_ref, (rising.index(i),), b, value)
+                elif plane == 2:
+                    put(from_above_ref, (falling.index(i),), b, value)
+                else:
+                    put(second_ref, (i, plane), b, value)
+
+
+def streamed(second_ref, from_below_ref, from_above_ref, plane, b):
+    f = {}
+    for i, c in enumerate(lattice_dirs):
+        source = plane - c[2]
+        if source == -1:
+            f[i] = get(from_below_ref, (rising.index(i),), b, c[0])
+        elif source == 2:
+            f[i] = get(from_above_ref, (falling.index(i),), b, c[0])
+        else:
+            f[i] = get(second_ref, (i, source), b, c[0])
+    return f
+
+
+sliding = [k for k, i in enumerate(rising + level + rising) if lattice_dirs[i][0] != 0]
+moving = [i for i, c in enumerate(lattice_dirs) if c[0] != 0]
+
+
+def seamed(seam_ref, slots, at):
+    for slot, key in enumerate(slots):
+        for part, b in enumerate((7, 8, 0)):
+            seam_ref[slot, 8 * part : 8 * part + 8, :] = at(key, b)
+
+    def read(key, b, shift, main):
+        if shift == 0:
+            return at(key, b)
+        slot = slots.index(key)
+        if b == 8:
+            return seam_ref[slot, 8 - shift : 16 - shift, :]
+        if b == 0 and shift == 1:
+            return seam_ref[slot, 15:23, :]
+        if b == 7 and shift == -1:
+            return seam_ref[slot, 1:9, :]
+        return main(8 * b - shift)
+
+    return read
+
+
+def reader(seam_ref, main_ref, edge_ref):
+    def at(j, b):
+        if edge_ref is None or b < 8:
+            return main_ref[j, rows_of(b), :]
+        return edge_ref[j, rows_of(0), :]
+
+    read = seamed(seam_ref, sliding, at)
+    return lambda j, b, shift: read(j, b, shift, lambda row: main_ref[j, row : row + 8, :])
+
+
+def own_reader(seam_ref, main_ref, edge_ref):
+    def at(key, b):
+        i, plane = key
+        return main_ref[i, plane, rows_of(b), :] if b < 8 else edge_ref[i, plane]
+
+    read = seamed(seam_ref, [(i, plane) for i in moving for plane in range(2)], at)
+    return lambda i, plane, b, shift: read(
+        (i, plane), b, shift, lambda row: main_ref[i, plane, row : row + 8, :]
+    )
+
+
+def middle_kernel(post_ref, post_edge_ref, below_ref, above_ref, below_edge_ref, above_edge_ref,
+                  relax_ref, relax_edge_ref,
+                  third_ref, up_ref, down_ref, relax_out_ref,
+                  second_ref, from_below_ref, from_above_ref, below_seam_ref, above_seam_ref,
+                  own_seam_ref):
+    odd = parity()
+    own = own_reader(own_seam_ref, post_ref, post_edge_ref)
+    below = reader(below_seam_ref, below_ref, below_edge_ref)
+    above = reader(above_seam_ref, above_ref, above_edge_ref)
+    for b in range(8):
+        relax_out_ref[0, rows_of(b), :] = below_ref[RELAX, rows_of(b), :]
+        relax_out_ref[3, rows_of(b), :] = above_ref[RELAX, rows_of(b), :]
+        for plane in range(2):
+            relax_out_ref[1 + plane, rows_of(b), :] = relax_ref[
+                jnp.where(odd == 1, 1 - plane, plane), rows_of(b), :
+            ]
+    relax_out_ref[0, rows_of(8), :] = below_edge_ref[RELAX, rows_of(0), :]
+    relax_out_ref[3, rows_of(8), :] = above_edge_ref[RELAX, rows_of(0), :]
+    for plane in range(2):
+        relax_out_ref[1 + plane, rows_of(8), :] = relax_edge_ref[plane]
+
+    def relax(plane, b):
+        return relax_out_ref[1 + plane, rows_of(b), :]
+
+    two_steps(own, below, above, relax, second_ref, from_below_ref, from_above_ref)
+    for b in range(9):
+        for plane in range(2):
+            f = streamed(second_ref, from_below_ref, from_above_ref, plane, b)
+            post = collided(f, relax(plane, b), everything)
+            for i in range(19):
+                put(third_ref, (i, plane), b, post[i])
+            send_planes(up_ref, down_ref, plane, rows_of(b), post, None)
+
+
+def last_kernel(post_ref, below_ref, above_ref, relax_ref, inv_ref,
+                f_ref, out_ref,
+                second_ref, from_below_ref, from_above_ref, below_seam_ref, above_seam_ref,
+                flow_ref):
+    odd = parity()
+    below = reader(below_seam_ref, below_ref, None)
+    above = reader(above_seam_ref, above_ref, None)
+
+    def own(i, plane, b, shift):
+        return get(post_ref, (i, plane), b, shift)
+
+    def relax(plane, b):
+        return relax_ref[1 + plane, rows_of(b), :]
+
+    two_steps(own, below, above, relax, second_ref, from_below_ref, from_above_ref)
+    upward = jnp.where(odd == 1, -velocity_scale / 128.0, velocity_scale / 128.0)
+    for plane in range(2):
+        actual_plane = jnp.where(odd == 1, 1 - plane, plane)
+        for b in range(8):
+            f = streamed(second_ref, from_below_ref, from_above_ref, plane, b)
+            for i in range(19):
+                f_ref[actual(i, odd), actual_plane, rows_of(b), :] = f[i]
+            density, flow = moments_of(f)
+            inverse = 1.0 / density
+            where = pl.ds(pl.multiple_of(actual_plane * 64 + 8 * b, 8), 8)
+            flow_ref[0, where, :] = flow[0] * inverse * (velocity_scale / 128.0)
+            flow_ref[1, where, :] = flow[1] * inverse * (velocity_scale / 128.0)
+            flow_ref[2, where, :] = flow[2] * inverse * upward
+            flow_ref[3, where, :] = density * (1.0 / 128.0)
+    means = [jnp.sum(flow_ref[c].T, axis=0, keepdims=True) for c in range(4)]
+    packed = jnp.concatenate(means * 4, axis=0)
+    inv16 = jnp.concatenate(
+        [jnp.broadcast_to(inv_ref[r : r + 1, :], (4, 128)) for r in range(4)], axis=0
+    )
+    picked = jnp.where(inv16 >= 0, lanes(packed, jnp.maximum(inv16, 0)), 0.0)
+    out_ref[...] = jnp.concatenate([picked, jnp.zeros((112, 128), f32)], axis=0).T
 
 
 def lanes(table, index):
@@ -155,15 +412,6 @@
     total = pair_sum([p8_ref[0], p8_ref[1], p8_ref[2]], nbr_ref)
     for c in range(3):
         force_ref[c] = total[c]
-
-
-def pack_kernel(t_ref, inv_ref, out_ref):
-    t16 = jnp.concatenate([t_ref[...]] * 4, axis=0)
-    inv16 = jnp.concatenate(
-        [jnp.broadcast_to(inv_ref[r : r + 1, :], (4, 128)) for r in range(4)], axis=0
-    )
-    picked = jnp.where(inv16 >= 0, lanes(t16, jnp.maximum(inv16, 0)), 0.0)
-    out_ref[...] = jnp.concatenate([picked, jnp.zeros((112, 128), f32)], axis=0).T
 
 
 def md_kernel(arr_ref, p8_ref, v8_ref, force_ref, nbr_ref, slot_ref, hot_ref, icnt_ref,
@@ -232,6 +480,10 @@
     return lax.all_to_all(rows, ("slab", "md"), split_axis=0, concat_axis=0, tiled=True)
 
 
+near_pairs = [(i, i ^ 1) for i in range(32)]
+far_pairs = [(i, (i + 1) % 32 if i % 2 else (i - 1) % 32) for i in range(32)]
+
+
 def on_device(populations, relax, owners, positions, velocities, neighbours, atom_slots):
     own = owners.reshape(128, 2).T
     slots = atom_slots.reshape(8, 128)
@@ -249,48 +501,59 @@
         ),
         name="prep",
     )(own, slots, positions, velocities, nbr)
-    f = populations
-    cz_len = f.shape[1]
-    cx_len = f.shape[2]
-    rising = [i for i, c in enumerate(lattice_dirs) if c[2] == 1]
-    falling = [i for i, c in enumerate(lattice_dirs) if c[2] == -1]
-    for step in range(LB_STEPS):
-        post = jnp.stack(collide(f, relax))
-        padded = padded_2(post, (("md", 2),), 1)
-        moved = jnp.stack(
-            [
-                jnp.roll(padded[i, :, 1 - c[0] : 1 - c[0] + cx_len, :], c[1], axis=2)
-                for i, c in enumerate(lattice_dirs)
-            ]
-        )
-        top_planes = jnp.stack([moved[i, cz_len - 1 :] for i in rising])
-        low_planes = jnp.stack([moved[i, :1] for i in falling])
-        below = shifted(top_planes, "slab", 1)
-        above = shifted(low_planes, "slab", -1)
-        pieces = []
-        for i, c in enumerate(lattice_dirs):
-            if c[2] == 1:
-                pieces.append(
-                    jnp.concatenate([below[rising.index(i)], moved[i, : cz_len - 1]], axis=0)
-                )
-            elif c[2] == -1:
-                pieces.append(jnp.concatenate([moved[i, 1:], above[falling.index(i)]], axis=0))
-            else:
-                pieces.append(moved[i])
-        f = jnp.stack(pieces)
-    density = jnp.sum(f, axis=0)
-    vel_x, vel_y, vel_z = velocity(f, density)
-    targets = jnp.stack(
-        [
-            jnp.mean(velocity_scale * vel_x, axis=2),
-            jnp.mean(velocity_scale * vel_y, axis=2),
-            jnp.mean(velocity_scale * vel_z, axis=2),
-            jnp.mean(density, axis=2),
-        ]
-    )
-    outgoing = pl.pallas_call(pack_kernel, out_shape=shape(128, 128), name="pack")(
-        targets.reshape(4, 128), inv
-    )
+    post, up, down, low, high = pl.pallas_call(
+        first_kernel,
+        out_shape=(
+            shape(19, 2, 64, 128),
+            shape(20, 64, 128),
+            shape(20, 64, 128),
+            shape(20, 2, 8, 128),
+            shape(20, 2, 8, 128),
+        ),
+        name="first",
+    )(populations, relax)
+    below = lax.ppermute(down, "slab", far_pairs)
+    above = lax.ppermute(up, "slab", near_pairs)
+    from_low = lax.ppermute(high, "md", [(i, (i + 1) % 4) for i in range(4)])
+    from_high = lax.ppermute(low, "md", [((i + 1) % 4, i) for i in range(4)])
+    post_edge, up_edge, down_edge, relax_edge = pl.pallas_call(
+        edge_kernel,
+        out_shape=(
+            shape(19, 2, 8, 128),
+            shape(20, 8, 128),
+            shape(20, 8, 128),
+            shape(2, 8, 128),
+        ),
+        name="edge",
+    )(from_low, from_high)
+    below_edge = lax.ppermute(down_edge, "slab", far_pairs)
+    above_edge = lax.ppermute(up_edge, "slab", near_pairs)
+    scratch = [
+        pltpu.VMEM((19, 2, PAD, 128), f32),
+        pltpu.VMEM((5, PAD, 128), f32),
+        pltpu.VMEM((5, PAD, 128), f32),
+        pltpu.VMEM((len(sliding), 24, 128), f32),
+        pltpu.VMEM((len(sliding), 24, 128), f32),
+    ]
+    post, up, down, relax_all = pl.pallas_call(
+        middle_kernel,
+        out_shape=(
+            shape(19, 2, PAD, 128),
+            shape(19, ROWS, 128),
+            shape(19, ROWS, 128),
+            shape(4, ROWS, 128),
+        ),
+        scratch_shapes=scratch + [pltpu.VMEM((2 * len(moving), 24, 128), f32)],
+        name="middle",
+    )(post, post_edge, below, above, below_edge, above_edge, relax, relax_edge)
+    below = lax.ppermute(down, "slab", far_pairs)
+    above = lax.ppermute(up, "slab", near_pairs)
+    f, outgoing = pl.pallas_call(
+        last_kernel,
+        out_shape=(shape(19, 2, 64, 128), shape(128, 128)),
+        scratch_shapes=scratch + [pltpu.VMEM((4, 128, 128), f32)],
+        name="last",
+    )(post, below, above, relax_all, inv)
     arrived = exchange(outgoing)
     pos_out, vel_out, moms = pl.pallas_call(
         md_kernel, out_shape=(shape(3, 1024), shape(3, 1024), shape(128, 128)), name="md"

time: 120 us -> 97.3 us (0.81)
  blocking collectives: 0 us -> 36.8 us
  starting transfers between devices: 51.7 us -> 15.2 us
  waiting for transfers between devices: 31.8 us -> 8.91 us
  Pallas kernels: 18.3 us -> 30.4 us
  other arithmetic: 9.22 us -> 0 us
  local copies, waits for them, and re-layouts: 6.97 us -> 4.94 us
    all_to_all x0 -> x2, blocking collectives: none -> 36.8 us  [exchange(): lax.all_to_all(rows, ('slab', 'md'), split_axis=0, concat_axis=0, tiled=T...]
    ppermute x16 -> x8, starting transfers between devices: 37.6 us -> 15.2 us  [the longest x2 8.62 us: on_device(): above = lax.ppermute(up, 'slab', near_pairs)]
    all_to_all x2 -> x0, waiting for transfers between devices: 19.4 us -> none  [exchange(): lax.all_to_all(rows, ('slab', 'md'), split_axis=0, concat_axis=0, tiled=T...]
    all_to_all x2 -> x0, starting transfers between devices: 14.1 us -> none  [exchange(): lax.all_to_all(rows, ('slab', 'md'), split_axis=0, concat_axis=0, tiled=T...]
    pallas_call x1 -> x4, Pallas kernels: 1.5 us -> 13.5 us  [the longest x1 4.62 us: on_device(): pl.pallas_call(middle_kernel, out_shape=(shape(19, 2, PAD, 128), shape(19...]
    unnamed x86 -> x0, other arithmetic: 4.74 us -> none
    ppermute x16 -> x8, waiting for transfers between devices: 12.4 us -> 8.91 us  [the longest x1 4.5 us: on_device(): from_low = lax.ppermute(high, 'md', [(i, (i + 1) % 4) for i in range(4)])]
    slice x44 -> x0, local copies, waits for them, and re-layouts: 3.37 us -> none  [the longest x40 3.25 us: on_device(): jnp.roll(padded[i, :, 1 - c[0]:1 - c[0] + cx_len, :], c[1], axis=2)]
  transfers between devices with their start and end apart: 18 -> 8, of which waited for: 13 -> 3; matrix products, arithmetic and copies ran while one was open for 4% -> 1% of each run, Pallas kernels for 3% -> 6%
where the time goes in v1:
time: 97.3 us; the launch traced here: 97 us
  blocking collectives  36.8 us (38%)
  Pallas kernels  30.4 us (31%)
  starting transfers between devices  15.2 us (16%)
  waiting for transfers between devices  8.91 us (9%)
  local copies, waits for them, and re-layouts  4.94 us (5%)
    all_to_all x2, blocking collectives, exchange(): lax.all_to_all(rows, ('slab', 'md'), split_axis=0, concat_axis=0, tiled=T...  36.8 us
    pallas_call x1, Pallas kernels, on_device(): pl.pallas_call(md_kernel, out_shape=(shape(3, 1024), shape(3, 1024), shap...  11.1 us
    ppermute x2, starting transfers between devices, on_device(): above = lax.ppermute(up, 'slab', near_pairs)  8.62 us
    pallas_call x1, Pallas kernels, on_device(): pl.pallas_call(middle_kernel, out_shape=(shape(19, 2, PAD, 128), shape(19...  4.62 us
    ppermute x1, waiting for transfers between devices, on_device(): from_low = lax.ppermute(high, 'md', [(i, (i + 1) % 4) for i in range(4)])  4.5 us
    unnamed x22, local copies, waits for them, and re-layouts  4.27 us
    pallas_call x1, Pallas kernels, on_device(): pl.pallas_call(prep_kernel, out_shape=(shape(8, 128, dtype=i32), shape(8,...  4.12 us
    pallas_call x1, Pallas kernels, on_device(): pl.pallas_call(last_kernel, out_shape=(shape(19, 2, 64, 128), shape(128,...  3.78 us
  transfers between devices with their start and end apart: 8, of which 3 were waited for; matrix products, arithmetic and copies ran while one was open for 1% of the time, Pallas kernels for 6%

profile of v1, /device:TPU:1, one launch (start us, length us, event | category | flops | bytes accessed | tf_op | source)
XLA Modules:
  0.0 97.0 jit_solution(917121006438291023)
XLA Ops:
  0.6 3.3 %first.1 = (f32[19,2,64,128]{3,2,1,0:T(8,128)}, f32[20,64,128]{2,1,0:T(8,128)}, f32[20,64,128]{2,1,0:T(8,128)}, f32[20,2,8,128]{3,2,1,0:T(8,128)}, f32[20,2,8,128]{3,2,1,0:T(8,128)}) custom-call(f32[19,2,64,128]{3,2,1,0:T(8,128)} %f_ref.1, f32[2,64,128]{2,1,0:T(8,128)} %relax_ref.3), custom_call_target="tpu_custom_call" | custom-call | tf_op jit(solution)/shard_map/first/pallas_call | solution.py:504
  4.0 3.0 %collective-permute-start.2 = (f32[20,64,128]{2,1,0:T(8,128)}, f32[20,64,128]{2,1,0:T(8,128)S(1)}, u32[]{:S(2)}, u32[]{:S(2)}) collective-permute-start(f32[20,64,128]{2,1,0:T(8,128)} %get-tuple-element.33), channel_id=1, source_target_pairs={{0,124},{4,8},{8,4},{12,16},{16,12},{20,24},{24,20},{28,32},{32,28... | collective-permute-start | bytes 1966088 | tf_op jit(solution)/shard_map/ppermute | solution.py:515
  7.0 4.4 %collective-permute-start.3 = (f32[20,64,128]{2,1,0:T(8,128)}, f32[20,64,128]{2,1,0:T(8,128)S(1)}, u32[]{:S(2)}, u32[]{:S(2)}) collective-permute-start(f32[20,64,128]{2,1,0:T(8,128)} %get-tuple-element.34), channel_id=1, source_target_pairs={{0,4},{4,0},{8,12},{12,8},{16,20},{20,16},{24,28},{28,24},{32,36},... | collective-permute-start | bytes 1966088 | tf_op jit(solution)/shard_map/ppermute | solution.py:516
  11.4 1.2 %collective-permute-start = (f32[20,2,8,128]{3,2,1,0:T(8,128)}, f32[20,2,8,128]{3,2,1,0:T(8,128)S(1)}, u32[]{:S(2)}, u32[]{:S(2)}) collective-permute-start(f32[20,2,8,128]{3,2,1,0:T(8,128)} %get-tuple-element.30), channel_id=1, source_target_pairs={{0,1},{1,2},{2,3},{3,0},{4,5},{5,6},{6,7},{7,4},{8,9},{9,10},{10,1... | collective-permute-start | bytes 491528 | tf_op jit(solution)/shard_map/ppermute | solution.py:517
  12.6 1.5 %collective-permute-start.1 = (f32[20,2,8,128]{3,2,1,0:T(8,128)}, f32[20,2,8,128]{3,2,1,0:T(8,128)S(1)}, u32[]{:S(2)}, u32[]{:S(2)}) collective-permute-start(f32[20,2,8,128]{3,2,1,0:T(8,128)} %get-tuple-element.31), channel_id=1, source_target_pairs={{1,0},{2,1},{3,2},{0,3},{5,4},{6,5},{7,6},{4,7},{9,8},{10,9},{11,1... | collective-permute-start | bytes 491528 | tf_op jit(solution)/shard_map/ppermute | solution.py:518
  14.1 4.5 %collective-permute-done.low_ref = f32[20,2,8,128]{3,2,1,0:T(8,128)S(1)} collective-permute-done((f32[20,2,8,128]{3,2,1,0:T(8,128)}, f32[20,2,8,128]{3,2,1,0:T(8,128)S(1)}, u32[]{:S(2)}, u32[]{:S(2)}) %collective-permute-start) | collective-permute-done | bytes 163872 | tf_op jit(solution)/shard_map/ppermute | solution.py:517
  18.6 0.0 collective-permute-done.1.high_ref
  18.6 0.7 copy-done.5
  19.2 0.7 copy-done.6
  19.9 1.8 %edge.1 = (f32[19,2,8,128]{3,2,1,0:T(8,128)}, f32[20,8,128]{2,1,0:T(8,128)}, f32[20,8,128]{2,1,0:T(8,128)}, f32[2,8,128]{2,1,0:T(8,128)}) custom-call(f32[20,2,8,128]{3,2,1,0:T(8,128)} %copy-done.5, f32[20,2,8,128]{3,2,1,0:T(8,128)} %copy-done.6), custom_call_target="tpu_custom_call" | custom-call | tf_op jit(solution)/shard_map/edge/pallas_call | solution.py:519
  21.7 0.0 collective-permute-start.4
  21.7 0.9 collective-permute-start.5
  22.6 3.2 %collective-permute-done.4.below_edge_ref = f32[20,8,128]{2,1,0:T(8,128)S(1)} collective-permute-done((f32[20,8,128]{2,1,0:T(8,128)}, f32[20,8,128]{2,1,0:T(8,128)S(1)}, u32[]{:S(2)}, u32[]{:S(2)}) %collective-permute-start.4) | collective-permute-done | bytes 81952 | tf_op jit(solution)/shard_map/ppermute | solution.py:529
  25.8 0.0 collective-permute-done.5.above_edge_ref
  25.8 0.6 copy-done.7
  26.4 0.0 copy-done.8
  26.5 0.2 copy-done.2
  26.7 0.2 copy-done.3
  26.9 4.6 %middle.1 = (f32[19,2,88,128]{3,2,1,0:T(8,128)}, f32[19,72,128]{2,1,0:T(8,128)}, f32[19,72,128]{2,1,0:T(8,128)}, f32[4,72,128]{2,1,0:T(8,128)}) custom-call(f32[19,2,64,128]{3,2,1,0:T(8,128)} %get-tuple-element.29.post_ref, f32[19,2,8,128]{3,2,1,0:T(8,128)} %get-tuple-element.32.post_edge_ref, f32[20,64,128]{2,1,0:T(8,128)} %copy-done.2, ...), custom_call_target="tpu_custom_call" | custom-call | tf_op jit(solution)/shard_map/middle/pallas_call | solution.py:538
  31.5 0.0 collective-permute-start.6
  31.6 4.2 %collective-permute-start.7 = (f32[19,72,128]{2,1,0:T(8,128)}, f32[19,72,128]{2,1,0:T(8,128)S(1)}, u32[]{:S(2)}, u32[]{:S(2)}) collective-permute-start(f32[19,72,128]{2,1,0:T(8,128)} %get-tuple-element.40), channel_id=1, source_target_pairs={{0,4},{4,0},{8,12},{12,8},{16,20},{20,16},{24,28},{28,24},{32,36},... | collective-permute-start | bytes 2101256 | tf_op jit(solution)/shard_map/ppermute | solution.py:550
  35.8 0.7 copy.15
  36.5 0.7 reshape.21
  37.2 4.1 %prep.1 = (s32[8,128]{1,0:T(8,128)}, s32[8,128]{1,0:T(8,128)}, bf16[128,1024]{1,0:T(8,128)(2,1)}, f32[128,16]{1,0:T(8,128)}, f32[3,8,128]{2,1,0:T(8,128)}, /*index=5*/f32[3,8,128]{2,1,0:T(8,128)}, f32[3,8,128]{2,1,0:T(8,128)}) custom-call(s32[2,128]{1,0:T(2,128)} %bitcast.27, s32[8,128]{1,0:T(8,128)} %bitcast.25, f32[3,1024]{1,0:T(4,128)} %pos_ref.1, ...), custom_call_target="tpu_custom_call" | custom-call | tf_op jit(solution)/shard_map/prep/pallas_call | solution.py:491
  41.3 1.2 %collective-permute-done.6.below_ref = f32[19,72,128]{2,1,0:T(8,128)S(1)} collective-permute-done((f32[19,72,128]{2,1,0:T(8,128)}, f32[19,72,128]{2,1,0:T(8,128)S(1)}, u32[]{:S(2)}, u32[]{:S(2)}) %collective-permute-start.6) | collective-permute-done | bytes 700448 | tf_op jit(solution)/shard_map/ppermute | solution.py:549
  42.5 0.9 copy-done
  43.4 0.2 copy-done.1
  43.6 3.8 %last.1 = (f32[19,2,64,128]{3,2,1,0:T(8,128)}, f32[128,128]{1,0:T(8,128)}) custom-call(f32[19,2,88,128]{3,2,1,0:T(8,128)} %get-tuple-element.38.post_ref, f32[19,72,128]{2,1,0:T(8,128)} %copy-done, f32[19,72,128]{2,1,0:T(8,128)} %copy-done.1, f32[4,72,128]{2,1,0:T(8,128)} %get-tuple-element.41.relax_ref, s32[8,128]{1,0:T(8,128)} %get-tuple-element.42.inv_ref), custom_call_target="tpu_custom_call" | custom-call | tf_op jit(solution)/shard_map/last/pallas_call | solution.py:551
  47.4 21.9 %all_to_all.22 = f32[128,1,128]{2,1,0:T(1,128)} all-to-all(f32[128,1,128]{2,1,0:T(1,128)} %bitcast.24), channel_id=1, replica_groups=mesh['slab'=32,'md'=4] {'slab','md'}, dimensions={0} | all-to-all | bytes 131072 | tf_op jit(solution)/shard_map/all_to_all | solution.py:480
  69.3 11.1 %md.1 = (f32[3,1024]{1,0:T(4,128)}, f32[3,1024]{1,0:T(4,128)}, f32[128,128]{1,0:T(8,128)}) custom-call(f32[128,128]{1,0:T(8,128)} %bitcast.22, f32[3,8,128]{2,1,0:T(8,128)} %get-tuple-element.45.p8_ref, f32[3,8,128]{2,1,0:T(8,128)} %get-tuple-element.46.v8_ref, f32[3,8,128]{2,1,0:T(8,128)} %get-tuple-element.47.force_ref, s32[64,8,128]{2,1,0:T(8,128)} %bitcast.19, ...), custom_call_target="tpu_custom_call" | custom-call | tf_op jit(solution)/shard_map/md/pallas_call | solution.py:558
  80.3 15.0 %all_to_all.23 = f32[128,1,128]{2,1,0:T(1,128)} all-to-all(f32[128,1,128]{2,1,0:T(1,128)} %bitcast.23), channel_id=1, replica_groups=mesh['slab'=32,'md'=4] {'slab','md'}, dimensions={0} | all-to-all | bytes 131072 | tf_op jit(solution)/shard_map/all_to_all | solution.py:480
  95.3 1.7 %cells.1 = f32[4,2,64]{2,1,0:T(2,128)} custom-call(f32[128,128]{1,0:T(8,128)} %bitcast.21, s32[2,128]{1,0:T(2,128)} %bitcast.28, s32[8,128]{1,0:T(8,128)} %get-tuple-element.53.rank_ref), custom_call_target="tpu_custom_call" | custom-call | tf_op jit(solution)/shard_map/cells/pallas_call | solution.py:562
  (16 shorter events, 0.0 us)
Async XLA Ops:
  4.0 21.8 %collective-permute-start.2 = (f32[20,64,128]{2,1,0:T(8,128)}, f32[20,64,128]{2,1,0:T(8,128)S(1)}, u32[]{:S(2)}, u32[]{:S(2)}) collective-permute-start(f32[20,64,128]{2,1,0:T(8,128)} %get-tuple-element.33), channel_id=1, source_target_pairs={{0,124},{4,8},{8,4},{12,16},{16,12},{20,24},{24,20},{28,32},{32,28... | collective-permute-start | bytes 1966088 | tf_op jit(solution)/shard_map/ppermute | solution.py:515
  7.0 18.8 %collective-permute-start.3 = (f32[20,64,128]{2,1,0:T(8,128)}, f32[20,64,128]{2,1,0:T(8,128)S(1)}, u32[]{:S(2)}, u32[]{:S(2)}) collective-permute-start(f32[20,64,128]{2,1,0:T(8,128)} %get-tuple-element.34), channel_id=1, source_target_pairs={{0,4},{4,0},{8,12},{12,8},{16,20},{20,16},{24,28},{28,24},{32,36},... | collective-permute-start | bytes 1966088 | tf_op jit(solution)/shard_map/ppermute | solution.py:516
  11.4 7.2 %collective-permute-start = (f32[20,2,8,128]{3,2,1,0:T(8,128)}, f32[20,2,8,128]{3,2,1,0:T(8,128)S(1)}, u32[]{:S(2)}, u32[]{:S(2)}) collective-permute-start(f32[20,2,8,128]{3,2,1,0:T(8,128)} %get-tuple-element.30), channel_id=1, source_target_pairs={{0,1},{1,2},{2,3},{3,0},{4,5},{5,6},{6,7},{7,4},{8,9},{9,10},{10,1... | collective-permute-start | bytes 491528 | tf_op jit(solution)/shard_map/ppermute | solution.py:517
  12.6 6.0 %collective-permute-start.1 = (f32[20,2,8,128]{3,2,1,0:T(8,128)}, f32[20,2,8,128]{3,2,1,0:T(8,128)S(1)}, u32[]{:S(2)}, u32[]{:S(2)}) collective-permute-start(f32[20,2,8,128]{3,2,1,0:T(8,128)} %get-tuple-element.31), channel_id=1, source_target_pairs={{1,0},{2,1},{3,2},{0,3},{5,4},{6,5},{7,6},{4,7},{9,8},{10,9},{11,1... | collective-permute-start | bytes 491528 | tf_op jit(solution)/shard_map/ppermute | solution.py:518
  18.6 0.7 copy-start.5
  19.2 0.7 copy-start.6
  21.7 4.1 %collective-permute-start.4 = (f32[20,8,128]{2,1,0:T(8,128)}, f32[20,8,128]{2,1,0:T(8,128)S(1)}, u32[]{:S(2)}, u32[]{:S(2)}) collective-permute-start(f32[20,8,128]{2,1,0:T(8,128)} %get-tuple-element.35), channel_id=1, source_target_pairs={{0,124},{4,8},{8,4},{12,16},{16,12},{20,24},{24,20},{28,32},{32,28... | collective-permute-start | bytes 245768 | tf_op jit(solution)/shard_map/ppermute | solution.py:529
  21.7 4.1 %collective-permute-start.5 = (f32[20,8,128]{2,1,0:T(8,128)}, f32[20,8,128]{2,1,0:T(8,128)S(1)}, u32[]{:S(2)}, u32[]{:S(2)}) collective-permute-start(f32[20,8,128]{2,1,0:T(8,128)} %get-tuple-element.36), channel_id=1, source_target_pairs={{0,4},{4,0},{8,12},{12,8},{16,20},{20,16},{24,28},{28,24},{32,36},... | collective-permute-start | bytes 245768 | tf_op jit(solution)/shard_map/ppermute | solution.py:530
  25.8 0.6 copy-start.7
  25.8 0.7 copy-start.8
  25.8 0.9 copy-start.2
  25.8 1.1 %copy-start.3 = (f32[20,64,128]{2,1,0:T(8,128)}, f32[20,64,128]{2,1,0:T(8,128)S(1)}, u32[]{:S(2)}) copy-start(f32[20,64,128]{2,1,0:T(8,128)S(1)} %collective-permute-done.3.above_ref) | copy-start | bytes 1966084
  26.9 8.9 %copy-start.4 = (s32[1024,64]{0,1:T(8,128)S(1)}, s32[1024,64]{0,1:T(8,128)}, u32[]{:S(2)}) copy-start(s32[1024,64]{0,1:T(8,128)} %param.12) | copy-start | bytes 786436
  26.9 9.6 %copy-start.9 = (s32[2,64,2]{1,2,0:T(2,128)S(1)}, s32[2,64,2]{1,2,0:T(2,128)}, u32[]{:S(2)}) copy-start(s32[2,64,2]{1,2,0:T(2,128)} %param.9) | copy-start | bytes 3076
  31.5 11.0 %collective-permute-start.6 = (f32[19,72,128]{2,1,0:T(8,128)}, f32[19,72,128]{2,1,0:T(8,128)S(1)}, u32[]{:S(2)}, u32[]{:S(2)}) collective-permute-start(f32[19,72,128]{2,1,0:T(8,128)} %get-tuple-element.39), channel_id=1, source_target_pairs={{0,124},{4,8},{8,4},{12,16},{16,12},{20,24},{24,20},{28,32},{32,28... | collective-permute-start | bytes 2101256 | tf_op jit(solution)/shard_map/ppermute | solution.py:549
  31.6 11.0 %collective-permute-start.7 = (f32[19,72,128]{2,1,0:T(8,128)}, f32[19,72,128]{2,1,0:T(8,128)S(1)}, u32[]{:S(2)}, u32[]{:S(2)}) collective-permute-start(f32[19,72,128]{2,1,0:T(8,128)} %get-tuple-element.40), channel_id=1, source_target_pairs={{0,4},{4,0},{8,12},{12,8},{16,20},{20,16},{24,28},{28,24},{32,36},... | collective-permute-start | bytes 2101256 | tf_op jit(solution)/shard_map/ppermute | solution.py:550
  42.5 0.9 copy-start
  42.5 1.1 %copy-start.1 = (f32[19,72,128]{2,1,0:T(8,128)}, f32[19,72,128]{2,1,0:T(8,128)S(1)}, u32[]{:S(2)}) copy-start(f32[19,72,128]{2,1,0:T(8,128)S(1)} %collective-permute-done.7.above_ref) | copy-start | bytes 2101252

commit v2 on v1

--- a/solution.py
+++ b/solution.py
@@ -472,6 +472,9 @@
     out_ref[:, 1, :] = cell[:, 64:]
 
 
+room = pltpu.CompilerParams(vmem_limit_bytes=16 << 20)
+
+
 def shape(*dims, dtype=f32):
     return jax.ShapeDtypeStruct(dims, dtype)
 
@@ -499,7 +502,7 @@
             shape(3, 8, 128),
             shape(3, 8, 128),
         ),
-        name="prep",
+        name="prep", compiler_params=room,
     )(own, slots, positions, velocities, nbr)
     post, up, down, low, high = pl.pallas_call(
         first_kernel,
@@ -510,7 +513,7 @@
             shape(20, 2, 8, 128),
             shape(20, 2, 8, 128),
         ),
-        name="first",
+        name="first", compiler_params=room,
     )(populations, relax)
     below = lax.ppermute(down, "slab", far_pairs)
     above = lax.ppermute(up, "slab", near_pairs)
@@ -524,7 +527,7 @@
             shape(20, 8, 128),
             shape(2, 8, 128),
         ),
-        name="edge",
+        name="edge", compiler_params=room,
     )(from_low, from_high)
     below_edge = lax.ppermute(down_edge, "slab", far_pairs)
     above_edge = lax.ppermute(up_edge, "slab", near_pairs)
@@ -544,7 +547,7 @@
             shape(4, ROWS, 128),
         ),
         scratch_shapes=scratch + [pltpu.VMEM((2 * len(moving), 24, 128), f32)],
-        name="middle",
+        name="middle", compiler_params=room,
     )(post, post_edge, below, above, below_edge, above_edge, relax, relax_edge)
     below = lax.ppermute(down, "slab", far_pairs)
     above = lax.ppermute(up, "slab", near_pairs)
@@ -552,14 +555,14 @@
         last_kernel,
         out_shape=(shape(19, 2, 64, 128), shape(128, 128)),
         scratch_shapes=scratch + [pltpu.VMEM((4, 128, 128), f32)],
-        name="last",
+        name="last", compiler_params=room,
     )(post, below, above, relax_all, inv)
     arrived = exchange(outgoing)
     pos_out, vel_out, moms = pl.pallas_call(
-        md_kernel, out_shape=(shape(3, 1024), shape(3, 1024), shape(128, 128)), name="md"
+        md_kernel, out_shape=(shape(3, 1024), shape(3, 1024), shape(128, 128)), name="md", compiler_params=room
     )(arrived, p8, v8, force, nbr, slots, hot, icnt)
     returned = exchange(moms)
-    cell = pl.pallas_call(cell_kernel, out_shape=shape(4, 2, 64), name="cells")(
+    cell = pl.pallas_call(cell_kernel, out_shape=shape(4, 2, 64), name="cells", compiler_params=room)(
         returned, own, rank
     )
     return (f, pos_out, vel_out, cell)

time: 97.3 us -> 82.6 us (0.85)
  Pallas kernels: 30.4 us -> 18.1 us
  blocking collectives: 36.8 us -> 34.5 us
  local copies, waits for them, and re-layouts: 4.94 us -> 3.01 us
  waiting for transfers between devices: 8.91 us -> 10.7 us
    pallas_call x1, Pallas kernels: 3.33 us -> 0.55 us  [on_device(): pl.pallas_call(first_kernel, out_shape=(shape(19, 2, 64, 128), shape(20,...]
    pallas_call x1, Pallas kernels: 4.62 us -> 2.28 us  [on_device(): pl.pallas_call(middle_kernel, out_shape=(shape(19, 2, PAD, 128), shape(19...]
    all_to_all x2, blocking collectives: 36.8 us -> 34.5 us  [exchange(): lax.all_to_all(rows, ('slab', 'md'), split_axis=0, concat_axis=0, tiled=T...]
    ppermute x2, waiting for transfers between devices: 1.2 us -> 3.46 us  [on_device(): below = lax.ppermute(down, 'slab', far_pairs)]
    pallas_call x1, Pallas kernels: 3.78 us -> 2.09 us  [on_device(): pl.pallas_call(last_kernel, out_shape=(shape(19, 2, 64, 128), shape(128,...]
    pallas_call x1, Pallas kernels: 1.82 us -> 0.13 us  [on_device(): pl.pallas_call(edge_kernel, out_shape=(shape(19, 2, 8, 128), shape(20, 8,...]
    pallas_call x1, Pallas kernels: 4.12 us -> 2.46 us  [on_device(): pl.pallas_call(prep_kernel, out_shape=(shape(8, 128, dtype=i32), shape(8,...]
    unnamed x22 -> x18, local copies, waits for them, and re-layouts: 4.27 us -> 2.92 us
  transfers between devices with their start and end apart: 8 -> 8, of which waited for: 3 -> 3; matrix products, arithmetic and copies ran while one was open for 1% -> 0% of each run, Pallas kernels for 6% -> 3%
where the time goes in v2:
time: 82.6 us; the launch traced here: 82.4 us
  blocking collectives  34.5 us (42%)
  Pallas kernels  18.1 us (22%)
  starting transfers between devices  15.4 us (19%)
  waiting for transfers between devices  10.7 us (13%)
  local copies, waits for them, and re-layouts  3.01 us (4%)
    all_to_all x2, blocking collectives, exchange(): lax.all_to_all(rows, ('slab', 'md'), split_axis=0, concat_axis=0, tiled=T...  34.5 us
    pallas_call x1, Pallas kernels, on_device(): pl.pallas_call(md_kernel, out_shape=(shape(3, 1024), shape(3, 1024), shap...  9.73 us
    ppermute x2, starting transfers between devices, on_device(): above = lax.ppermute(up, 'slab', near_pairs)  8.59 us
    ppermute x1, waiting for transfers between devices, on_device(): from_low = lax.ppermute(high, 'md', [(i, (i + 1) % 4) for i in range(4)])  4.29 us
    ppermute x2, waiting for transfers between devices, on_device(): below = lax.ppermute(down, 'slab', far_pairs)  3.46 us
    ppermute x2, starting transfers between devices, on_device(): below = lax.ppermute(down, 'slab', far_pairs)  3.09 us
    unnamed x18, local copies, waits for them, and re-layouts  2.92 us
    ppermute x1, waiting for transfers between devices, on_device(): below_edge = lax.ppermute(down_edge, 'slab', far_pairs)  2.91 us
  transfers between devices with their start and end apart: 8, of which 3 were waited for; matrix products, arithmetic and copies ran while one was open for 0% of the time, Pallas kernels for 3%

profile of v2, /device:TPU:1, one launch (start us, length us, event | category | flops | bytes accessed | tf_op | source)
XLA Modules:
  0.0 82.4 jit_solution(7194130571749507491)
XLA Ops:
  0.6 1.3 %copy-done = f32[19,2,64,128]{3,2,1,0:T(8,128)S(1)} copy-done((f32[19,2,64,128]{3,2,1,0:T(8,128)S(1)}, f32[19,2,64,128]{3,2,1,0:T(8,128)}, u32[]{:S(2)}) %copy-start) | copy-done | bytes 1245208
  1.9 0.8 %copy-done.1 = f32[2,64,128]{2,1,0:T(8,128)S(1)} copy-done((f32[2,64,128]{2,1,0:T(8,128)S(1)}, f32[2,64,128]{2,1,0:T(8,128)}, u32[]{:S(2)}) %copy-start.1) | copy-done | bytes 65560
  2.8 0.5 first.1
  3.3 3.1 %collective-permute-start.2 = (f32[20,64,128]{2,1,0:T(8,128)S(1)}, f32[20,64,128]{2,1,0:T(8,128)S(1)}, u32[]{:S(2)}, u32[]{:S(2)}) collective-permute-start(f32[20,64,128]{2,1,0:T(8,128)S(1)} %get-tuple-element.33), channel_id=1, source_target_pairs={{0,124},{4,8},{8,4},{12,16},{16,12},{20,24},{24,20},{28,32},{32,28... | collective-permute-start | bytes 1966088 | tf_op jit(solution)/shard_map/ppermute | solution.py:518
  6.4 4.4 %collective-permute-start.3 = (f32[20,64,128]{2,1,0:T(8,128)S(1)}, f32[20,64,128]{2,1,0:T(8,128)S(1)}, u32[]{:S(2)}, u32[]{:S(2)}) collective-permute-start(f32[20,64,128]{2,1,0:T(8,128)S(1)} %get-tuple-element.34), channel_id=1, source_target_pairs={{0,4},{4,0},{8,12},{12,8},{16,20},{20,16},{24,28},{28,24},{32,36},... | collective-permute-start | bytes 1966088 | tf_op jit(solution)/shard_map/ppermute | solution.py:519
  10.8 1.2 %collective-permute-start = (f32[20,2,8,128]{3,2,1,0:T(8,128)S(1)}, f32[20,2,8,128]{3,2,1,0:T(8,128)S(1)}, u32[]{:S(2)}, u32[]{:S(2)}) collective-permute-start(f32[20,2,8,128]{3,2,1,0:T(8,128)S(1)} %get-tuple-element.30), channel_id=1, source_target_pairs={{0,1},{1,2},{2,3},{3,0},{4,5},{5,6},{6,7},{7,4},{8,9},{9,10},{10,1... | collective-permute-start | bytes 491528 | tf_op jit(solution)/shard_map/ppermute | solution.py:520
  12.0 1.5 %collective-permute-start.1 = (f32[20,2,8,128]{3,2,1,0:T(8,128)S(1)}, f32[20,2,8,128]{3,2,1,0:T(8,128)S(1)}, u32[]{:S(2)}, u32[]{:S(2)}) collective-permute-start(f32[20,2,8,128]{3,2,1,0:T(8,128)S(1)} %get-tuple-element.31), channel_id=1, source_target_pairs={{1,0},{2,1},{3,2},{0,3},{5,4},{6,5},{7,6},{4,7},{9,8},{10,9},{11,1... | collective-permute-start | bytes 491528 | tf_op jit(solution)/shard_map/ppermute | solution.py:521
  13.5 4.3 %collective-permute-done.low_ref = f32[20,2,8,128]{3,2,1,0:T(8,128)S(1)} collective-permute-done((f32[20,2,8,128]{3,2,1,0:T(8,128)S(1)}, f32[20,2,8,128]{3,2,1,0:T(8,128)S(1)}, u32[]{:S(2)}, u32[]{:S(2)}) %collective-permute-start) | collective-permute-done | bytes 163872 | tf_op jit(solution)/shard_map/ppermute | solution.py:520
  17.8 0.1 edge.1
  17.9 0.1 collective-permute-start.4
  18.0 0.9 %collective-permute-start.5 = (f32[20,8,128]{2,1,0:T(8,128)S(1)}, f32[20,8,128]{2,1,0:T(8,128)S(1)}, u32[]{:S(2)}, u32[]{:S(2)}) collective-permute-start(f32[20,8,128]{2,1,0:T(8,128)S(1)} %get-tuple-element.36), channel_id=1, source_target_pairs={{0,4},{4,0},{8,12},{12,8},{16,20},{20,16},{24,28},{28,24},{32,36},... | collective-permute-start | bytes 245768 | tf_op jit(solution)/shard_map/ppermute | solution.py:533
  18.9 2.9 %collective-permute-done.4.below_edge_ref = f32[20,8,128]{2,1,0:T(8,128)S(1)} collective-permute-done((f32[20,8,128]{2,1,0:T(8,128)S(1)}, f32[20,8,128]{2,1,0:T(8,128)S(1)}, u32[]{:S(2)}, u32[]{:S(2)}) %collective-permute-start.4) | collective-permute-done | bytes 81952 | tf_op jit(solution)/shard_map/ppermute | solution.py:532
  21.8 0.0 collective-permute-done.5.above_edge_ref
  21.9 0.0 collective-permute-done.2.below_ref
  21.9 0.0 collective-permute-done.3.above_ref
  21.9 0.0 copy-start.6
  21.9 0.0 copy-start.7
  21.9 0.0 copy-start.3
  21.9 0.0 copy-start.4
  21.9 2.3 %middle.1 = (f32[19,2,88,128]{3,2,1,0:T(8,128)S(1)}, f32[19,72,128]{2,1,0:T(8,128)}, f32[19,72,128]{2,1,0:T(8,128)}, f32[4,72,128]{2,1,0:T(8,128)S(1)}) custom-call(f32[19,2,64,128]{3,2,1,0:T(8,128)S(1)} %get-tuple-element.29.post_ref, f32[19,2,8,128]{3,2,1,0:T(8,128)S(1)} %get-tuple-element.32.post_edge_ref, ...), custom_call_target="tpu_custom_call" | custom-call | tf_op jit(solution)/shard_map/middle/pallas_call | solution.py:541
  24.2 0.0 collective-permute-start.6
  24.2 4.2 %collective-permute-start.7 = (f32[19,72,128]{2,1,0:T(8,128)}, f32[19,72,128]{2,1,0:T(8,128)S(1)}, u32[]{:S(2)}, u32[]{:S(2)}) collective-permute-start(f32[19,72,128]{2,1,0:T(8,128)} %get-tuple-element.40), channel_id=1, source_target_pairs={{0,4},{4,0},{8,12},{12,8},{16,20},{20,16},{24,28},{28,24},{32,36},... | collective-permute-start | bytes 2101256 | tf_op jit(solution)/shard_map/ppermute | solution.py:553
  28.5 0.1 reshape.21
  28.6 0.7 copy-done.5
  29.3 2.5 %prep.1 = (s32[8,128]{1,0:T(8,128)S(1)}, s32[8,128]{1,0:T(8,128)S(1)}, bf16[128,1024]{1,0:T(8,128)(2,1)S(1)}, f32[128,16]{1,0:T(8,128)S(1)}, f32[3,8,128]{2,1,0:...) custom-call(s32[2,128]{1,0:T(2,128)S(1)} %bitcast.26, s32[8,128]{1,0:T(8,128)S(1)} %bitcast.24, ...), custom_call_target="tpu_custom_call" | custom-call | tf_op jit(solution)/shard_map/prep/pallas_call | solution.py:494
  31.7 3.5 %collective-permute-done.6.below_ref = f32[19,72,128]{2,1,0:T(8,128)S(1)} collective-permute-done((f32[19,72,128]{2,1,0:T(8,128)}, f32[19,72,128]{2,1,0:T(8,128)S(1)}, u32[]{:S(2)}, u32[]{:S(2)}) %collective-permute-start.6) | collective-permute-done | bytes 700448 | tf_op jit(solution)/shard_map/ppermute | solution.py:552
  35.2 0.0 collective-permute-done.7.above_ref
  35.2 2.1 %last.1 = (f32[19,2,64,128]{3,2,1,0:T(8,128)}, f32[128,128]{1,0:T(8,128)S(1)}) custom-call(f32[19,2,88,128]{3,2,1,0:T(8,128)S(1)} %get-tuple-element.38.post_ref, f32[19,72,128]{2,1,0:T(8,128)S(1)} %collective-permute-done.6.below_ref, f32[19,72,128]{2,1,0:T(8,128)S(1)} %collective-permute-done.7.above_ref, f32[4,72,128]{2,1,0:T(8,128)S(1)} %get-tuple-element.41.relax_ref, ...), custom_call_target="tpu_custom_call" | custom-call | tf_op jit(solution)/shard_map/last/pallas_call | solution.py:554
  37.3 20.7 %all_to_all.22 = f32[128,1,128]{2,1,0:T(1,128)S(1)} all-to-all(f32[128,1,128]{2,1,0:T(1,128)S(1)} %bitcast.23), channel_id=1, replica_groups=mesh['slab'=32,'md'=4] {'slab','md'}, dimensions={0} | all-to-all | bytes 131072 | tf_op jit(solution)/shard_map/all_to_all | solution.py:483
  58.0 9.7 %md.1 = (f32[3,1024]{1,0:T(4,128)}, f32[3,1024]{1,0:T(4,128)}, f32[128,128]{1,0:T(8,128)S(1)}) custom-call(f32[128,128]{1,0:T(8,128)S(1)} %bitcast.21, f32[3,8,128]{2,1,0:T(8,128)S(1)} %get-tuple-element.45.p8_ref, f32[3,8,128]{2,1,0:T(8,128)S(1)} %get-tuple-element.46.v8_ref, f32[3,8,128]{2,1,0:T(8,128)S(1)} %get-tuple-element.47.force_ref, ...), custom_call_target="tpu_custom_call" | custom-call | tf_op jit(solution)/shard_map/md/pallas_call | solution.py:561
  67.8 13.8 %all_to_all.23 = f32[128,1,128]{2,1,0:T(1,128)S(1)} all-to-all(f32[128,1,128]{2,1,0:T(1,128)S(1)} %bitcast.22), channel_id=1, replica_groups=mesh['slab'=32,'md'=4] {'slab','md'}, dimensions={0} | all-to-all | bytes 131072 | tf_op jit(solution)/shard_map/all_to_all | solution.py:483
  81.5 0.8 cells.1
  (12 shorter events, 0.1 us)
Async XLA Ops:
  0.6 1.3 %copy-start = (f32[19,2,64,128]{3,2,1,0:T(8,128)S(1)}, f32[19,2,64,128]{3,2,1,0:T(8,128)}, u32[]{:S(2)}) copy-start(f32[19,2,64,128]{3,2,1,0:T(8,128)} %f_ref.1) | copy-start | bytes 3735556
  1.9 0.8 %copy-start.1 = (f32[2,64,128]{2,1,0:T(8,128)S(1)}, f32[2,64,128]{2,1,0:T(8,128)}, u32[]{:S(2)}) copy-start(f32[2,64,128]{2,1,0:T(8,128)} %relax_ref.3) | copy-start | bytes 196612
  2.8 19.1 %copy-start.2 = (f32[2,64,128]{2,1,0:T(8,128)S(1)}, f32[2,64,128]{2,1,0:T(8,128)}, u32[]{:S(2)}) copy-start(f32[2,64,128]{2,1,0:T(8,128)} %relax_ref.3) | copy-start | bytes 196612
  3.3 18.5 %collective-permute-start.2 = (f32[20,64,128]{2,1,0:T(8,128)S(1)}, f32[20,64,128]{2,1,0:T(8,128)S(1)}, u32[]{:S(2)}, u32[]{:S(2)}) collective-permute-start(f32[20,64,128]{2,1,0:T(8,128)S(1)} %get-tuple-element.33), channel_id=1, source_target_pairs={{0,124},{4,8},{8,4},{12,16},{16,12},{20,24},{24,20},{28,32},{32,28... | collective-permute-start | bytes 1966088 | tf_op jit(solution)/shard_map/ppermute | solution.py:518
  6.4 15.5 %collective-permute-start.3 = (f32[20,64,128]{2,1,0:T(8,128)S(1)}, f32[20,64,128]{2,1,0:T(8,128)S(1)}, u32[]{:S(2)}, u32[]{:S(2)}) collective-permute-start(f32[20,64,128]{2,1,0:T(8,128)S(1)} %get-tuple-element.34), channel_id=1, source_target_pairs={{0,4},{4,0},{8,12},{12,8},{16,20},{20,16},{24,28},{28,24},{32,36},... | collective-permute-start | bytes 1966088 | tf_op jit(solution)/shard_map/ppermute | solution.py:519
  10.8 7.0 %collective-permute-start = (f32[20,2,8,128]{3,2,1,0:T(8,128)S(1)}, f32[20,2,8,128]{3,2,1,0:T(8,128)S(1)}, u32[]{:S(2)}, u32[]{:S(2)}) collective-permute-start(f32[20,2,8,128]{3,2,1,0:T(8,128)S(1)} %get-tuple-element.30), channel_id=1, source_target_pairs={{0,1},{1,2},{2,3},{3,0},{4,5},{5,6},{6,7},{7,4},{8,9},{9,10},{10,1... | collective-permute-start | bytes 491528 | tf_op jit(solution)/shard_map/ppermute | solution.py:520
  12.0 5.8 %collective-permute-start.1 = (f32[20,2,8,128]{3,2,1,0:T(8,128)S(1)}, f32[20,2,8,128]{3,2,1,0:T(8,128)S(1)}, u32[]{:S(2)}, u32[]{:S(2)}) collective-permute-start(f32[20,2,8,128]{3,2,1,0:T(8,128)S(1)} %get-tuple-element.31), channel_id=1, source_target_pairs={{1,0},{2,1},{3,2},{0,3},{5,4},{6,5},{7,6},{4,7},{9,8},{10,9},{11,1... | collective-permute-start | bytes 491528 | tf_op jit(solution)/shard_map/ppermute | solution.py:521
  17.9 3.9 %collective-permute-start.4 = (f32[20,8,128]{2,1,0:T(8,128)S(1)}, f32[20,8,128]{2,1,0:T(8,128)S(1)}, u32[]{:S(2)}, u32[]{:S(2)}) collective-permute-start(f32[20,8,128]{2,1,0:T(8,128)S(1)} %get-tuple-element.35), channel_id=1, source_target_pairs={{0,124},{4,8},{8,4},{12,16},{16,12},{20,24},{24,20},{28,32},{32,28... | collective-permute-start | bytes 245768 | tf_op jit(solution)/shard_map/ppermute | solution.py:532
  18.0 3.9 %collective-permute-start.5 = (f32[20,8,128]{2,1,0:T(8,128)S(1)}, f32[20,8,128]{2,1,0:T(8,128)S(1)}, u32[]{:S(2)}, u32[]{:S(2)}) collective-permute-start(f32[20,8,128]{2,1,0:T(8,128)S(1)} %get-tuple-element.36), channel_id=1, source_target_pairs={{0,4},{4,0},{8,12},{12,8},{16,20},{20,16},{24,28},{28,24},{32,36},... | collective-permute-start | bytes 245768 | tf_op jit(solution)/shard_map/ppermute | solution.py:533
  21.9 6.5 %copy-start.6 = (s32[1024,64]{0,1:T(8,128)S(1)}, s32[1024,64]{0,1:T(8,128)}, u32[]{:S(2)}) copy-start(s32[1024,64]{0,1:T(8,128)} %param.12) | copy-start | bytes 786436
  21.9 6.6 %copy-start.7 = (s32[2,64,2]{1,2,0:T(2,128)S(1)}, s32[2,64,2]{1,2,0:T(2,128)}, u32[]{:S(2)}) copy-start(s32[2,64,2]{1,2,0:T(2,128)} %param.9) | copy-start | bytes 3076
  21.9 6.7 %copy-start.3 = (s32[1024]{0:T(1024)S(1)}, s32[1024]{0:T(1024)}, u32[]{:S(2)}) copy-start(s32[1024]{0:T(1024)} %param.13) | copy-start | bytes 12292
  21.9 6.6 %copy-start.4 = (f32[3,1024]{1,0:T(4,128)S(1)}, f32[3,1024]{1,0:T(4,128)}, u32[]{:S(2)}) copy-start(f32[3,1024]{1,0:T(4,128)} %pos_ref.1) | copy-start | bytes 36868
  24.2 11.0 %collective-permute-start.6 = (f32[19,72,128]{2,1,0:T(8,128)}, f32[19,72,128]{2,1,0:T(8,128)S(1)}, u32[]{:S(2)}, u32[]{:S(2)}) collective-permute-start(f32[19,72,128]{2,1,0:T(8,128)} %get-tuple-element.39), channel_id=1, source_target_pairs={{0,124},{4,8},{8,4},{12,16},{16,12},{20,24},{24,20},{28,32},{32,28... | collective-permute-start | bytes 2101256 | tf_op jit(solution)/shard_map/ppermute | solution.py:552
  24.2 11.0 %collective-permute-start.7 = (f32[19,72,128]{2,1,0:T(8,128)}, f32[19,72,128]{2,1,0:T(8,128)S(1)}, u32[]{:S(2)}, u32[]{:S(2)}) collective-permute-start(f32[19,72,128]{2,1,0:T(8,128)} %get-tuple-element.40), channel_id=1, source_target_pairs={{0,4},{4,0},{8,12},{12,8},{16,20},{20,16},{24,28},{28,24},{32,36},... | collective-permute-start | bytes 2101256 | tf_op jit(solution)/shard_map/ppermute | solution.py:553
  28.6 0.7 copy-start.5

commit v3 on v2

--- a/solution.py
+++ b/solution.py
@@ -151,18 +151,30 @@
 everything = set(range(19))
 
 
-def first_kernel(f_ref, relax_ref, post_ref, up_ref, down_ref, low_ref, high_ref):
+def load_kernel(f_ref, relax_ref, low_ref, high_ref, f_out_ref, relax_out_ref, sems):
+    moves = []
+    for edge_ref, row in ((low_ref, 0), (high_ref, 56)):
+        rows = pl.ds(row, 8)
+        moves.append((f_ref.at[:, :, rows, :], edge_ref.at[0:19]))
+        moves.append((relax_ref.at[:, rows, :], edge_ref.at[RELAX]))
+    moves.append((relax_ref, relax_out_ref))
+    for part in range(4):
+        some = slice(5 * part, min(5 * part + 5, 19))
+        moves.append((f_ref.at[some], f_out_ref.at[some]))
+    copies = [pltpu.make_async_copy(*move, sems.at[n]) for n, move in enumerate(moves)]
+    for copy in copies:
+        copy.start()
+    for copy in copies:
+        copy.wait()
+
+
+def first_kernel(f_ref, relax_ref, post_ref, up_ref, down_ref):
     odd = parity()
     for plane in range(2):
         actual_plane = jnp.where(odd == 1, 1 - plane, plane)
         for b in range(8):
             f = {i: f_ref[actual(i, odd), actual_plane, rows_of(b), :] for i in range(19)}
             relax = relax_ref[actual_plane, rows_of(b), :]
-            if b in (0, 7):
-                edge_ref = low_ref if b == 0 else high_ref
-                for i in range(19):
-                    edge_ref[i, plane] = f[i]
-                edge_ref[RELAX, plane] = relax
             post = collided(f, relax, everything)
             for i in range(19):
                 post_ref[i, plane, rows_of(b), :] = post[i]
@@ -170,9 +182,14 @@
 
 
 def edge_kernel(low_ref, high_ref, post_ref, up_ref, down_ref, relax_ref):
+    odd = parity()
     head = lax.broadcasted_iota(i32, (8, 128), 0) < 4
     for plane in range(2):
-        mixed = [jnp.where(head, high_ref[i, plane], low_ref[i, plane]) for i in range(20)]
+        actual_plane = jnp.where(odd == 1, 1 - plane, plane)
+        mixed = []
+        for i in range(20):
+            j = actual(i, odd) if i < 19 else i
+            mixed.append(jnp.where(head, high_ref[j, actual_plane], low_ref[j, actual_plane]))
         post = collided(dict(enumerate(mixed[:19])), mixed[RELAX], everything)
         relax_ref[plane] = mixed[RELAX]
         for i in range(19):
@@ -350,30 +367,42 @@
     return jnp.broadcast_to(block[index : index + 1, :], (rows, 128))
 
 
-def pair_sum(coords, nbr_ref):
-    tables = [[spread(comp, chunk) for chunk in range(8)] for comp in coords]
-
-    def entry(k, total):
-        index = nbr_ref[k]
-        low = index & 127
-        bits = [(index & mask) != 0 for mask in (128, 256, 512)]
-        gaps = []
-        for comp in range(3):
-            level = [lanes(table, low) for table in tables[comp]]
-            for bit in bits:
-                level = [
-                    jnp.where(bit, level[2 * j + 1], level[2 * j]) for j in range(len(level) // 2)
-                ]
-            gaps.append(level[0] - coords[comp])
-        weight = jnp.exp(-0.5 * (gaps[0] * gaps[0] + gaps[1] * gaps[1] + gaps[2] * gaps[2]))
-        return tuple(t + g * weight for t, g in zip(total, gaps))
-
-    zero = jnp.zeros((8, 128), f32)
-    return lax.fori_loop(0, nbr_ref.shape[0], entry, (zero, zero, zero), unroll=16)
-
-
-def prep_kernel(own_ref, slot_ref, pos_ref, vel_ref, nbr_ref,
-                inv_ref, rank_ref, hot_ref, icnt_ref, force_ref, p8_ref, v8_ref):
+def lookup(tables, index):
+    low = index & 127
+    found = [[lanes(chunk, low) for chunk in table] for table in tables]
+    for mask in (128, 256, 512):
+        bit = (index & mask) != 0
+        found = [
+            [jnp.where(bit, f[2 * j + 1], f[2 * j]) for j in range(len(f) // 2)] for f in found
+        ]
+    return [f[0] for f in found]
+
+
+def chunks(block):
+    return [spread(block, chunk) for chunk in range(8)]
+
+
+def pull(total, near, here):
+    gaps = [n - h for n, h in zip(near, here)]
+    weight = jnp.exp(-0.5 * (gaps[0] * gaps[0] + gaps[1] * gaps[1] + gaps[2] * gaps[2]))
+    return tuple(t + g * weight for t, g in zip(total, gaps))
+
+
+def over_list(entry, start):
+    return lax.fori_loop(0, 64, entry, start, unroll=16)
+
+
+def blank():
+    return tuple(jnp.zeros((8, 128), f32) for _ in range(3))
+
+
+def prep_kernel(own_in_ref, slot_ref, pos_ref, vel_ref, nbr_ref,
+                own_ref, inv_ref, rank_ref, hot_ref, icnt_ref, force_ref, p8_ref, v8_ref,
+                list_ref, near_ref, drift_ref):
+    for k in range(2):
+        for z in range(2):
+            own_ref[k : k + 1, z * 64 : (z + 1) * 64] = own_in_ref[z, k : k + 1, :]
+    own_ref[2:8, :] = jnp.zeros((6, 128), i32)
     row_id = lax.broadcasted_iota(i32, (128, 128), 0)
     lane_id = lax.broadcasted_iota(i32, (128, 128), 1)
     own = [spread(own_ref[...], k, 128) for k in range(2)]
@@ -409,13 +438,39 @@
         for s in range(8):
             p8_ref[c, s : s + 1, :] = pos_ref[c : c + 1, s * 128 : (s + 1) * 128]
             v8_ref[c, s : s + 1, :] = vel_ref[c : c + 1, s * 128 : (s + 1) * 128]
-    total = pair_sum([p8_ref[0], p8_ref[1], p8_ref[2]], nbr_ref)
+    for k in range(8):
+        for part in range(8):
+            list_ref[8 * k : 8 * k + 8, part, :] = nbr_ref[
+                8 * k : 8 * k + 8, part * 128 : (part + 1) * 128
+            ]
+    here = [p8_ref[c] for c in range(3)]
+    tables = [chunks(h) for h in here]
+
+    def positions(k, total):
+        near = lookup(tables, list_ref[k])
+        for c in range(3):
+            near_ref[k, c] = near[c]
+        return pull(total, near, here)
+
+    total = over_list(positions, blank())
     for c in range(3):
         force_ref[c] = total[c]
-
-
-def md_kernel(arr_ref, p8_ref, v8_ref, force_ref, nbr_ref, slot_ref, hot_ref, icnt_ref,
-              pos_ref, vel_ref, mom_ref):
+    speeds = [chunks(v8_ref[c]) for c in range(3)]
+
+    def drifts(k, none):
+        for c, speed in enumerate(lookup(speeds, list_ref[k])):
+            drift_ref[k, c] = time_step * speed
+        return none
+
+    over_list(drifts, 0)
+
+
+def md_kernel(arr_ref, p8_ref, v8_ref, force_ref, list_ref, near_in_ref, drift_in_ref,
+              slot_ref, hot_ref, icnt_ref, f_ref,
+              pos_ref, vel_ref, mom_ref, f_out_ref,
+              near_ref, drift_ref, sem):
+    saved = pltpu.make_async_copy(f_ref, f_out_ref, sem)
+    saved.start()
     table = arr_ref[...].T
     slots = slot_ref[...]
     source = slots >> 2
@@ -429,8 +484,45 @@
     drag = friction * target[3]
     pos = [p8_ref[c] for c in range(3)]
     vel = [v8_ref[c] for c in range(3)]
+    here = list(pos)
+    drift = [time_step * v for v in vel]
     for step in range(MD_STEPS):
-        pair = [force_ref[c] for c in range(3)] if step == 0 else pair_sum(pos, nbr_ref)
+        if step == 0:
+            pair = [force_ref[c] for c in range(3)]
+        else:
+            from_near, from_drift = (
+                (near_in_ref, drift_in_ref) if step == 1 else (near_ref, drift_ref)
+            )
+            miss = [pos[c] - (here[c] + drift[c]) for c in range(3)]
+            largest = jnp.maximum(jnp.maximum(abs(miss[0]), abs(miss[1])), abs(miss[2]))
+            largest = jnp.max(jnp.max(largest, axis=0, keepdims=True), axis=1, keepdims=True)
+            largest = jnp.broadcast_to(jnp.maximum(largest, 1e-30), (8, 128))
+            units = [largest * (1.0 / 1023.0), largest * (1.0 / 511.0)]
+            rates = [1023.0 / largest, 511.0 / largest]
+            pick = (0, 0, 1)
+            whole_units = [
+                jnp.floor(miss[c] * rates[pick[c]] + 0.5).astype(i32) for c in range(3)
+            ]
+            code = (
+                (whole_units[0] << 21) | ((whole_units[1] & 2047) << 10) | (whole_units[2] & 1023)
+            )
+            for c in range(3):
+                drift[c] = drift[c] + whole_units[c].astype(f32) * units[pick[c]]
+                here[c] = here[c] + drift[c]
+            tables = [chunks(code)]
+
+            def entry(k, total):
+                (word,) = lookup(tables, list_ref[k])
+                words = (word >> 21, (word << 11) >> 21, (word << 22) >> 22)
+                near = []
+                for c in range(3):
+                    move = from_drift[k, c] + words[c].astype(f32) * units[pick[c]]
+                    drift_ref[k, c] = move
+                    near.append(from_near[k, c] + move)
+                    near_ref[k, c] = near[c]
+                return pull(total, near, here)
+
+            pair = over_list(entry, blank())
         for c in range(3):
             force = pair_strength * pair[c] + drag * (target[c] - vel[c])
             vel[c] = vel[c] + time_step * force
@@ -458,6 +550,7 @@
         for s in range(8):
             pos_ref[c : c + 1, s * 128 : (s + 1) * 128] = pos[c][s : s + 1, :]
             vel_ref[c : c + 1, s * 128 : (s + 1) * 128] = vel[c][s : s + 1, :]
+    saved.wait()
 
 
 def cell_kernel(back_ref, own_ref, rank_ref, out_ref):
@@ -488,37 +581,50 @@
 
 
 def on_device(populations, relax, owners, positions, velocities, neighbours, atom_slots):
-    own = owners.reshape(128, 2).T
     slots = atom_slots.reshape(8, 128)
-    nbr = neighbours.reshape(8, 128, 64).transpose(2, 0, 1)
-    inv, rank, hot, icnt, force, p8, v8 = pl.pallas_call(
+    eights = shape(3, 8, 128)
+    own, inv, rank, hot, icnt, force, p8, v8, lists, near, drift = pl.pallas_call(
         prep_kernel,
         out_shape=(
             shape(8, 128, dtype=i32),
             shape(8, 128, dtype=i32),
+            shape(8, 128, dtype=i32),
             shape(128, 1024, dtype=bf16),
             shape(128, 16),
-            shape(3, 8, 128),
-            shape(3, 8, 128),
-            shape(3, 8, 128),
+            eights,
+            eights,
+            eights,
+            shape(64, 8, 128, dtype=i32),
+            shape(64, 3, 8, 128),
+            shape(64, 3, 8, 128),
         ),
         name="prep", compiler_params=room,
-    )(own, slots, positions, velocities, nbr)
-    post, up, down, low, high = pl.pallas_call(
+    )(owners.transpose(0, 2, 1), slots, positions, velocities, neighbours.T)
+    hbm = pl.BlockSpec(memory_space=pltpu.HBM)
+    low, high, f_near, relax = pl.pallas_call(
+        load_kernel,
+        in_specs=[hbm, hbm],
+        out_shape=(
+            pltpu.VMEM((20, 2, 8, 128), f32),
+            pltpu.VMEM((20, 2, 8, 128), f32),
+            pltpu.VMEM((19, 2, 64, 128), f32),
+            pltpu.VMEM((2, 64, 128), f32),
+        ),
+        scratch_shapes=[pltpu.SemaphoreType.DMA((9,))],
+        name="load", compiler_params=room,
+    )(
+        pltpu.with_memory_space_constraint(populations, pltpu.HBM),
+        pltpu.with_memory_space_constraint(relax, pltpu.HBM),
+    )
+    from_low = lax.ppermute(high, "md", [(i, (i + 1) % 4) for i in range(4)])
+    from_high = lax.ppermute(low, "md", [((i + 1) % 4, i) for i in range(4)])
+    post, up, down = pl.pallas_call(
         first_kernel,
-        out_shape=(
-            shape(19, 2, 64, 128),
-            shape(20, 64, 128),
-            shape(20, 64, 128),
-            shape(20, 2, 8, 128),
-            shape(20, 2, 8, 128),
-        ),
+        out_shape=(shape(19, 2, 64, 128), shape(20, 64, 128), shape(20, 64, 128)),
         name="first", compiler_params=room,
-    )(populations, relax)
+    )(f_near, relax)
     below = lax.ppermute(down, "slab", far_pairs)
     above = lax.ppermute(up, "slab", near_pairs)
-    from_low = lax.ppermute(high, "md", [(i, (i + 1) % 4) for i in range(4)])
-    from_high = lax.ppermute(low, "md", [((i + 1) % 4, i) for i in range(4)])
     post_edge, up_edge, down_edge, relax_edge = pl.pallas_call(
         edge_kernel,
         out_shape=(
@@ -553,19 +659,29 @@
     above = lax.ppermute(up, "slab", near_pairs)
     f, outgoing = pl.pallas_call(
         last_kernel,
-        out_shape=(shape(19, 2, 64, 128), shape(128, 128)),
+        out_shape=(pltpu.VMEM((19, 2, 64, 128), f32), shape(128, 128)),
         scratch_shapes=scratch + [pltpu.VMEM((4, 128, 128), f32)],
         name="last", compiler_params=room,
     )(post, below, above, relax_all, inv)
     arrived = exchange(outgoing)
-    pos_out, vel_out, moms = pl.pallas_call(
-        md_kernel, out_shape=(shape(3, 1024), shape(3, 1024), shape(128, 128)), name="md", compiler_params=room
-    )(arrived, p8, v8, force, nbr, slots, hot, icnt)
+    vmem = pl.BlockSpec(memory_space=pltpu.VMEM)
+    pos_out, vel_out, moms, f_out = pl.pallas_call(
+        md_kernel,
+        in_specs=[vmem] * 11,
+        out_specs=(vmem, vmem, vmem, hbm),
+        out_shape=(shape(3, 1024), shape(3, 1024), shape(128, 128), shape(19, 2, 64, 128)),
+        scratch_shapes=[
+            pltpu.VMEM((64, 3, 8, 128), f32),
+            pltpu.VMEM((64, 3, 8, 128), f32),
+            pltpu.SemaphoreType.DMA,
+        ],
+        name="md", compiler_params=room,
+    )(arrived, p8, v8, force, lists, near, drift, slots, hot, icnt, f)
     returned = exchange(moms)
     cell = pl.pallas_call(cell_kernel, out_shape=shape(4, 2, 64), name="cells", compiler_params=room)(
         returned, own, rank
     )
-    return (f, pos_out, vel_out, cell)
+    return (f_out, pos_out, vel_out, cell)
 
 
 def solution(mesh):

time: 82.6 us -> 76.1 us (0.921)
  local copies, waits for them, and re-layouts: 3.01 us -> 0.03 us
  Pallas kernels: 18.1 us -> 16.1 us
  waiting for transfers between devices: 10.7 us -> 9 us
    pallas_call x2 -> x3, Pallas kernels: 11.8 us -> 8.73 us  [the longest x1 5.97 us: on_device(): pl.pallas_call(md_kernel, in_specs=[vmem] * 11, out_specs=(vmem, vmem, vm...]
    unnamed x18 -> x10, local copies, waits for them, and re-layouts: 2.92 us -> 0.03 us
    pallas_call x1, Pallas kernels: 2.46 us -> 4.7 us  [on_device(): pl.pallas_call(prep_kernel, out_shape=(shape(8, 128, dtype=i32), shape(8,...]
    ppermute x2, waiting for transfers between devices: 3.46 us -> 1.79 us  [on_device(): below = lax.ppermute(down, 'slab', far_pairs)]
    pallas_call x1, Pallas kernels: 2.28 us -> 1.21 us  [on_device(): pl.pallas_call(middle_kernel, out_shape=(shape(19, 2, PAD, 128), shape(19...]
  transfers between devices with their start and end apart: 8 -> 8, of which waited for: 3 -> 3; matrix products, arithmetic and copies ran while one was open for 0% -> 0% of each run, Pallas kernels for 3% -> 6%
where the time goes in v3:
time: 76.1 us; the launch traced here: 75.9 us
  blocking collectives  34.5 us (45%)
  Pallas kernels  16.1 us (21%)
  starting transfers between devices  15.5 us (20%)
  waiting for transfers between devices  9 us (12%)
    all_to_all x2, blocking collectives, exchange(): lax.all_to_all(rows, ('slab', 'md'), split_axis=0, concat_axis=0, tiled=T...  34.5 us
    ppermute x2, starting transfers between devices, on_device(): above = lax.ppermute(up, 'slab', near_pairs)  8.67 us
    pallas_call x1, Pallas kernels, on_device(): pl.pallas_call(md_kernel, in_specs=[vmem] * 11, out_specs=(vmem, vmem, vm...  5.97 us
    pallas_call x1, Pallas kernels, on_device(): pl.pallas_call(prep_kernel, out_shape=(shape(8, 128, dtype=i32), shape(8,...  4.7 us
    ppermute x1, waiting for transfers between devices, on_device(): from_low = lax.ppermute(high, 'md', [(i, (i + 1) % 4) for i in range(4)])  4.29 us
    ppermute x2, starting transfers between devices, on_device(): below = lax.ppermute(down, 'slab', far_pairs)  3.17 us
    ppermute x1, waiting for transfers between devices, on_device(): below_edge = lax.ppermute(down_edge, 'slab', far_pairs)  2.91 us
    ppermute x2, waiting for transfers between devices, on_device(): below = lax.ppermute(down, 'slab', far_pairs)  1.79 us
  transfers between devices with their start and end apart: 8, of which 3 were waited for; matrix products, arithmetic and copies ran while one was open for 0% of the time, Pallas kernels for 6%

profile of v3, /device:TPU:1, one launch (start us, length us, event | category | flops | bytes accessed | tf_op | source)
XLA Modules:
  0.0 75.9 jit_solution(9397514397727911847)
XLA Ops:
  0.6 1.6 %load.1 = (f32[20,2,8,128]{3,2,1,0:T(8,128)S(1)}, f32[20,2,8,128]{3,2,1,0:T(8,128)S(1)}, f32[19,2,64,128]{3,2,1,0:T(8,128)S(1)}, f32[2,64,128]{2,1,0:T(8,128)S(1)}) custom-call(f32[19,2,64,128]{3,2,1,0:T(8,128)} %f_ref.1, f32[2,64,128]{2,1,0:T(8,128)} %relax_ref.1), custom_call_target="tpu_custom_call" | custom-call | tf_op jit(solution)/shard_map/load/pallas_call | solution.py:604
  2.2 0.5 first.1
  2.7 3.1 %collective-permute-start.2 = (f32[20,64,128]{2,1,0:T(8,128)S(1)}, f32[20,64,128]{2,1,0:T(8,128)S(1)}, u32[]{:S(2)}, u32[]{:S(2)}) collective-permute-start(f32[20,64,128]{2,1,0:T(8,128)S(1)} %get-tuple-element.42), channel_id=1, source_target_pairs={{0,124},{4,8},{8,4},{12,16},{16,12},{20,24},{24,20},{28,32},{32,28... | collective-permute-start | bytes 1966088 | tf_op jit(solution)/shard_map/ppermute | solution.py:626
  5.8 4.4 %collective-permute-start.3 = (f32[20,64,128]{2,1,0:T(8,128)S(1)}, f32[20,64,128]{2,1,0:T(8,128)S(1)}, u32[]{:S(2)}, u32[]{:S(2)}) collective-permute-start(f32[20,64,128]{2,1,0:T(8,128)S(1)} %get-tuple-element.43), channel_id=1, source_target_pairs={{0,4},{4,0},{8,12},{12,8},{16,20},{20,16},{24,28},{28,24},{32,36},... | collective-permute-start | bytes 1966088 | tf_op jit(solution)/shard_map/ppermute | solution.py:627
  10.2 1.2 %collective-permute-start = (f32[20,2,8,128]{3,2,1,0:T(8,128)S(1)}, f32[20,2,8,128]{3,2,1,0:T(8,128)S(1)}, u32[]{:S(2)}, u32[]{:S(2)}) collective-permute-start(f32[20,2,8,128]{3,2,1,0:T(8,128)S(1)} %get-tuple-element.39), channel_id=1, source_target_pairs={{0,1},{1,2},{2,3},{3,0},{4,5},{5,6},{6,7},{7,4},{8,9},{9,10},{10,1... | collective-permute-start | bytes 491528 | tf_op jit(solution)/shard_map/ppermute | solution.py:619
  11.4 1.5 %collective-permute-start.1 = (f32[20,2,8,128]{3,2,1,0:T(8,128)S(1)}, f32[20,2,8,128]{3,2,1,0:T(8,128)S(1)}, u32[]{:S(2)}, u32[]{:S(2)}) collective-permute-start(f32[20,2,8,128]{3,2,1,0:T(8,128)S(1)} %get-tuple-element.40), channel_id=1, source_target_pairs={{1,0},{2,1},{3,2},{0,3},{5,4},{6,5},{7,6},{4,7},{9,8},{10,9},{11,1... | collective-permute-start | bytes 491528 | tf_op jit(solution)/shard_map/ppermute | solution.py:620
  12.8 4.3 %collective-permute-done.low_ref = f32[20,2,8,128]{3,2,1,0:T(8,128)S(1)} collective-permute-done((f32[20,2,8,128]{3,2,1,0:T(8,128)S(1)}, f32[20,2,8,128]{3,2,1,0:T(8,128)S(1)}, u32[]{:S(2)}, u32[]{:S(2)}) %collective-permute-start) | collective-permute-done | bytes 163872 | tf_op jit(solution)/shard_map/ppermute | solution.py:619
  17.1 0.0 collective-permute-done.1.high_ref
  17.1 0.2 edge.1
  17.3 0.1 collective-permute-start.4
  17.4 0.9 %collective-permute-start.5 = (f32[20,8,128]{2,1,0:T(8,128)S(1)}, f32[20,8,128]{2,1,0:T(8,128)S(1)}, u32[]{:S(2)}, u32[]{:S(2)}) collective-permute-start(f32[20,8,128]{2,1,0:T(8,128)S(1)} %get-tuple-element.45), channel_id=1, source_target_pairs={{0,4},{4,0},{8,12},{12,8},{16,20},{20,16},{24,28},{28,24},{32,36},... | collective-permute-start | bytes 245768 | tf_op jit(solution)/shard_map/ppermute | solution.py:639
  18.3 2.9 %collective-permute-done.4.below_edge_ref = f32[20,8,128]{2,1,0:T(8,128)S(1)} collective-permute-done((f32[20,8,128]{2,1,0:T(8,128)S(1)}, f32[20,8,128]{2,1,0:T(8,128)S(1)}, u32[]{:S(2)}, u32[]{:S(2)}) %collective-permute-start.4) | collective-permute-done | bytes 81952 | tf_op jit(solution)/shard_map/ppermute | solution.py:638
  21.2 0.0 collective-permute-done.5.above_edge_ref
  21.2 0.0 collective-permute-done.2.below_ref
  21.2 0.0 collective-permute-done.3.above_ref
  21.2 0.0 copy-start
  21.3 0.0 copy-start.1
  21.3 0.0 copy-start.2
  21.3 0.0 copy-start.3
  21.3 0.0 copy-start.4
  21.3 1.2 %middle.1 = (f32[19,2,88,128]{3,2,1,0:T(8,128)S(1)}, f32[19,72,128]{2,1,0:T(8,128)S(1)}, f32[19,72,128]{2,1,0:T(8,128)S(1)}, f32[4,72,128]{2,1,0:T(8,128)S(1)}) custom-call(f32[19,2,64,128]{3,2,1,0:T(8,128)S(1)} %get-tuple-element.38.post_ref, f32[19,2,8,128]{3,2,1,0:T(8,128)S(1)} %get-tuple-element.41.post_edge_ref, ...), custom_call_target="tpu_custom_call" | custom-call | tf_op jit(solution)/shard_map/middle/pallas_call | solution.py:647
  22.5 0.1 collective-permute-start.6
  22.6 4.3 %collective-permute-start.7 = (f32[19,72,128]{2,1,0:T(8,128)S(1)}, f32[19,72,128]{2,1,0:T(8,128)S(1)}, u32[]{:S(2)}, u32[]{:S(2)}) collective-permute-start(f32[19,72,128]{2,1,0:T(8,128)S(1)} %get-tuple-element.49), channel_id=1, source_target_pairs={{0,4},{4,0},{8,12},{12,8},{16,20},{20,16},{24,28},{28,24},{32,36},... | collective-permute-start | bytes 2101256 | tf_op jit(solution)/shard_map/ppermute | solution.py:659
  26.9 0.0 copy-done.3
  26.9 4.7 %prep.1 = (s32[8,128]{1,0:T(8,128)S(1)}, s32[8,128]{1,0:T(8,128)S(1)}, s32[8,128]{1,0:T(8,128)S(1)}, bf16[128,1024]{1,0:T(8,128)(2,1)S(1)}, f32[128,16]{1,0:T(8,...) custom-call(s32[2,2,64]{2,1,0:T(2,128)S(1)} %bitcast.18, ...), custom_call_target="tpu_custom_call" | custom-call | tf_op jit(solution)/shard_map/prep/pallas_call | solution.py:586
  31.6 1.8 %collective-permute-done.6.below_ref = f32[19,72,128]{2,1,0:T(8,128)S(1)} collective-permute-done((f32[19,72,128]{2,1,0:T(8,128)S(1)}, f32[19,72,128]{2,1,0:T(8,128)S(1)}, u32[]{:S(2)}, u32[]{:S(2)}) %collective-permute-start.6) | collective-permute-done | bytes 700448 | tf_op jit(solution)/shard_map/ppermute | solution.py:658
  33.4 0.0 collective-permute-done.7.above_ref
  33.4 1.2 %last.1 = (f32[19,2,64,128]{3,2,1,0:T(8,128)S(1)}, f32[128,128]{1,0:T(8,128)S(1)}) custom-call(f32[19,2,88,128]{3,2,1,0:T(8,128)S(1)} %get-tuple-element.47.post_ref, f32[19,72,128]{2,1,0:T(8,128)S(1)} %collective-permute-done.6.below_ref, f32[19,72,128]{2,1,0:T(8,128)S(1)} %collective-permute-done.7.above_ref, ...), custom_call_target="tpu_custom_call" | custom-call | tf_op jit(solution)/shard_map/last/pallas_call | solution.py:660
  34.6 20.8 %all_to_all.22 = f32[128,1,128]{2,1,0:T(1,128)S(1)} all-to-all(f32[128,1,128]{2,1,0:T(1,128)S(1)} %bitcast.15), channel_id=1, replica_groups=mesh['slab'=32,'md'=4] {'slab','md'}, dimensions={0} | all-to-all | bytes 131072 | tf_op jit(solution)/shard_map/all_to_all | solution.py:576
  55.4 6.0 %md.1 = (f32[3,1024]{1,0:T(4,128)}, f32[3,1024]{1,0:T(4,128)}, f32[128,128]{1,0:T(8,128)S(1)}, f32[19,2,64,128]{3,2,1,0:T(8,128)}) custom-call(f32[128,128]{1,0:T(8,128)S(1)} %bitcast.11, f32[3,8,128]{2,1,0:T(8,128)S(1)} %get-tuple-element.53.p8_ref, f32[3,8,128]{2,1,0:T(8,128)S(1)} %get-tuple-element.54.v8_ref, ...), custom_call_target="tpu_custom_call" | custom-call | tf_op jit(solution)/shard_map/md/pallas_call | solution.py:668
  61.3 13.8 %all_to_all.23 = f32[128,1,128]{2,1,0:T(1,128)S(1)} all-to-all(f32[128,1,128]{2,1,0:T(1,128)S(1)} %bitcast.14), channel_id=1, replica_groups=mesh['slab'=32,'md'=4] {'slab','md'}, dimensions={0} | all-to-all | bytes 131072 | tf_op jit(solution)/shard_map/all_to_all | solution.py:576
  75.1 0.8 %cells.1 = f32[4,2,64]{2,1,0:T(2,128)} custom-call(f32[128,128]{1,0:T(8,128)S(1)} %bitcast.13, s32[8,128]{1,0:T(8,128)S(1)} %get-tuple-element.66.own_ref, s32[8,128]{1,0:T(8,128)S(1)} %get-tuple-element.67.rank_ref), custom_call_target="tpu_custom_call" | custom-call | tf_op jit(solution)/shard_map/cells/pallas_call | solution.py:681
  (4 shorter events, 0.0 us)
Async XLA Ops:
  2.7 18.6 %collective-permute-start.2 = (f32[20,64,128]{2,1,0:T(8,128)S(1)}, f32[20,64,128]{2,1,0:T(8,128)S(1)}, u32[]{:S(2)}, u32[]{:S(2)}) collective-permute-start(f32[20,64,128]{2,1,0:T(8,128)S(1)} %get-tuple-element.42), channel_id=1, source_target_pairs={{0,124},{4,8},{8,4},{12,16},{16,12},{20,24},{24,20},{28,32},{32,28... | collective-permute-start | bytes 1966088 | tf_op jit(solution)/shard_map/ppermute | solution.py:626
  5.8 15.5 %collective-permute-start.3 = (f32[20,64,128]{2,1,0:T(8,128)S(1)}, f32[20,64,128]{2,1,0:T(8,128)S(1)}, u32[]{:S(2)}, u32[]{:S(2)}) collective-permute-start(f32[20,64,128]{2,1,0:T(8,128)S(1)} %get-tuple-element.43), channel_id=1, source_target_pairs={{0,4},{4,0},{8,12},{12,8},{16,20},{20,16},{24,28},{28,24},{32,36},... | collective-permute-start | bytes 1966088 | tf_op jit(solution)/shard_map/ppermute | solution.py:627
  10.2 7.0 %collective-permute-start = (f32[20,2,8,128]{3,2,1,0:T(8,128)S(1)}, f32[20,2,8,128]{3,2,1,0:T(8,128)S(1)}, u32[]{:S(2)}, u32[]{:S(2)}) collective-permute-start(f32[20,2,8,128]{3,2,1,0:T(8,128)S(1)} %get-tuple-element.39), channel_id=1, source_target_pairs={{0,1},{1,2},{2,3},{3,0},{4,5},{5,6},{6,7},{7,4},{8,9},{9,10},{10,1... | collective-permute-start | bytes 491528 | tf_op jit(solution)/shard_map/ppermute | solution.py:619
  11.4 5.8 %collective-permute-start.1 = (f32[20,2,8,128]{3,2,1,0:T(8,128)S(1)}, f32[20,2,8,128]{3,2,1,0:T(8,128)S(1)}, u32[]{:S(2)}, u32[]{:S(2)}) collective-permute-start(f32[20,2,8,128]{3,2,1,0:T(8,128)S(1)} %get-tuple-element.40), channel_id=1, source_target_pairs={{1,0},{2,1},{3,2},{0,3},{5,4},{6,5},{7,6},{4,7},{9,8},{10,9},{11,1... | collective-permute-start | bytes 491528 | tf_op jit(solution)/shard_map/ppermute | solution.py:620
  17.3 3.9 %collective-permute-start.4 = (f32[20,8,128]{2,1,0:T(8,128)S(1)}, f32[20,8,128]{2,1,0:T(8,128)S(1)}, u32[]{:S(2)}, u32[]{:S(2)}) collective-permute-start(f32[20,8,128]{2,1,0:T(8,128)S(1)} %get-tuple-element.44), channel_id=1, source_target_pairs={{0,124},{4,8},{8,4},{12,16},{16,12},{20,24},{24,20},{28,32},{32,28... | collective-permute-start | bytes 245768 | tf_op jit(solution)/shard_map/ppermute | solution.py:638
  17.4 3.9 %collective-permute-start.5 = (f32[20,8,128]{2,1,0:T(8,128)S(1)}, f32[20,8,128]{2,1,0:T(8,128)S(1)}, u32[]{:S(2)}, u32[]{:S(2)}) collective-permute-start(f32[20,8,128]{2,1,0:T(8,128)S(1)} %get-tuple-element.45), channel_id=1, source_target_pairs={{0,4},{4,0},{8,12},{12,8},{16,20},{20,16},{24,28},{28,24},{32,36},... | collective-permute-start | bytes 245768 | tf_op jit(solution)/shard_map/ppermute | solution.py:639
  21.2 5.6 %copy-start = (s32[1024,64]{0,1:T(8,128)S(1)}, s32[1024,64]{0,1:T(8,128)}, u32[]{:S(2)}) copy-start(s32[1024,64]{0,1:T(8,128)} %param.12) | copy-start | bytes 786436
  21.3 5.6 %copy-start.1 = (s32[1024]{0:T(1024)S(1)}, s32[1024]{0:T(1024)}, u32[]{:S(2)}) copy-start(s32[1024]{0:T(1024)} %param.13) | copy-start | bytes 12292
  21.3 5.6 %copy-start.2 = (f32[3,1024]{1,0:T(4,128)S(1)}, f32[3,1024]{1,0:T(4,128)}, u32[]{:S(2)}) copy-start(f32[3,1024]{1,0:T(4,128)} %pos_ref.1) | copy-start | bytes 36868
  21.3 5.6 %copy-start.3 = (f32[3,1024]{1,0:T(4,128)S(1)}, f32[3,1024]{1,0:T(4,128)}, u32[]{:S(2)}) copy-start(f32[3,1024]{1,0:T(4,128)} %vel_ref.1) | copy-start | bytes 36868
  21.3 5.6 %copy-start.4 = (s32[2,64,2]{1,2,0:T(2,128)S(1)}, s32[2,64,2]{1,2,0:T(2,128)}, u32[]{:S(2)}) copy-start(s32[2,64,2]{1,2,0:T(2,128)} %param.9) | copy-start | bytes 3076
  22.5 10.9 %collective-permute-start.6 = (f32[19,72,128]{2,1,0:T(8,128)S(1)}, f32[19,72,128]{2,1,0:T(8,128)S(1)}, u32[]{:S(2)}, u32[]{:S(2)}) collective-permute-start(f32[19,72,128]{2,1,0:T(8,128)S(1)} %get-tuple-element.48), channel_id=1, source_target_pairs={{0,124},{4,8},{8,4},{12,16},{16,12},{20,24},{24,20},{28,32},{32,28... | collective-permute-start | bytes 2101256 | tf_op jit(solution)/shard_map/ppermute | solution.py:658
  22.6 10.8 %collective-permute-start.7 = (f32[19,72,128]{2,1,0:T(8,128)S(1)}, f32[19,72,128]{2,1,0:T(8,128)S(1)}, u32[]{:S(2)}, u32[]{:S(2)}) collective-permute-start(f32[19,72,128]{2,1,0:T(8,128)S(1)} %get-tuple-element.49), channel_id=1, source_target_pairs={{0,4},{4,0},{8,12},{12,8},{16,20},{20,16},{24,28},{28,24},{32,36},... | collective-permute-start | bytes 2101256 | tf_op jit(solution)/shard_map/ppermute | solution.py:659

commit v4 on v3

--- a/solution.py
+++ b/solution.py
@@ -47,8 +47,7 @@
 falling = [flip[i] for i in rising]
 level = [i for i, c in enumerate(lattice_dirs) if c[2] == 0]
 pairs = [(1, 2), (3, 4), (5, 6)] + [(i, i + 1) for i in range(7, 19, 2)]
-NEAR = 14
-RELAX = 19
+SENT = 13
 ROWS = 72
 PAD = 88
 
@@ -137,96 +136,184 @@
     return pl.ds(8 * block_id, 8)
 
 
-def send_planes(up_ref, down_ref, plane, block, post, relax):
+def outgoing_planes(store, read, near, far, ways, relax):
+    for k, i in enumerate(ways):
+        store(k, read(i, near))
+        store(5 + k, read(i, far))
+    flat = {i: read(i, near) for i in level}
+    sums = [None, None, None]
+    for i, value in flat.items():
+        for n, sign in enumerate((1,) + lattice_dirs[i][:2]):
+            if sign == 0:
+                continue
+            if sums[n] is None:
+                sums[n] = value if sign > 0 else -value
+            else:
+                sums[n] = sums[n] + value if sign > 0 else sums[n] - value
+    for n in range(3):
+        store(10 + n, sums[n])
+    if relax is not None:
+        store(SENT, relax)
+
+
+def storing(out_ref, b):
+    def store(j, value):
+        out_ref[j, rows_of(b), :] = value
+
+    return store
+
+
+def halo_collided(from_halo, from_own, sums, relax, ways, back):
+    density, flow_x, flow_y = sums
+    arriving = None
+    leaving = None
     for k in range(5):
-        up_ref[k if plane == 1 else NEAR + k, block, :] = post[rising[k]]
-        down_ref[k if plane == 0 else NEAR + k, block, :] = post[falling[k]]
-    near_ref = up_ref if plane == 1 else down_ref
-    for k, i in enumerate(level):
-        near_ref[5 + k, block, :] = post[i]
-    if relax is not None:
-        near_ref[RELAX, block, :] = relax
+        x, y, _ = lattice_dirs[ways[k]]
+        density = density + (from_halo[k] + from_own[k])
+        arriving = from_halo[k] if arriving is None else arriving + from_halo[k]
+        leaving = from_own[k] if leaving is None else leaving + from_own[k]
+        back_x, back_y, _ = lattice_dirs[back[k]]
+        for sign, value in ((x, from_halo[k]), (back_x, from_own[k])):
+            if sign != 0:
+                flow_x = flow_x + value if sign > 0 else flow_x - value
+        for sign, value in ((y, from_halo[k]), (back_y, from_own[k])):
+            if sign != 0:
+                flow_y = flow_y + value if sign > 0 else flow_y - value
+    inverse = 1.0 / density
+    vel_x = flow_x * inverse
+    vel_y = flow_y * inverse
+    towards = (arriving - leaving) * inverse
+    usq = vel_x * vel_x + vel_y * vel_y + towards * towards
+    keep = 1.0 - relax
+    gain = relax * density
+    base = gain - (1.5 * gain) * usq
+    result = []
+    for k in range(5):
+        x, y, _ = lattice_dirs[ways[k]]
+        along = towards
+        if x != 0:
+            along = along + vel_x if x > 0 else along - vel_x
+        if y != 0:
+            along = along + vel_y if y > 0 else along - vel_y
+        weight = lattice_weights[ways[k]]
+        slope = (3.0 * weight) * (gain * along)
+        equil = weight * base + (slope + 1.5 * (along * slope))
+        result.append(rolled(keep * from_halo[k] + equil, y))
+    return result
 
 
 everything = set(range(19))
 
 
-def load_kernel(f_ref, relax_ref, low_ref, high_ref, f_out_ref, relax_out_ref, sems):
-    moves = []
-    for edge_ref, row in ((low_ref, 0), (high_ref, 56)):
-        rows = pl.ds(row, 8)
-        moves.append((f_ref.at[:, :, rows, :], edge_ref.at[0:19]))
-        moves.append((relax_ref.at[:, rows, :], edge_ref.at[RELAX]))
-    moves.append((relax_ref, relax_out_ref))
-    for part in range(4):
-        some = slice(5 * part, min(5 * part + 5, 19))
-        moves.append((f_ref.at[some], f_out_ref.at[some]))
-    copies = [pltpu.make_async_copy(*move, sems.at[n]) for n, move in enumerate(moves)]
+def first_kernel(f_hbm_ref, relax_hbm_ref,
+                 low_ref, high_ref, relax_ref, post_ref, up_ref, down_ref,
+                 f_ref, pad_ref, sems):
+    odd = parity()
+    copies = [pltpu.make_async_copy(relax_hbm_ref, relax_ref, sems.at[4])]
+    quarters = [(plane, half) for plane in range(2) for half in range(2)]
+    for n, (plane, half) in enumerate(quarters):
+        part = (slice(None), plane, pl.ds(32 * half, 32), slice(None))
+        copies.append(pltpu.make_async_copy(f_hbm_ref.at[part], f_ref.at[part], sems.at[n]))
     for copy in copies:
         copy.start()
-    for copy in copies:
-        copy.wait()
-
-
-def first_kernel(f_ref, relax_ref, post_ref, up_ref, down_ref):
-    odd = parity()
+    copies[0].wait()
+    for n, (actual_plane, half) in enumerate(quarters):
+        copies[1 + n].wait()
+        plane = jnp.where(odd == 1, 1 - actual_plane, actual_plane)
+        for b in range(4 * half, 4 * half + 4):
+            f = {i: f_ref[actual(i, odd), actual_plane, rows_of(b), :] for i in range(19)}
+            post = collided(f, relax_ref[actual_plane, rows_of(b), :], everything)
+            for i in range(19):
+                post_ref[i, plane, rows_of(b), :] = post[i]
+                if lattice_dirs[i][0] != 0:
+                    pad_ref[i, plane, pl.ds(8 + 8 * b, 8), :] = post[i]
+    head = lax.broadcasted_iota(i32, (8, 128), 0) < 4
+    for i in range(20):
+        ends = [
+            [
+                (f_ref[i, plane, rows_of(b), :] if i < 19 else relax_ref[plane, rows_of(b), :])
+                for plane in range(2)
+            ]
+            for b in (0, 7)
+        ]
+        low_ref[i] = jnp.where(head, ends[0][0], pltpu.roll(ends[0][1], 4, 0))
+        high_ref[i] = jnp.where(head, pltpu.roll(ends[1][0], 4, 0), ends[1][1])
     for plane in range(2):
         actual_plane = jnp.where(odd == 1, 1 - plane, plane)
+        out_ref, ways = (up_ref, rising) if plane == 1 else (down_ref, falling)
         for b in range(8):
-            f = {i: f_ref[actual(i, odd), actual_plane, rows_of(b), :] for i in range(19)}
-            relax = relax_ref[actual_plane, rows_of(b), :]
-            post = collided(f, relax, everything)
-            for i in range(19):
-                post_ref[i, plane, rows_of(b), :] = post[i]
-            send_planes(up_ref, down_ref, plane, rows_of(b), post, relax)
-
-
-def edge_kernel(low_ref, high_ref, post_ref, up_ref, down_ref, relax_ref):
+
+            def read(i, source):
+                shift = lattice_dirs[i][0]
+                if shift == 0:
+                    return post_ref[i, source, rows_of(b), :]
+                return pad_ref[i, source, pl.ds(8 + 8 * b - shift, 8), :]
+
+            outgoing_planes(
+                storing(out_ref, b), read, plane, 1 - plane, ways,
+                relax_ref[actual_plane, rows_of(b), :],
+            )
+
+
+def edge_kernel(low_ref, high_ref, post_ref, seam_ref, up_ref, down_ref, relax_ref):
     odd = parity()
-    head = lax.broadcasted_iota(i32, (8, 128), 0) < 4
+    row_id = lax.broadcasted_iota(i32, (8, 128), 0)
+    mixed_relax = []
     for plane in range(2):
         actual_plane = jnp.where(odd == 1, 1 - plane, plane)
+        upper = jnp.broadcast_to(actual_plane, (8, 128)) == 1
         mixed = []
         for i in range(20):
             j = actual(i, odd) if i < 19 else i
-            mixed.append(jnp.where(head, high_ref[j, actual_plane], low_ref[j, actual_plane]))
-        post = collided(dict(enumerate(mixed[:19])), mixed[RELAX], everything)
-        relax_ref[plane] = mixed[RELAX]
+            high = high_ref[j]
+            low = low_ref[j]
+            high = jnp.where(upper, pltpu.roll(high, 4, 0), high)
+            low = jnp.where(upper, low, pltpu.roll(low, 4, 0))
+            mixed.append(jnp.where(row_id < 4, high, low))
+        post = collided(dict(enumerate(mixed[:19])), mixed[19], everything)
+        relax_ref[plane] = mixed[19]
+        mixed_relax.append(mixed[19])
         for i in range(19):
-            post_ref[i, plane] = post[i]
-        send_planes(up_ref, down_ref, plane, rows_of(0), post, mixed[RELAX])
+            seam_ref[2 * i + plane, 0:8, :] = post_ref[i, plane, 56:64, :]
+            seam_ref[2 * i + plane, 8:16, :] = post[i]
+            seam_ref[2 * i + plane, 16:24, :] = post_ref[i, plane, 0:8, :]
+
+    def read(i, source):
+        shift = lattice_dirs[i][0]
+        at = [seam_ref[2 * i + source, pl.ds(start - shift, 8), :] for start in (4, 8, 12)]
+        return jnp.where(row_id == 3, at[0], jnp.where(row_id == 4, at[2], at[1]))
+
+    outgoing_planes(storing(up_ref, 0), read, 1, 0, rising, mixed_relax[1])
+    outgoing_planes(storing(down_ref, 0), read, 0, 1, falling, mixed_relax[0])
 
 
 def two_steps(own, below, above, relax, second_ref, from_below_ref, from_above_ref):
     for b in range(9):
-        for plane in (-1, 0, 1, 2):
+        for plane in range(2):
             f = {}
             for i, c in enumerate(lattice_dirs):
                 source = plane - c[2]
                 if source in (0, 1):
                     f[i] = own(i, source, b, c[0])
+                elif source < 0:
+                    f[i] = below(rising.index(i), b)
                 else:
-                    side = below if source < 0 else above
-                    if c[2] == 0:
-                        j = 5 + level.index(i)
-                    else:
-                        j = (rising if c[2] == 1 else falling).index(i)
-                        if source in (-2, 3):
-                            j = NEAR + j
-                    f[i] = side(j, b, c[0])
-            wanted = everything
-            if plane == -1:
-                wanted = set(rising)
-            elif plane == 2:
-                wanted = set(falling)
-            post = collided(f, relax(plane, b), wanted)
+                    f[i] = above(falling.index(i), b)
+            post = collided(f, relax(plane, b), everything)
             for i, value in post.items():
-                if plane == -1:
-                    put(from_below_ref, (rising.index(i),), b, value)
-                elif plane == 2:
-                    put(from_above_ref, (falling.index(i),), b, value)
-                else:
-                    put(second_ref, (i, plane), b, value)
+                put(second_ref, (i, plane), b, value)
+        for side, ways, back, source, plane, out_ref in (
+            (below, rising, falling, 0, -1, from_below_ref),
+            (above, falling, rising, 1, 2, from_above_ref),
+        ):
+            post = halo_collided(
+                [side(5 + k, b) for k in range(5)],
+                [own(i, source, b, lattice_dirs[i][0]) for i in back],
+                [side(10 + n, b) for n in range(3)],
+                relax(plane, b), ways, back,
+            )
+            for k in range(5):
+                put(out_ref, (k,), b, post[k])
 
 
 def streamed(second_ref, from_below_ref, from_above_ref, plane, b):
@@ -242,69 +329,44 @@
     return f
 
 
-sliding = [k for k, i in enumerate(rising + level + rising) if lattice_dirs[i][0] != 0]
-moving = [i for i, c in enumerate(lattice_dirs) if c[0] != 0]
-
-
-def seamed(seam_ref, slots, at):
-    for slot, key in enumerate(slots):
-        for part, b in enumerate((7, 8, 0)):
-            seam_ref[slot, 8 * part : 8 * part + 8, :] = at(key, b)
-
-    def read(key, b, shift, main):
-        if shift == 0:
-            return at(key, b)
-        slot = slots.index(key)
-        if b == 8:
-            return seam_ref[slot, 8 - shift : 16 - shift, :]
-        if b == 0 and shift == 1:
-            return seam_ref[slot, 15:23, :]
-        if b == 7 and shift == -1:
-            return seam_ref[slot, 1:9, :]
-        return main(8 * b - shift)
-
-    return read
-
-
-def reader(seam_ref, main_ref, edge_ref):
-    def at(j, b):
-        if edge_ref is None or b < 8:
-            return main_ref[j, rows_of(b), :]
-        return edge_ref[j, rows_of(0), :]
-
-    read = seamed(seam_ref, sliding, at)
-    return lambda j, b, shift: read(j, b, shift, lambda row: main_ref[j, row : row + 8, :])
-
-
-def own_reader(seam_ref, main_ref, edge_ref):
-    def at(key, b):
-        i, plane = key
-        return main_ref[i, plane, rows_of(b), :] if b < 8 else edge_ref[i, plane]
-
-    read = seamed(seam_ref, [(i, plane) for i in moving for plane in range(2)], at)
-    return lambda i, plane, b, shift: read(
-        (i, plane), b, shift, lambda row: main_ref[i, plane, row : row + 8, :]
-    )
-
-
-def middle_kernel(post_ref, post_edge_ref, below_ref, above_ref, below_edge_ref, above_edge_ref,
+def middle_kernel(post_ref, seam_ref, below_ref, above_ref, below_edge_ref, above_edge_ref,
                   relax_ref, relax_edge_ref,
                   third_ref, up_ref, down_ref, relax_out_ref,
-                  second_ref, from_below_ref, from_above_ref, below_seam_ref, above_seam_ref,
-                  own_seam_ref):
+                  second_ref, from_below_ref, from_above_ref):
     odd = parity()
-    own = own_reader(own_seam_ref, post_ref, post_edge_ref)
-    below = reader(below_seam_ref, below_ref, below_edge_ref)
-    above = reader(above_seam_ref, above_ref, above_edge_ref)
+    row_id = lax.broadcasted_iota(i32, (8, 128), 0)
+
+    def own(i, plane, b, shift):
+        if b == 8:
+            return seam_ref[2 * i + plane, 8 - shift : 16 - shift, :]
+        if b == 0 and shift == 1:
+            return seam_ref[2 * i + plane, 15:23, :]
+        if b == 7 and shift == -1:
+            return seam_ref[2 * i + plane, 1:9, :]
+        return post_ref[i, plane, 8 * b - shift : 8 * b - shift + 8, :]
+
+    def joined(main_ref, edge_ref):
+        def read(j, b):
+            if b == 8:
+                return edge_ref[j]
+            if b in (0, 7):
+                turned = pltpu.roll(edge_ref[j], 4, 0)
+                return jnp.where(row_id == b, turned, main_ref[j, rows_of(b), :])
+            return main_ref[j, rows_of(b), :]
+
+        return read
+
+    below = joined(below_ref, below_edge_ref)
+    above = joined(above_ref, above_edge_ref)
     for b in range(8):
-        relax_out_ref[0, rows_of(b), :] = below_ref[RELAX, rows_of(b), :]
-        relax_out_ref[3, rows_of(b), :] = above_ref[RELAX, rows_of(b), :]
+        relax_out_ref[0, rows_of(b), :] = below_ref[SENT, rows_of(b), :]
+        relax_out_ref[3, rows_of(b), :] = above_ref[SENT, rows_of(b), :]
         for plane in range(2):
             relax_out_ref[1 + plane, rows_of(b), :] = relax_ref[
                 jnp.where(odd == 1, 1 - plane, plane), rows_of(b), :
             ]
-    relax_out_ref[0, rows_of(8), :] = below_edge_ref[RELAX, rows_of(0), :]
-    relax_out_ref[3, rows_of(8), :] = above_edge_ref[RELAX, rows_of(0), :]
+    relax_out_ref[0, rows_of(8), :] = below_edge_ref[SENT]
+    relax_out_ref[3, rows_of(8), :] = above_edge_ref[SENT]
     for plane in range(2):
         relax_out_ref[1 + plane, rows_of(8), :] = relax_edge_ref[plane]
 
@@ -318,16 +380,43 @@
             post = collided(f, relax(plane, b), everything)
             for i in range(19):
                 put(third_ref, (i, plane), b, post[i])
-            send_planes(up_ref, down_ref, plane, rows_of(b), post, None)
+    for b in range(9):
+
+        def read(i, source):
+            return get(third_ref, (i, source), b, lattice_dirs[i][0])
+
+        for out_ref, near, ways in ((up_ref, 1, rising), (down_ref, 0, falling)):
+            ends = {}
+
+            def store(j, value):
+                if b < 8:
+                    out_ref[8 * j + b] = value
+                else:
+                    ends[j] = pltpu.roll(value, 2 * (j % 4) + 1, 0)
+
+            outgoing_planes(store, read, near, 1 - near, ways, None)
+            for group in range(4 if ends else 0):
+                block = ends[4 * group]
+                for m in range(1, min(4, SENT - 4 * group)):
+                    block = jnp.where((row_id >> 1) == m, ends[4 * group + m], block)
+                out_ref[8 * SENT + group] = block
 
 
 def last_kernel(post_ref, below_ref, above_ref, relax_ref, inv_ref,
                 f_ref, out_ref,
-                second_ref, from_below_ref, from_above_ref, below_seam_ref, above_seam_ref,
-                flow_ref):
+                second_ref, from_below_ref, from_above_ref, flow_ref):
     odd = parity()
-    below = reader(below_seam_ref, below_ref, None)
-    above = reader(above_seam_ref, above_ref, None)
+
+    def side(ref):
+        def read(j, b):
+            if b < 8:
+                return ref[8 * j + b]
+            return pltpu.roll(ref[8 * SENT + j // 4], 7 - 2 * (j % 4), 0)
+
+        return read
+
+    below = side(below_ref)
+    above = side(above_ref)
 
     def own(i, plane, b, shift):
         return get(post_ref, (i, plane), b, shift)
@@ -388,8 +477,8 @@
     return tuple(t + g * weight for t, g in zip(total, gaps))
 
 
-def over_list(entry, start):
-    return lax.fori_loop(0, 64, entry, start, unroll=16)
+def over_list(entry, start, unroll):
+    return lax.fori_loop(0, 64, entry, start, unroll=unroll)
 
 
 def blank():
@@ -452,7 +541,7 @@
             near_ref[k, c] = near[c]
         return pull(total, near, here)
 
-    total = over_list(positions, blank())
+    total = over_list(positions, blank(), 32)
     for c in range(3):
         force_ref[c] = total[c]
     speeds = [chunks(v8_ref[c]) for c in range(3)]
@@ -462,15 +551,19 @@
             drift_ref[k, c] = time_step * speed
         return none
 
-    over_list(drifts, 0)
+    over_list(drifts, 0, 32)
 
 
 def md_kernel(arr_ref, p8_ref, v8_ref, force_ref, list_ref, near_in_ref, drift_in_ref,
               slot_ref, hot_ref, icnt_ref, f_ref,
-              pos_ref, vel_ref, mom_ref, f_out_ref,
-              near_ref, drift_ref, sem):
-    saved = pltpu.make_async_copy(f_ref, f_out_ref, sem)
-    saved.start()
+              pos_out_ref, vel_out_ref, mom_ref, f_out_ref,
+              near_ref, drift_ref, pos_ref, vel_ref, sems):
+    saved = [
+        pltpu.make_async_copy(f_ref, f_out_ref, sems.at[0]),
+        pltpu.make_async_copy(pos_ref, pos_out_ref, sems.at[1]),
+        pltpu.make_async_copy(vel_ref, vel_out_ref, sems.at[2]),
+    ]
+    saved[0].start()
     table = arr_ref[...].T
     slots = slot_ref[...]
     source = slots >> 2
@@ -522,11 +615,17 @@
                     near_ref[k, c] = near[c]
                 return pull(total, near, here)
 
-            pair = over_list(entry, blank())
+            pair = over_list(entry, blank(), 64)
         for c in range(3):
             force = pair_strength * pair[c] + drag * (target[c] - vel[c])
             vel[c] = vel[c] + time_step * force
             pos[c] = pos[c] + time_step * vel[c]
+    for c in range(3):
+        for s in range(8):
+            pos_ref[c : c + 1, s * 128 : (s + 1) * 128] = pos[c][s : s + 1, :]
+            vel_ref[c : c + 1, s * 128 : (s + 1) * 128] = vel[c][s : s + 1, :]
+    saved[1].start()
+    saved[2].start()
     speed = vel[0] * vel[0] + vel[1] * vel[1] + vel[2] * vel[2]
     data = vel + [speed]
     row_id = lax.broadcasted_iota(i32, (16, 128), 0)
@@ -538,7 +637,7 @@
             value = jnp.where(comp == c, spread(data[c], s, 16), value)
         value = jnp.where((spread(slots, s, 16) & 3) == (row_id >> 2), value, 0.0)
         hot = hot_ref[:, s * 128 : (s + 1) * 128]
-        for part in range(3):
+        for _ in range(3):
             piece = value.astype(bf16)
             value = value - piece.astype(f32)
             sums = sums + lax.dot_general(
@@ -546,11 +645,8 @@
             )
     mom_ref[...] = jnp.zeros((128, 128), f32)
     mom_ref[:, :16] = sums * icnt_ref[...]
-    for c in range(3):
-        for s in range(8):
-            pos_ref[c : c + 1, s * 128 : (s + 1) * 128] = pos[c][s : s + 1, :]
-            vel_ref[c : c + 1, s * 128 : (s + 1) * 128] = vel[c][s : s + 1, :]
-    saved.wait()
+    for copy in saved:
+        copy.wait()
 
 
 def cell_kernel(back_ref, own_ref, rank_ref, out_ref):
@@ -580,7 +676,7 @@
 far_pairs = [(i, (i + 1) % 32 if i % 2 else (i - 1) % 32) for i in range(32)]
 
 
-def on_device(populations, relax, owners, positions, velocities, neighbours, atom_slots):
+def whole(populations, relax, owners, positions, velocities, neighbours, atom_slots):
     slots = atom_slots.reshape(8, 128)
     eights = shape(3, 8, 128)
     own, inv, rank, hot, icnt, force, p8, v8, lists, near, drift = pl.pallas_call(
@@ -601,60 +697,59 @@
         name="prep", compiler_params=room,
     )(owners.transpose(0, 2, 1), slots, positions, velocities, neighbours.T)
     hbm = pl.BlockSpec(memory_space=pltpu.HBM)
-    low, high, f_near, relax = pl.pallas_call(
-        load_kernel,
+    low, high, relax, post, up, down = pl.pallas_call(
+        first_kernel,
         in_specs=[hbm, hbm],
         out_shape=(
-            pltpu.VMEM((20, 2, 8, 128), f32),
-            pltpu.VMEM((20, 2, 8, 128), f32),
+            pltpu.VMEM((20, 8, 128), f32),
+            pltpu.VMEM((20, 8, 128), f32),
+            pltpu.VMEM((2, 64, 128), f32),
             pltpu.VMEM((19, 2, 64, 128), f32),
-            pltpu.VMEM((2, 64, 128), f32),
+            pltpu.VMEM((SENT + 1, 64, 128), f32),
+            pltpu.VMEM((SENT + 1, 64, 128), f32),
         ),
-        scratch_shapes=[pltpu.SemaphoreType.DMA((9,))],
-        name="load", compiler_params=room,
+        scratch_shapes=[
+            pltpu.VMEM((19, 2, 64, 128), f32),
+            pltpu.VMEM((19, 2, 80, 128), f32),
+            pltpu.SemaphoreType.DMA((5,)),
+        ],
+        name="first", compiler_params=room,
     )(
         pltpu.with_memory_space_constraint(populations, pltpu.HBM),
         pltpu.with_memory_space_constraint(relax, pltpu.HBM),
     )
+    below = lax.ppermute(down, "slab", far_pairs)
     from_low = lax.ppermute(high, "md", [(i, (i + 1) % 4) for i in range(4)])
     from_high = lax.ppermute(low, "md", [((i + 1) % 4, i) for i in range(4)])
-    post, up, down = pl.pallas_call(
-        first_kernel,
-        out_shape=(shape(19, 2, 64, 128), shape(20, 64, 128), shape(20, 64, 128)),
-        name="first", compiler_params=room,
-    )(f_near, relax)
-    below = lax.ppermute(down, "slab", far_pairs)
     above = lax.ppermute(up, "slab", near_pairs)
-    post_edge, up_edge, down_edge, relax_edge = pl.pallas_call(
+    seam, up_edge, down_edge, relax_edge = pl.pallas_call(
         edge_kernel,
         out_shape=(
-            shape(19, 2, 8, 128),
-            shape(20, 8, 128),
-            shape(20, 8, 128),
+            shape(38, 24, 128),
+            shape(SENT + 1, 8, 128),
+            shape(SENT + 1, 8, 128),
             shape(2, 8, 128),
         ),
         name="edge", compiler_params=room,
-    )(from_low, from_high)
+    )(from_low, from_high, post)
     below_edge = lax.ppermute(down_edge, "slab", far_pairs)
     above_edge = lax.ppermute(up_edge, "slab", near_pairs)
     scratch = [
         pltpu.VMEM((19, 2, PAD, 128), f32),
         pltpu.VMEM((5, PAD, 128), f32),
         pltpu.VMEM((5, PAD, 128), f32),
-        pltpu.VMEM((len(sliding), 24, 128), f32),
-        pltpu.VMEM((len(sliding), 24, 128), f32),
     ]
     post, up, down, relax_all = pl.pallas_call(
         middle_kernel,
         out_shape=(
             shape(19, 2, PAD, 128),
-            shape(19, ROWS, 128),
-            shape(19, ROWS, 128),
+            shape(8 * SENT + 4, 8, 128),
+            shape(8 * SENT + 4, 8, 128),
             shape(4, ROWS, 128),
         ),
-        scratch_shapes=scratch + [pltpu.VMEM((2 * len(moving), 24, 128), f32)],
+        scratch_shapes=scratch,
         name="middle", compiler_params=room,
-    )(post, post_edge, below, above, below_edge, above_edge, relax, relax_edge)
+    )(post, seam, below, above, below_edge, above_edge, relax, relax_edge)
     below = lax.ppermute(down, "slab", far_pairs)
     above = lax.ppermute(up, "slab", near_pairs)
     f, outgoing = pl.pallas_call(
@@ -668,25 +763,29 @@
     pos_out, vel_out, moms, f_out = pl.pallas_call(
         md_kernel,
         in_specs=[vmem] * 11,
-        out_specs=(vmem, vmem, vmem, hbm),
-        out_shape=(shape(3, 1024), shape(3, 1024), shape(128, 128), shape(19, 2, 64, 128)),
+        out_specs=(hbm, hbm, vmem, hbm),
+        out_shape=(
+            shape(3, 1024), shape(3, 1024), shape(128, 128), shape(19, 2, 64, 128)
+        ),
         scratch_shapes=[
             pltpu.VMEM((64, 3, 8, 128), f32),
             pltpu.VMEM((64, 3, 8, 128), f32),
-            pltpu.SemaphoreType.DMA,
+            pltpu.VMEM((3, 1024), f32),
+            pltpu.VMEM((3, 1024), f32),
+            pltpu.SemaphoreType.DMA((3,)),
         ],
         name="md", compiler_params=room,
     )(arrived, p8, v8, force, lists, near, drift, slots, hot, icnt, f)
     returned = exchange(moms)
-    cell = pl.pallas_call(cell_kernel, out_shape=shape(4, 2, 64), name="cells", compiler_params=room)(
-        returned, own, rank
-    )
+    cell = pl.pallas_call(
+        cell_kernel, out_shape=shape(4, 2, 64), name="cells", compiler_params=room
+    )(returned, own, rank)
     return (f_out, pos_out, vel_out, cell)
 
 
 def solution(mesh):
     return jax.shard_map(
-        on_device,
+        whole,
         mesh=mesh,
         in_specs=(
             P(None, "slab", "md", None),

time: 76.1 us -> 70.1 us (0.921)
  waiting for transfers between devices: 9 us -> 5.19 us
  Pallas kernels: 16.1 us -> 14.6 us
    ppermute x8, waiting for transfers between devices: 9 us -> 5.19 us  [the longest x1 2.65 us: whole(): below_edge = lax.ppermute(down_edge, 'slab', far_pairs)]
    pallas_call x8 -> x7, Pallas kernels: 16.1 us -> 14.6 us  [the longest x1 4.81 us: whole(): pl.pallas_call(md_kernel, in_specs=[vmem] * 11, out_specs=(hbm, hbm, vmem...]
  transfers between devices with their start and end apart: 8 -> 8, of which waited for: 3 -> 2; matrix products, arithmetic and copies ran while one was open for 0% -> 0% of each run, Pallas kernels for 6% -> 7%
where the time goes in v4:
time: 70.1 us; the launch traced here: 69.9 us
  blocking collectives  33.8 us (48%)
  starting transfers between devices  15.6 us (22%)
  Pallas kernels  14.6 us (21%)
  waiting for transfers between devices  5.19 us (7%)
  between operations  0.77 us (1%)
    all_to_all x2, blocking collectives, exchange(): lax.all_to_all(rows, ('slab', 'md'), split_axis=0, concat_axis=0, tiled=T...  33.8 us
    ppermute x2, starting transfers between devices, whole(): above = lax.ppermute(up, 'slab', near_pairs)  8.67 us
    pallas_call x1, Pallas kernels, whole(): pl.pallas_call(md_kernel, in_specs=[vmem] * 11, out_specs=(hbm, hbm, vmem...  4.81 us
    pallas_call x1, Pallas kernels, whole(): pl.pallas_call(prep_kernel, out_shape=(shape(8, 128, dtype=i32), shape(8,...  4.39 us
    ppermute x2, starting transfers between devices, whole(): below = lax.ppermute(down, 'slab', far_pairs)  3.18 us
    ppermute x1, waiting for transfers between devices, whole(): below_edge = lax.ppermute(down_edge, 'slab', far_pairs)  2.65 us
    ppermute x1, waiting for transfers between devices, whole(): from_low = lax.ppermute(high, 'md', [(i, (i + 1) % 4) for i in range(4)])  2.53 us
    pallas_call x1, Pallas kernels, whole(): pl.pallas_call(first_kernel, in_specs=[hbm, hbm], out_shape=(pltpu.VMEM((...  1.9 us
  transfers between devices with their start and end apart: 8, of which 2 were waited for; matrix products, arithmetic and copies ran while one was open for 0% of the time, Pallas kernels for 7%

profile of v4, /device:TPU:1, one launch (start us, length us, event | category | flops | bytes accessed | tf_op | source)
XLA Modules:
  0.0 69.9 jit_solution(13592527437274734591)
XLA Ops:
  0.6 1.9 %first.1 = (f32[20,8,128]{2,1,0:T(8,128)S(1)}, f32[20,8,128]{2,1,0:T(8,128)S(1)}, f32[2,64,128]{2,1,0:T(8,128)S(1)}, f32[19,2,64,128]{3,2,1,0:T(8,128)S(1)}, f32...) custom-call(f32[19,2,64,128]{3,2,1,0:T(8,128)} %f_hbm_ref.1, f32[2,64,128]{2,1,0:T(8,128)} %relax_hbm_ref.1), custom_call_target="tpu_custom_call" | custom-call | tf_op jit(solution)/shard_map/first/pallas_call | solution.py:700
  2.5 3.1 %collective-permute-start.2 = (f32[14,64,128]{2,1,0:T(8,128)S(1)}, f32[14,64,128]{2,1,0:T(8,128)S(1)}, u32[]{:S(2)}, u32[]{:S(2)}) collective-permute-start(f32[14,64,128]{2,1,0:T(8,128)S(1)} %get-tuple-element.39), channel_id=1, source_target_pairs={{0,124},{4,8},{8,4},{12,16},{16,12},{20,24},{24,20},{28,32},{32,28... | collective-permute-start | bytes 1376264 | tf_op jit(solution)/shard_map/ppermute | solution.py:721
  5.6 4.4 %collective-permute-start.3 = (f32[14,64,128]{2,1,0:T(8,128)S(1)}, f32[14,64,128]{2,1,0:T(8,128)S(1)}, u32[]{:S(2)}, u32[]{:S(2)}) collective-permute-start(f32[14,64,128]{2,1,0:T(8,128)S(1)} %get-tuple-element.40), channel_id=1, source_target_pairs={{0,4},{4,0},{8,12},{12,8},{16,20},{20,16},{24,28},{28,24},{32,36},... | collective-permute-start | bytes 1376264 | tf_op jit(solution)/shard_map/ppermute | solution.py:724
  10.0 1.2 %collective-permute-start = (f32[20,8,128]{2,1,0:T(8,128)S(1)}, f32[20,8,128]{2,1,0:T(8,128)S(1)}, u32[]{:S(2)}, u32[]{:S(2)}) collective-permute-start(f32[20,8,128]{2,1,0:T(8,128)S(1)} %get-tuple-element.36), channel_id=1, source_target_pairs={{0,1},{1,2},{2,3},{3,0},{4,5},{5,6},{6,7},{7,4},{8,9},{9,10},{10,1... | collective-permute-start | bytes 245768 | tf_op jit(solution)/shard_map/ppermute | solution.py:722
  11.2 1.5 %collective-permute-start.1 = (f32[20,8,128]{2,1,0:T(8,128)S(1)}, f32[20,8,128]{2,1,0:T(8,128)S(1)}, u32[]{:S(2)}, u32[]{:S(2)}) collective-permute-start(f32[20,8,128]{2,1,0:T(8,128)S(1)} %get-tuple-element.37), channel_id=1, source_target_pairs={{1,0},{2,1},{3,2},{0,3},{5,4},{6,5},{7,6},{4,7},{9,8},{10,9},{11,1... | collective-permute-start | bytes 245768 | tf_op jit(solution)/shard_map/ppermute | solution.py:723
  12.7 2.5 %collective-permute-done.low_ref = f32[20,8,128]{2,1,0:T(8,128)S(1)} collective-permute-done((f32[20,8,128]{2,1,0:T(8,128)S(1)}, f32[20,8,128]{2,1,0:T(8,128)S(1)}, u32[]{:S(2)}, u32[]{:S(2)}) %collective-permute-start) | collective-permute-done | bytes 81952 | tf_op jit(solution)/shard_map/ppermute | solution.py:722
  15.2 0.0 collective-permute-done.1.high_ref
  15.2 0.2 edge.1
  15.4 0.1 collective-permute-start.4
  15.5 0.9 %collective-permute-start.5 = (f32[14,8,128]{2,1,0:T(8,128)S(1)}, f32[14,8,128]{2,1,0:T(8,128)S(1)}, u32[]{:S(2)}, u32[]{:S(2)}) collective-permute-start(f32[14,8,128]{2,1,0:T(8,128)S(1)} %get-tuple-element.42), channel_id=1, source_target_pairs={{0,4},{4,0},{8,12},{12,8},{16,20},{20,16},{24,28},{28,24},{32,36},... | collective-permute-start | bytes 172040 | tf_op jit(solution)/shard_map/ppermute | solution.py:736
  16.5 2.6 %collective-permute-done.4.below_edge_ref = f32[14,8,128]{2,1,0:T(8,128)S(1)} collective-permute-done((f32[14,8,128]{2,1,0:T(8,128)S(1)}, f32[14,8,128]{2,1,0:T(8,128)S(1)}, u32[]{:S(2)}, u32[]{:S(2)}) %collective-permute-start.4) | collective-permute-done | bytes 57376 | tf_op jit(solution)/shard_map/ppermute | solution.py:735
  19.1 0.0 collective-permute-done.5.above_edge_ref
  19.1 0.0 collective-permute-done.2.below_ref
  19.1 0.0 collective-permute-done.3.above_ref
  19.1 0.0 copy-start
  19.1 0.0 copy-start.1
  19.2 0.0 copy-start.2
  19.2 0.0 copy-start.3
  19.2 0.0 copy-start.4
  19.2 1.3 %middle.1 = (f32[19,2,88,128]{3,2,1,0:T(8,128)S(1)}, f32[108,8,128]{2,1,0:T(8,128)S(1)}, f32[108,8,128]{2,1,0:T(8,128)S(1)}, f32[4,72,128]{2,1,0:T(8,128)S(1)}) custom-call(f32[19,2,64,128]{3,2,1,0:T(8,128)S(1)} %get-tuple-element.35.post_ref, f32[38,24,128]{2,1,0:T(8,128)S(1)} %get-tuple-element.38.seam_ref, ...), custom_call_target="tpu_custom_call" | custom-call | tf_op jit(solution)/shard_map/middle/pallas_call | solution.py:742
  20.5 0.1 collective-permute-start.6
  20.6 4.3 %collective-permute-start.7 = (f32[108,8,128]{2,1,0:T(8,128)S(1)}, f32[108,8,128]{2,1,0:T(8,128)S(1)}, u32[]{:S(2)}, u32[]{:S(2)}) collective-permute-start(f32[108,8,128]{2,1,0:T(8,128)S(1)} %get-tuple-element.47), channel_id=1, source_target_pairs={{0,4},{4,0},{8,12},{12,8},{16,20},{20,16},{24,28},{28,24},{32,36},... | collective-permute-start | bytes 1327112 | tf_op jit(solution)/shard_map/ppermute | solution.py:754
  24.8 0.0 copy-done
  24.8 0.0 copy-done.3
  24.8 4.4 %prep.1 = (s32[8,128]{1,0:T(8,128)S(1)}, s32[8,128]{1,0:T(8,128)S(1)}, s32[8,128]{1,0:T(8,128)S(1)}, bf16[128,1024]{1,0:T(8,128)(2,1)S(1)}, f32[128,16]{1,0:T(8,...) custom-call(s32[2,2,64]{2,1,0:T(2,128)S(1)} %bitcast.18, ...), custom_call_target="tpu_custom_call" | custom-call | tf_op jit(solution)/shard_map/prep/pallas_call | solution.py:682
  29.2 0.0 collective-permute-done.6.below_ref
  29.2 0.0 collective-permute-done.7.above_ref
  29.3 1.2 %last.1 = (f32[19,2,64,128]{3,2,1,0:T(8,128)S(1)}, f32[128,128]{1,0:T(8,128)S(1)}) custom-call(f32[19,2,88,128]{3,2,1,0:T(8,128)S(1)} %get-tuple-element.45.post_ref, f32[108,8,128]{2,1,0:T(8,128)S(1)} %collective-permute-done.6.below_ref, f32[108,8,128]{2,1,0:T(8,128)S(1)} %collective-permute-done.7.above_ref, ...), custom_call_target="tpu_custom_call" | custom-call | tf_op jit(solution)/shard_map/last/pallas_call | solution.py:755
  30.4 20.1 %all_to_all.22 = f32[128,1,128]{2,1,0:T(1,128)S(1)} all-to-all(f32[128,1,128]{2,1,0:T(1,128)S(1)} %bitcast.15), channel_id=1, replica_groups=mesh['slab'=32,'md'=4] {'slab','md'}, dimensions={0} | all-to-all | bytes 131072 | tf_op jit(solution)/shard_map/all_to_all | solution.py:672
  50.5 4.8 %md.1 = (f32[3,1024]{1,0:T(4,128)}, f32[3,1024]{1,0:T(4,128)}, f32[128,128]{1,0:T(8,128)S(1)}, f32[19,2,64,128]{3,2,1,0:T(8,128)}) custom-call(f32[128,128]{1,0:T(8,128)S(1)} %bitcast.11, f32[3,8,128]{2,1,0:T(8,128)S(1)} %get-tuple-element.51.p8_ref, f32[3,8,128]{2,1,0:T(8,128)S(1)} %get-tuple-element.52.v8_ref, ...), custom_call_target="tpu_custom_call" | custom-call | tf_op jit(solution)/shard_map/md/pallas_call | solution.py:763
  55.3 13.8 %all_to_all.23 = f32[128,1,128]{2,1,0:T(1,128)S(1)} all-to-all(f32[128,1,128]{2,1,0:T(1,128)S(1)} %bitcast.14), channel_id=1, replica_groups=mesh['slab'=32,'md'=4] {'slab','md'}, dimensions={0} | all-to-all | bytes 131072 | tf_op jit(solution)/shard_map/all_to_all | solution.py:672
  69.1 0.8 %cells.1 = f32[4,2,64]{2,1,0:T(2,128)} custom-call(f32[128,128]{1,0:T(8,128)S(1)} %bitcast.13, s32[8,128]{1,0:T(8,128)S(1)} %get-tuple-element.64.own_ref, s32[8,128]{1,0:T(8,128)S(1)} %get-tuple-element.65.rank_ref), custom_call_target="tpu_custom_call" | custom-call | tf_op jit(solution)/shard_map/cells/pallas_call | solution.py:780
  (3 shorter events, 0.0 us)
Async XLA Ops:
  2.5 16.6 %collective-permute-start.2 = (f32[14,64,128]{2,1,0:T(8,128)S(1)}, f32[14,64,128]{2,1,0:T(8,128)S(1)}, u32[]{:S(2)}, u32[]{:S(2)}) collective-permute-start(f32[14,64,128]{2,1,0:T(8,128)S(1)} %get-tuple-element.39), channel_id=1, source_target_pairs={{0,124},{4,8},{8,4},{12,16},{16,12},{20,24},{24,20},{28,32},{32,28... | collective-permute-start | bytes 1376264 | tf_op jit(solution)/shard_map/ppermute | solution.py:721
  5.6 13.5 %collective-permute-start.3 = (f32[14,64,128]{2,1,0:T(8,128)S(1)}, f32[14,64,128]{2,1,0:T(8,128)S(1)}, u32[]{:S(2)}, u32[]{:S(2)}) collective-permute-start(f32[14,64,128]{2,1,0:T(8,128)S(1)} %get-tuple-element.40), channel_id=1, source_target_pairs={{0,4},{4,0},{8,12},{12,8},{16,20},{20,16},{24,28},{28,24},{32,36},... | collective-permute-start | bytes 1376264 | tf_op jit(solution)/shard_map/ppermute | solution.py:724
  10.0 5.2 %collective-permute-start = (f32[20,8,128]{2,1,0:T(8,128)S(1)}, f32[20,8,128]{2,1,0:T(8,128)S(1)}, u32[]{:S(2)}, u32[]{:S(2)}) collective-permute-start(f32[20,8,128]{2,1,0:T(8,128)S(1)} %get-tuple-element.36), channel_id=1, source_target_pairs={{0,1},{1,2},{2,3},{3,0},{4,5},{5,6},{6,7},{7,4},{8,9},{9,10},{10,1... | collective-permute-start | bytes 245768 | tf_op jit(solution)/shard_map/ppermute | solution.py:722
  11.2 4.0 %collective-permute-start.1 = (f32[20,8,128]{2,1,0:T(8,128)S(1)}, f32[20,8,128]{2,1,0:T(8,128)S(1)}, u32[]{:S(2)}, u32[]{:S(2)}) collective-permute-start(f32[20,8,128]{2,1,0:T(8,128)S(1)} %get-tuple-element.37), channel_id=1, source_target_pairs={{1,0},{2,1},{3,2},{0,3},{5,4},{6,5},{7,6},{4,7},{9,8},{10,9},{11,1... | collective-permute-start | bytes 245768 | tf_op jit(solution)/shard_map/ppermute | solution.py:723
  15.4 3.7 %collective-permute-start.4 = (f32[14,8,128]{2,1,0:T(8,128)S(1)}, f32[14,8,128]{2,1,0:T(8,128)S(1)}, u32[]{:S(2)}, u32[]{:S(2)}) collective-permute-start(f32[14,8,128]{2,1,0:T(8,128)S(1)} %get-tuple-element.41), channel_id=1, source_target_pairs={{0,124},{4,8},{8,4},{12,16},{16,12},{20,24},{24,20},{28,32},{32,28... | collective-permute-start | bytes 172040 | tf_op jit(solution)/shard_map/ppermute | solution.py:735
  15.5 3.6 %collective-permute-start.5 = (f32[14,8,128]{2,1,0:T(8,128)S(1)}, f32[14,8,128]{2,1,0:T(8,128)S(1)}, u32[]{:S(2)}, u32[]{:S(2)}) collective-permute-start(f32[14,8,128]{2,1,0:T(8,128)S(1)} %get-tuple-element.42), channel_id=1, source_target_pairs={{0,4},{4,0},{8,12},{12,8},{16,20},{20,16},{24,28},{28,24},{32,36},... | collective-permute-start | bytes 172040 | tf_op jit(solution)/shard_map/ppermute | solution.py:736
  19.1 5.7 %copy-start = (s32[1024,64]{0,1:T(8,128)S(1)}, s32[1024,64]{0,1:T(8,128)}, u32[]{:S(2)}) copy-start(s32[1024,64]{0,1:T(8,128)} %param.12) | copy-start | bytes 786436
  19.1 5.7 %copy-start.1 = (s32[1024]{0:T(1024)S(1)}, s32[1024]{0:T(1024)}, u32[]{:S(2)}) copy-start(s32[1024]{0:T(1024)} %param.13) | copy-start | bytes 12292
  19.2 5.7 %copy-start.2 = (f32[3,1024]{1,0:T(4,128)S(1)}, f32[3,1024]{1,0:T(4,128)}, u32[]{:S(2)}) copy-start(f32[3,1024]{1,0:T(4,128)} %pos_ref.1) | copy-start | bytes 36868
  19.2 5.7 %copy-start.3 = (f32[3,1024]{1,0:T(4,128)S(1)}, f32[3,1024]{1,0:T(4,128)}, u32[]{:S(2)}) copy-start(f32[3,1024]{1,0:T(4,128)} %vel_ref.1) | copy-start | bytes 36868
  19.2 5.7 %copy-start.4 = (s32[2,64,2]{1,2,0:T(2,128)S(1)}, s32[2,64,2]{1,2,0:T(2,128)}, u32[]{:S(2)}) copy-start(s32[2,64,2]{1,2,0:T(2,128)} %param.9) | copy-start | bytes 3076
  20.5 8.8 %collective-permute-start.6 = (f32[108,8,128]{2,1,0:T(8,128)S(1)}, f32[108,8,128]{2,1,0:T(8,128)S(1)}, u32[]{:S(2)}, u32[]{:S(2)}) collective-permute-start(f32[108,8,128]{2,1,0:T(8,128)S(1)} %get-tuple-element.46), channel_id=1, source_target_pairs={{0,124},{4,8},{8,4},{12,16},{16,12},{20,24},{24,20},{28,32},{32,28... | collective-permute-start | bytes 1327112 | tf_op jit(solution)/shard_map/ppermute | solution.py:753
  20.6 8.7 %collective-permute-start.7 = (f32[108,8,128]{2,1,0:T(8,128)S(1)}, f32[108,8,128]{2,1,0:T(8,128)S(1)}, u32[]{:S(2)}, u32[]{:S(2)}) collective-permute-start(f32[108,8,128]{2,1,0:T(8,128)S(1)} %get-tuple-element.47), channel_id=1, source_target_pairs={{0,4},{4,0},{8,12},{12,8},{16,20},{20,16},{24,28},{28,24},{32,36},... | collective-permute-start | bytes 1327112 | tf_op jit(solution)/shard_map/ppermute | solution.py:754

commit v5 on v4

--- a/solution.py
+++ b/solution.py
@@ -1,3 +1,5 @@
+import math
+
 import jax
 import jax.numpy as jnp
 from jax import lax
@@ -91,6 +93,7 @@
     keep = 1.0 - relax
     gain = relax * density
     base = gain - (1.5 * gain) * usq
+    scaled = {w: (w * base, (3.0 * w) * gain, (4.5 * w) * gain) for w in lattice_weights[1::6]}
     result = {}
     if 0 in wanted:
         result[0] = keep * f[0] + lattice_weights[0] * base
@@ -106,9 +109,9 @@
                     along = part
                 else:
                     along = along + part if sign > 0 else along - part
-        weight = lattice_weights[plus]
-        slope = (3.0 * weight) * (gain * along)
-        even = weight * base + 1.5 * (along * slope)
+        still, linear, square = scaled[lattice_weights[plus]]
+        slope = linear * along
+        even = still + (square * along) * along
         if plus in wanted:
             result[plus] = keep * f[plus] + (even + slope)
         if minus in wanted:
@@ -187,6 +190,7 @@
     keep = 1.0 - relax
     gain = relax * density
     base = gain - (1.5 * gain) * usq
+    scaled = {w: (w * base, (3.0 * w) * gain, (4.5 * w) * gain) for w in lattice_weights[1::6]}
     result = []
     for k in range(5):
         x, y, _ = lattice_dirs[ways[k]]
@@ -195,9 +199,8 @@
             along = along + vel_x if x > 0 else along - vel_x
         if y != 0:
             along = along + vel_y if y > 0 else along - vel_y
-        weight = lattice_weights[ways[k]]
-        slope = (3.0 * weight) * (gain * along)
-        equil = weight * base + (slope + 1.5 * (along * slope))
+        still, linear, square = scaled[lattice_weights[ways[k]]]
+        equil = still + (linear + square * along) * along
         result.append(rolled(keep * from_halo[k] + equil, y))
     return result
 
@@ -467,13 +470,49 @@
     return [f[0] for f in found]
 
 
+first_chunk = [0, 0, 0, 0, 0, 0, 0, 0, 0, 0, 0, 0, 0, 0, 0, 0, 0, 0, 0, 0, 0, 0, 0, 0, 0, 0, 0, 1, 1, 1, 1, 1, 1, 1, 1, 1, 1, 1, 1, 2, 2, 2, 2, 2, 2, 2, 2, 2, 3, 3, 3, 3, 3, 3, 3, 4, 4, 4, 4, 4, 5, 5, 5, 5]
+last_chunk = [2, 2, 2, 2, 3, 3, 3, 3, 3, 4, 4, 4, 4, 4, 4, 4, 5, 5, 5, 5, 5, 5, 5, 5, 5, 6, 6, 6, 6, 6, 6, 6, 6, 6, 6, 6, 6, 7, 7, 7, 7, 7, 7, 7, 7, 7, 7, 7, 7, 7, 7, 7, 7, 7, 7, 7, 7, 7, 7, 7, 7, 7, 7, 7]
+
+
+def sorted_entries(values):
+    values = list(values)
+    count = len(values)
+    p = 1
+    while p < count:
+        k = p
+        while k >= 1:
+            for j in range(k % p, count - k, 2 * k):
+                for i in range(min(k, count - j - k)):
+                    a, b = i + j, i + j + k
+                    if a // (2 * p) == b // (2 * p):
+                        swap = values[a] > values[b]
+                        values[a], values[b] = (
+                            jnp.where(swap, values[b], values[a]),
+                            jnp.where(swap, values[a], values[b]),
+                        )
+            k //= 2
+        p *= 2
+    return values
+
+
+def lookup_between(table, index, first, last):
+    low = index & 127
+    chunk = index >> 7
+    value = lanes(table[first], low)
+    for c in range(first + 1, last + 1):
+        value = jnp.where(chunk >= c, lanes(table[c], low), value)
+    return value
+
+
 def chunks(block):
     return [spread(block, chunk) for chunk in range(8)]
 
 
 def pull(total, near, here):
     gaps = [n - h for n, h in zip(near, here)]
-    weight = jnp.exp(-0.5 * (gaps[0] * gaps[0] + gaps[1] * gaps[1] + gaps[2] * gaps[2]))
+    weight = jnp.exp2(
+        (-0.5 / math.log(2.0)) * (gaps[0] * gaps[0] + gaps[1] * gaps[1] + gaps[2] * gaps[2])
+    )
     return tuple(t + g * weight for t, g in zip(total, gaps))
 
 
@@ -487,7 +526,7 @@
 
 def prep_kernel(own_in_ref, slot_ref, pos_ref, vel_ref, nbr_ref,
                 own_ref, inv_ref, rank_ref, hot_ref, icnt_ref, force_ref, p8_ref, v8_ref,
-                list_ref, near_ref, drift_ref):
+                list_ref, near_ref, drift_ref, uneven_ref):
     for k in range(2):
         for z in range(2):
             own_ref[k : k + 1, z * 64 : (z + 1) * 64] = own_in_ref[z, k : k + 1, :]
@@ -532,6 +571,15 @@
             list_ref[8 * k : 8 * k + 8, part, :] = nbr_ref[
                 8 * k : 8 * k + 8, part * 128 : (part + 1) * 128
             ]
+    ordered = sorted_entries([list_ref[k] for k in range(64)])
+    uneven = jnp.zeros((8, 128), f32)
+    for k, entry in enumerate(ordered):
+        list_ref[k] = entry
+        if first_chunk[k] > 0:
+            uneven = jnp.where(entry < 128 * first_chunk[k], 1.0, uneven)
+        if last_chunk[k] < 7:
+            uneven = jnp.where(entry >= 128 * (last_chunk[k] + 1), 1.0, uneven)
+    uneven_ref[0] = jnp.max(uneven).astype(i32)
     here = [p8_ref[c] for c in range(3)]
     tables = [chunks(h) for h in here]
 
@@ -555,7 +603,7 @@
 
 
 def md_kernel(arr_ref, p8_ref, v8_ref, force_ref, list_ref, near_in_ref, drift_in_ref,
-              slot_ref, hot_ref, icnt_ref, f_ref,
+              slot_ref, hot_ref, icnt_ref, f_ref, uneven_ref,
               pos_out_ref, vel_out_ref, mom_ref, f_out_ref,
               near_ref, drift_ref, pos_ref, vel_ref, sems):
     saved = [
@@ -602,10 +650,9 @@
             for c in range(3):
                 drift[c] = drift[c] + whole_units[c].astype(f32) * units[pick[c]]
                 here[c] = here[c] + drift[c]
-            tables = [chunks(code)]
-
-            def entry(k, total):
-                (word,) = lookup(tables, list_ref[k])
+            table = chunks(code)
+
+            def entry(k, total, word):
                 words = (word >> 21, (word << 11) >> 21, (word << 22) >> 22)
                 near = []
                 for c in range(3):
@@ -615,7 +662,19 @@
                     near_ref[k, c] = near[c]
                 return pull(total, near, here)
 
-            pair = over_list(entry, blank(), 64)
+            def even(total):
+                for k in range(64):
+                    word = lookup_between(table, list_ref[k], first_chunk[k], last_chunk[k])
+                    total = entry(k, total, word)
+                return total
+
+            def any_list(total):
+                def one(k, total):
+                    return entry(k, total, lookup([table], list_ref[k])[0])
+
+                return over_list(one, total, 8)
+
+            pair = lax.cond(uneven_ref[0] == 0, even, any_list, blank())
         for c in range(3):
             force = pair_strength * pair[c] + drag * (target[c] - vel[c])
             vel[c] = vel[c] + time_step * force
@@ -677,9 +736,12 @@
 
 
 def whole(populations, relax, owners, positions, velocities, neighbours, atom_slots):
+    hbm = pl.BlockSpec(memory_space=pltpu.HBM)
+    vmem = pl.BlockSpec(memory_space=pltpu.VMEM)
+    smem = pl.BlockSpec(memory_space=pltpu.SMEM)
     slots = atom_slots.reshape(8, 128)
     eights = shape(3, 8, 128)
-    own, inv, rank, hot, icnt, force, p8, v8, lists, near, drift = pl.pallas_call(
+    own, inv, rank, hot, icnt, force, p8, v8, lists, near, drift, uneven = pl.pallas_call(
         prep_kernel,
         out_shape=(
             shape(8, 128, dtype=i32),
@@ -693,10 +755,12 @@
             shape(64, 8, 128, dtype=i32),
             shape(64, 3, 8, 128),
             shape(64, 3, 8, 128),
+            shape(1, dtype=i32),
         ),
+        in_specs=[vmem] * 5,
+        out_specs=(vmem,) * 11 + (smem,),
         name="prep", compiler_params=room,
     )(owners.transpose(0, 2, 1), slots, positions, velocities, neighbours.T)
-    hbm = pl.BlockSpec(memory_space=pltpu.HBM)
     low, high, relax, post, up, down = pl.pallas_call(
         first_kernel,
         in_specs=[hbm, hbm],
@@ -759,10 +823,9 @@
         name="last", compiler_params=room,
     )(post, below, above, relax_all, inv)
     arrived = exchange(outgoing)
-    vmem = pl.BlockSpec(memory_space=pltpu.VMEM)
     pos_out, vel_out, moms, f_out = pl.pallas_call(
         md_kernel,
-        in_specs=[vmem] * 11,
+        in_specs=[vmem] * 11 + [smem],
         out_specs=(hbm, hbm, vmem, hbm),
         out_shape=(
             shape(3, 1024), shape(3, 1024), shape(128, 128), shape(19, 2, 64, 128)
@@ -775,7 +838,7 @@
             pltpu.SemaphoreType.DMA((3,)),
         ],
         name="md", compiler_params=room,
-    )(arrived, p8, v8, force, lists, near, drift, slots, hot, icnt, f)
+    )(arrived, p8, v8, force, lists, near, drift, slots, hot, icnt, f, uneven)
     returned = exchange(moms)
     cell = pl.pallas_call(
         cell_kernel, out_shape=shape(4, 2, 64), name="cells", compiler_params=room

time: 70.1 us -> 69.9 us (level)
  no operation moved by 1% of the time
where the time goes in v5:
time: 69.9 us; the launch traced here: 69.7 us
  blocking collectives  33.5 us (48%)
  starting transfers between devices  15.5 us (22%)
  Pallas kernels  14.7 us (21%)
  waiting for transfers between devices  5.19 us (7%)
  between operations  0.77 us (1%)
    all_to_all x2, blocking collectives, exchange(): lax.all_to_all(rows, ('slab', 'md'), split_axis=0, concat_axis=0, tiled=T...  33.5 us
    ppermute x2, starting transfers between devices, whole(): above = lax.ppermute(up, 'slab', near_pairs)  8.66 us
    pallas_call x1, Pallas kernels, whole(): pl.pallas_call(prep_kernel, out_shape=(shape(8, 128, dtype=i32), shape(8,...  4.72 us
    pallas_call x1, Pallas kernels, whole(): pl.pallas_call(md_kernel, in_specs=[vmem] * 11 + [smem], out_specs=(hbm,...  4.67 us
    ppermute x2, starting transfers between devices, whole(): below = lax.ppermute(down, 'slab', far_pairs)  3.18 us
    ppermute x1, waiting for transfers between devices, whole(): below_edge = lax.ppermute(down_edge, 'slab', far_pairs)  2.65 us
    ppermute x1, waiting for transfers between devices, whole(): from_low = lax.ppermute(high, 'md', [(i, (i + 1) % 4) for i in range(4)])  2.53 us
    pallas_call x1, Pallas kernels, whole(): pl.pallas_call(first_kernel, in_specs=[hbm, hbm], out_shape=(pltpu.VMEM((...  1.87 us
  transfers between devices with their start and end apart: 8, of which 2 were waited for; matrix products, arithmetic and copies ran while one was open for 0% of the time, Pallas kernels for 7%

profile of v5, /device:TPU:1, one launch (start us, length us, event | category | flops | bytes accessed | tf_op | source)
XLA Modules:
  0.0 69.7 jit_solution(4511807331568193607)
XLA Ops:
  0.6 1.9 %first.1 = (f32[20,8,128]{2,1,0:T(8,128)S(1)}, f32[20,8,128]{2,1,0:T(8,128)S(1)}, f32[2,64,128]{2,1,0:T(8,128)S(1)}, f32[19,2,64,128]{3,2,1,0:T(8,128)S(1)}, f32...) custom-call(f32[19,2,64,128]{3,2,1,0:T(8,128)} %f_hbm_ref.1, f32[2,64,128]{2,1,0:T(8,128)} %relax_hbm_ref.1), custom_call_target="tpu_custom_call" | custom-call | tf_op jit(solution)/shard_map/first/pallas_call | solution.py:764
  2.5 3.1 %collective-permute-start.2 = (f32[14,64,128]{2,1,0:T(8,128)S(1)}, f32[14,64,128]{2,1,0:T(8,128)S(1)}, u32[]{:S(2)}, u32[]{:S(2)}) collective-permute-start(f32[14,64,128]{2,1,0:T(8,128)S(1)} %get-tuple-element.40), channel_id=1, source_target_pairs={{0,124},{4,8},{8,4},{12,16},{16,12},{20,24},{24,20},{28,32},{32,28... | collective-permute-start | bytes 1376264 | tf_op jit(solution)/shard_map/ppermute | solution.py:785
  5.6 4.4 %collective-permute-start.3 = (f32[14,64,128]{2,1,0:T(8,128)S(1)}, f32[14,64,128]{2,1,0:T(8,128)S(1)}, u32[]{:S(2)}, u32[]{:S(2)}) collective-permute-start(f32[14,64,128]{2,1,0:T(8,128)S(1)} %get-tuple-element.41), channel_id=1, source_target_pairs={{0,4},{4,0},{8,12},{12,8},{16,20},{20,16},{24,28},{28,24},{32,36},... | collective-permute-start | bytes 1376264 | tf_op jit(solution)/shard_map/ppermute | solution.py:788
  10.0 1.2 %collective-permute-start = (f32[20,8,128]{2,1,0:T(8,128)S(1)}, f32[20,8,128]{2,1,0:T(8,128)S(1)}, u32[]{:S(2)}, u32[]{:S(2)}) collective-permute-start(f32[20,8,128]{2,1,0:T(8,128)S(1)} %get-tuple-element.37), channel_id=1, source_target_pairs={{0,1},{1,2},{2,3},{3,0},{4,5},{5,6},{6,7},{7,4},{8,9},{9,10},{10,1... | collective-permute-start | bytes 245768 | tf_op jit(solution)/shard_map/ppermute | solution.py:786
  11.2 1.5 %collective-permute-start.1 = (f32[20,8,128]{2,1,0:T(8,128)S(1)}, f32[20,8,128]{2,1,0:T(8,128)S(1)}, u32[]{:S(2)}, u32[]{:S(2)}) collective-permute-start(f32[20,8,128]{2,1,0:T(8,128)S(1)} %get-tuple-element.38), channel_id=1, source_target_pairs={{1,0},{2,1},{3,2},{0,3},{5,4},{6,5},{7,6},{4,7},{9,8},{10,9},{11,1... | collective-permute-start | bytes 245768 | tf_op jit(solution)/shard_map/ppermute | solution.py:787
  12.7 2.5 %collective-permute-done.low_ref = f32[20,8,128]{2,1,0:T(8,128)S(1)} collective-permute-done((f32[20,8,128]{2,1,0:T(8,128)S(1)}, f32[20,8,128]{2,1,0:T(8,128)S(1)}, u32[]{:S(2)}, u32[]{:S(2)}) %collective-permute-start) | collective-permute-done | bytes 81952 | tf_op jit(solution)/shard_map/ppermute | solution.py:786
  15.2 0.0 collective-permute-done.1.high_ref
  15.2 0.2 edge.1
  15.4 0.1 collective-permute-start.4
  15.5 0.9 %collective-permute-start.5 = (f32[14,8,128]{2,1,0:T(8,128)S(1)}, f32[14,8,128]{2,1,0:T(8,128)S(1)}, u32[]{:S(2)}, u32[]{:S(2)}) collective-permute-start(f32[14,8,128]{2,1,0:T(8,128)S(1)} %get-tuple-element.43), channel_id=1, source_target_pairs={{0,4},{4,0},{8,12},{12,8},{16,20},{20,16},{24,28},{28,24},{32,36},... | collective-permute-start | bytes 172040 | tf_op jit(solution)/shard_map/ppermute | solution.py:800
  16.4 2.6 %collective-permute-done.4.below_edge_ref = f32[14,8,128]{2,1,0:T(8,128)S(1)} collective-permute-done((f32[14,8,128]{2,1,0:T(8,128)S(1)}, f32[14,8,128]{2,1,0:T(8,128)S(1)}, u32[]{:S(2)}, u32[]{:S(2)}) %collective-permute-start.4) | collective-permute-done | bytes 57376 | tf_op jit(solution)/shard_map/ppermute | solution.py:799
  19.1 0.0 collective-permute-done.5.above_edge_ref
  19.1 0.0 collective-permute-done.2.below_ref
  19.1 0.0 collective-permute-done.3.above_ref
  19.1 0.0 copy-start
  19.1 0.0 copy-start.1
  19.1 0.0 copy-start.2
  19.1 0.0 copy-start.3
  19.1 0.0 copy-start.4
  19.2 1.2 %middle.1 = (f32[19,2,88,128]{3,2,1,0:T(8,128)S(1)}, f32[108,8,128]{2,1,0:T(8,128)S(1)}, f32[108,8,128]{2,1,0:T(8,128)S(1)}, f32[4,72,128]{2,1,0:T(8,128)S(1)}) custom-call(f32[19,2,64,128]{3,2,1,0:T(8,128)S(1)} %get-tuple-element.36.post_ref, f32[38,24,128]{2,1,0:T(8,128)S(1)} %get-tuple-element.39.seam_ref, ...), custom_call_target="tpu_custom_call" | custom-call | tf_op jit(solution)/shard_map/middle/pallas_call | solution.py:806
  20.4 0.1 collective-permute-start.6
  20.5 4.3 %collective-permute-start.7 = (f32[108,8,128]{2,1,0:T(8,128)S(1)}, f32[108,8,128]{2,1,0:T(8,128)S(1)}, u32[]{:S(2)}, u32[]{:S(2)}) collective-permute-start(f32[108,8,128]{2,1,0:T(8,128)S(1)} %get-tuple-element.48), channel_id=1, source_target_pairs={{0,4},{4,0},{8,12},{12,8},{16,20},{20,16},{24,28},{28,24},{32,36},... | collective-permute-start | bytes 1327112 | tf_op jit(solution)/shard_map/ppermute | solution.py:818
  24.8 0.0 copy-done
  24.8 0.0 copy-done.1
  24.8 4.7 %prep.1 = (s32[8,128]{1,0:T(8,128)S(1)}, s32[8,128]{1,0:T(8,128)S(1)}, s32[8,128]{1,0:T(8,128)S(1)}, bf16[128,1024]{1,0:T(8,128)(2,1)S(1)}, f32[128,16]{1,0:T(8,...) custom-call(s32[2,2,64]{2,1,0:T(2,128)S(1)} %bitcast.18, ...), custom_call_target="tpu_custom_call" | custom-call | tf_op jit(solution)/shard_map/prep/pallas_call | solution.py:744
  29.5 0.0 collective-permute-done.6.below_ref
  29.5 0.0 collective-permute-done.7.above_ref
  29.5 1.2 %last.1 = (f32[19,2,64,128]{3,2,1,0:T(8,128)S(1)}, f32[128,128]{1,0:T(8,128)S(1)}) custom-call(f32[19,2,88,128]{3,2,1,0:T(8,128)S(1)} %get-tuple-element.46.post_ref, f32[108,8,128]{2,1,0:T(8,128)S(1)} %collective-permute-done.6.below_ref, f32[108,8,128]{2,1,0:T(8,128)S(1)} %collective-permute-done.7.above_ref, ...), custom_call_target="tpu_custom_call" | custom-call | tf_op jit(solution)/shard_map/last/pallas_call | solution.py:819
  30.7 19.7 %all_to_all.22 = f32[128,1,128]{2,1,0:T(1,128)S(1)} all-to-all(f32[128,1,128]{2,1,0:T(1,128)S(1)} %bitcast.15), channel_id=1, replica_groups=mesh['slab'=32,'md'=4] {'slab','md'}, dimensions={0} | all-to-all | bytes 131072 | tf_op jit(solution)/shard_map/all_to_all | solution.py:731
  50.5 4.7 %md.1 = (f32[3,1024]{1,0:T(4,128)}, f32[3,1024]{1,0:T(4,128)}, f32[128,128]{1,0:T(8,128)S(1)}, f32[19,2,64,128]{3,2,1,0:T(8,128)}) custom-call(f32[128,128]{1,0:T(8,128)S(1)} %bitcast.11, f32[3,8,128]{2,1,0:T(8,128)S(1)} %get-tuple-element.52.p8_ref, f32[3,8,128]{2,1,0:T(8,128)S(1)} %get-tuple-element.53.v8_ref, ...), custom_call_target="tpu_custom_call" | custom-call | tf_op jit(solution)/shard_map/md/pallas_call | solution.py:826
  55.1 13.8 %all_to_all.23 = f32[128,1,128]{2,1,0:T(1,128)S(1)} all-to-all(f32[128,1,128]{2,1,0:T(1,128)S(1)} %bitcast.14), channel_id=1, replica_groups=mesh['slab'=32,'md'=4] {'slab','md'}, dimensions={0} | all-to-all | bytes 131072 | tf_op jit(solution)/shard_map/all_to_all | solution.py:731
  68.9 0.8 %cells.1 = f32[4,2,64]{2,1,0:T(2,128)} custom-call(f32[128,128]{1,0:T(8,128)S(1)} %bitcast.13, s32[8,128]{1,0:T(8,128)S(1)} %get-tuple-element.66.own_ref, s32[8,128]{1,0:T(8,128)S(1)} %get-tuple-element.67.rank_ref), custom_call_target="tpu_custom_call" | custom-call | tf_op jit(solution)/shard_map/cells/pallas_call | solution.py:843
  (3 shorter events, 0.0 us)
Async XLA Ops:
  2.5 16.6 %collective-permute-start.2 = (f32[14,64,128]{2,1,0:T(8,128)S(1)}, f32[14,64,128]{2,1,0:T(8,128)S(1)}, u32[]{:S(2)}, u32[]{:S(2)}) collective-permute-start(f32[14,64,128]{2,1,0:T(8,128)S(1)} %get-tuple-element.40), channel_id=1, source_target_pairs={{0,124},{4,8},{8,4},{12,16},{16,12},{20,24},{24,20},{28,32},{32,28... | collective-permute-start | bytes 1376264 | tf_op jit(solution)/shard_map/ppermute | solution.py:785
  5.6 13.5 %collective-permute-start.3 = (f32[14,64,128]{2,1,0:T(8,128)S(1)}, f32[14,64,128]{2,1,0:T(8,128)S(1)}, u32[]{:S(2)}, u32[]{:S(2)}) collective-permute-start(f32[14,64,128]{2,1,0:T(8,128)S(1)} %get-tuple-element.41), channel_id=1, source_target_pairs={{0,4},{4,0},{8,12},{12,8},{16,20},{20,16},{24,28},{28,24},{32,36},... | collective-permute-start | bytes 1376264 | tf_op jit(solution)/shard_map/ppermute | solution.py:788
  10.0 5.2 %collective-permute-start = (f32[20,8,128]{2,1,0:T(8,128)S(1)}, f32[20,8,128]{2,1,0:T(8,128)S(1)}, u32[]{:S(2)}, u32[]{:S(2)}) collective-permute-start(f32[20,8,128]{2,1,0:T(8,128)S(1)} %get-tuple-element.37), channel_id=1, source_target_pairs={{0,1},{1,2},{2,3},{3,0},{4,5},{5,6},{6,7},{7,4},{8,9},{9,10},{10,1... | collective-permute-start | bytes 245768 | tf_op jit(solution)/shard_map/ppermute | solution.py:786
  11.2 4.0 %collective-permute-start.1 = (f32[20,8,128]{2,1,0:T(8,128)S(1)}, f32[20,8,128]{2,1,0:T(8,128)S(1)}, u32[]{:S(2)}, u32[]{:S(2)}) collective-permute-start(f32[20,8,128]{2,1,0:T(8,128)S(1)} %get-tuple-element.38), channel_id=1, source_target_pairs={{1,0},{2,1},{3,2},{0,3},{5,4},{6,5},{7,6},{4,7},{9,8},{10,9},{11,1... | collective-permute-start | bytes 245768 | tf_op jit(solution)/shard_map/ppermute | solution.py:787
  15.4 3.7 %collective-permute-start.4 = (f32[14,8,128]{2,1,0:T(8,128)S(1)}, f32[14,8,128]{2,1,0:T(8,128)S(1)}, u32[]{:S(2)}, u32[]{:S(2)}) collective-permute-start(f32[14,8,128]{2,1,0:T(8,128)S(1)} %get-tuple-element.42), channel_id=1, source_target_pairs={{0,124},{4,8},{8,4},{12,16},{16,12},{20,24},{24,20},{28,32},{32,28... | collective-permute-start | bytes 172040 | tf_op jit(solution)/shard_map/ppermute | solution.py:799
  15.5 3.6 %collective-permute-start.5 = (f32[14,8,128]{2,1,0:T(8,128)S(1)}, f32[14,8,128]{2,1,0:T(8,128)S(1)}, u32[]{:S(2)}, u32[]{:S(2)}) collective-permute-start(f32[14,8,128]{2,1,0:T(8,128)S(1)} %get-tuple-element.43), channel_id=1, source_target_pairs={{0,4},{4,0},{8,12},{12,8},{16,20},{20,16},{24,28},{28,24},{32,36},... | collective-permute-start | bytes 172040 | tf_op jit(solution)/shard_map/ppermute | solution.py:800
  19.1 5.7 %copy-start = (s32[1024,64]{0,1:T(8,128)S(1)}, s32[1024,64]{0,1:T(8,128)}, u32[]{:S(2)}) copy-start(s32[1024,64]{0,1:T(8,128)} %param.12) | copy-start | bytes 786436
  19.1 5.7 %copy-start.1 = (s32[1024]{0:T(1024)S(1)}, s32[1024]{0:T(1024)}, u32[]{:S(2)}) copy-start(s32[1024]{0:T(1024)} %param.13) | copy-start | bytes 12292
  19.1 5.7 %copy-start.2 = (f32[3,1024]{1,0:T(4,128)S(1)}, f32[3,1024]{1,0:T(4,128)}, u32[]{:S(2)}) copy-start(f32[3,1024]{1,0:T(4,128)} %pos_ref.1) | copy-start | bytes 36868
  19.1 5.6 %copy-start.3 = (f32[3,1024]{1,0:T(4,128)S(1)}, f32[3,1024]{1,0:T(4,128)}, u32[]{:S(2)}) copy-start(f32[3,1024]{1,0:T(4,128)} %vel_ref.1) | copy-start | bytes 36868
  19.1 5.6 %copy-start.4 = (s32[2,64,2]{1,2,0:T(2,128)S(1)}, s32[2,64,2]{1,2,0:T(2,128)}, u32[]{:S(2)}) copy-start(s32[2,64,2]{1,2,0:T(2,128)} %param.9) | copy-start | bytes 3076
  20.4 9.1 %collective-permute-start.6 = (f32[108,8,128]{2,1,0:T(8,128)S(1)}, f32[108,8,128]{2,1,0:T(8,128)S(1)}, u32[]{:S(2)}, u32[]{:S(2)}) collective-permute-start(f32[108,8,128]{2,1,0:T(8,128)S(1)} %get-tuple-element.47), channel_id=1, source_target_pairs={{0,124},{4,8},{8,4},{12,16},{16,12},{20,24},{24,20},{28,32},{32,28... | collective-permute-start | bytes 1327112 | tf_op jit(solution)/shard_map/ppermute | solution.py:817
  20.5 9.0 %collective-permute-start.7 = (f32[108,8,128]{2,1,0:T(8,128)S(1)}, f32[108,8,128]{2,1,0:T(8,128)S(1)}, u32[]{:S(2)}, u32[]{:S(2)}) collective-permute-start(f32[108,8,128]{2,1,0:T(8,128)S(1)} %get-tuple-element.48), channel_id=1, source_target_pairs={{0,4},{4,0},{8,12},{12,8},{16,20},{20,16},{24,28},{28,24},{32,36},... | collective-permute-start | bytes 1327112 | tf_op jit(solution)/shard_map/ppermute | solution.py:818
